TPU v7x, 128 devices: a whole 4x4x4 slice. The times are simulated.
128 devices in a mesh: layer: 2 (over core), px: 16 (over x, z), py: 4 (over y).
Axes of the slice: x: 4, y: 4, z: 4, core: 2. Of those that a mesh axis runs over, the one named last changes fastest.
Arguments:
- right_side: float32 [8, 2048, 4096], P('layer', 'px', 'py'), may hold values from -30 to 30
- row_conduct: float32 [8, 2048, 4096], P('layer', 'px', 'py'), may hold values from 0.5 to 2
- column_conduct: float32 [8, 2048, 4096], P('layer', 'px', 'py'), may hold values from 0.5 to 2
- via_conduct: float32 [8, 2048, 4096], P('layer', 'px', 'py'), may hold values from 0.5 to 4
- via_mask: int32 [8, 2048, 4096], P('layer', 'px', 'py'), may hold values 0 or 1
- ground_conduct: float32 [8, 2048, 4096], P('layer', 'px', 'py'), may hold values from 0.01 to 0.1
Outputs:
- solution_field: float32 [8, 2048, 4096], P('layer', 'px', 'py')
- residual: float32 [8, 2048, 4096], P('layer', 'px', 'py')
All inputs are finite; a program needn't handle non-finite values. No bound on the sum of `via_mask` on one device may be relied on, other than what follows from the above.
Results may differ from a plain program's by a relative error of at most 0.0001.
Values sent between devices are 32-bit elements; how exact they have to be, the bound alone decides.
No kernel may reach another device: no remote copies, remote signals or barrier semaphores. Data moves between devices by JAX's collectives and lax.ppermute only.
A program may use at most 128 MiB of HBM per device.

v0:
```python
import jax
import jax.numpy as jnp
from jax import lax
from jax.sharding import Mesh
from jax.sharding import PartitionSpec as P

ITERS = 2
LAYER_PX_PY = ("layer", "px_0", "px_1", "py")
PX = ("px_0", "px_1")


def extended(value, sides, width):
    edges = {}
    for axis, dim in sides:
        count, length = (lax.axis_size(axis), value.shape[dim])
        up = [(i, (i + 1) % count) for i in range(count - 1)]
        last = lax.slice_in_dim(value, length - width, length, axis=dim)
        initial = lax.slice_in_dim(value, 0, width, axis=dim)
        edges[dim] = (
            lax.ppermute(last, axis, up),
            lax.ppermute(initial, axis, [(b, a) for a, b in up]),
        )
    done = []
    for _, dim in sides:
        low, high = edges[dim]
        around = [(width, width) if d in done else (0, 0) for d in range(value.ndim)]
        value = jnp.concatenate([jnp.pad(low, around), value, jnp.pad(high, around)], axis=dim)
        done.append(dim)
    return value


def by_axis(value, axes):
    for axis in axes:
        value = lax.psum(value, axis)
    return value


def from_behind(value, axis, by):
    count = lax.axis_size(axis)
    pairs = [(i, i + by) for i in range(count) if 0 <= i + by < count]
    return lax.ppermute(value, axis, pairs)


def factor_layers(diagonal, vertical, vertical_below, carried):
    gains = []
    inverses = []
    previous = carried
    for index in range(diagonal.shape[0]):
        inverse = 1.0 / (diagonal[index] - vertical_below[index] * previous)
        previous = vertical[index] * inverse
        gains.append(previous)
        inverses.append(inverse)
    return (jnp.stack(gains), jnp.stack(inverses))


def forward_layers(residual, vertical_below, inverses, carried):
    values = []
    previous = carried
    for index in range(residual.shape[0]):
        previous = (residual[index] + vertical_below[index] * previous) * inverses[index]
        values.append(previous)
    return jnp.stack(values)


def back_layers(forward, gains, carried):
    count = forward.shape[0]
    values = [None] * count
    following = carried
    for index in range(count - 1, -1, -1):
        following = forward[index] + gains[index] * following
        values[index] = following
    return jnp.stack(values)


def operate(field, coeffs):
    diagonal, row_conduct, row_upper, column_conduct, column_left, vertical, vertical_below = coeffs
    padded = extended(field, (("layer", 0), (PX, 1), ("py", 2)), 1)
    return (
        diagonal * field
        - row_conduct * padded[1:-1, 2:, 1:-1]
        - row_upper * padded[1:-1, :-2, 1:-1]
        - column_conduct * padded[1:-1, 1:-1, 2:]
        - column_left * padded[1:-1, 1:-1, :-2]
        - vertical * padded[2:, 1:-1, 1:-1]
        - vertical_below * padded[:-2, 1:-1, 1:-1]
    )


def paired_sums(residual, precond, image):
    return (
        by_axis(jnp.sum(residual * precond), LAYER_PX_PY),
        by_axis(jnp.sum(image * precond), LAYER_PX_PY),
    )


def shards(right_side, row_conduct, column_conduct, via_conduct, via_mask, ground_conduct):
    depth = right_side.shape[0]
    members = lax.axis_size("layer")
    layers_total = depth * members
    level = lax.axis_index("layer") * depth + jnp.arange(depth, dtype=jnp.int32)
    keep = (level < layers_total - 1).astype(jnp.float32)[:, None, None]
    vertical = via_conduct * via_mask.astype(jnp.float32) * keep
    row_edge = from_behind(row_conduct[:, -1:, :], PX, 1)
    row_upper = jnp.concatenate([row_edge, row_conduct[:, :-1, :]], axis=1)
    column_edge = from_behind(column_conduct[:, :, -1:], "py", 1)
    column_left = jnp.concatenate([column_edge, column_conduct[:, :, :-1]], axis=2)
    vertical_edge = from_behind(vertical[-1:], "layer", 1)
    vertical_below = jnp.concatenate([vertical_edge, vertical[:-1]], axis=0)
    diagonal = (
        ground_conduct
        + row_conduct
        + row_upper
        + column_conduct
        + column_left
        + vertical
        + vertical_below
    )
    coeffs = (
        diagonal,
        row_conduct,
        row_upper,
        column_conduct,
        column_left,
        vertical,
        vertical_below,
    )
    plane = jnp.zeros_like(right_side[0])
    carried = plane
    gains, inverses = factor_layers(diagonal, vertical, vertical_below, carried)
    carried = from_behind(gains[-1], "layer", 1)
    gains, inverses = factor_layers(diagonal, vertical, vertical_below, carried)

    def precondition(residual):
        incoming = plane
        forward = forward_layers(residual, vertical_below, inverses, incoming)
        incoming = from_behind(forward[-1], "layer", 1)
        forward = forward_layers(residual, vertical_below, inverses, incoming)
        returning = plane
        solved = back_layers(forward, gains, returning)
        returning = from_behind(solved[0], "layer", -1)
        return back_layers(forward, gains, returning)

    solution_field = jnp.zeros_like(right_side)
    residual = right_side
    precond = precondition(residual)
    image = operate(precond, coeffs)
    rho, curvature = paired_sums(residual, precond, image)
    alpha = rho / curvature
    direction, along = (precond, image)
    for step in range(ITERS):
        solution_field = solution_field + alpha * direction
        residual = residual - alpha * along
        if step + 1 < ITERS:
            precond = precondition(residual)
            image = operate(precond, coeffs)
            rho_next, curvature = paired_sums(residual, precond, image)
            ratio = rho_next / rho
            alpha = rho_next / (curvature - ratio * rho_next / alpha)
            direction = precond + ratio * direction
            along = image + ratio * along
            rho = rho_next
    return (solution_field, residual)


def solution(mesh):
    split = Mesh(
        mesh.devices.reshape(mesh.shape["layer"], 4, 4, mesh.shape["py"]),
        ("layer", "px_0", "px_1", "py"),
    )
    return jax.shard_map(
        shards,
        mesh=split,
        in_specs=(
            P("layer", PX, "py"),
            P("layer", PX, "py"),
            P("layer", PX, "py"),
            P("layer", PX, "py"),
            P("layer", PX, "py"),
            P("layer", PX, "py"),
        ),
        out_specs=(P("layer", PX, "py"), P("layer", PX, "py")),
        check_vma=False,
    )
```

profile of v0, /device:TPU:2, one launch (start us, length us, event | category | flops | bytes accessed | tf_op | source)
XLA Modules:
  0.0 200.5 jit_solution(8595721129554607159)
XLA Ops:
  0.7 2.9 %multiply_multiply_fusion = f32[4,128,1024]{2,1,0:T(8,128)S(1)} fusion(f32[4,128,1024]{2,1,0:T(8,128)} %param.9, s32[4,128,1024]{2,1,0:T(8,128)} %param.10, f32[4]{0:T(128)S(1)} %compare_convert_fusion), kind=kLoop, calls=%fused_computation.59 | loop fusion | flops 1572864 | bytes 6291472 | tf_op jit(solution)/shard_map/mul | solution.py:102
  3.7 1.9 collective-permute-start
  5.6 3.8 %collective-permute-start.1 = (f32[4,1,1024]{2,1,0:T(1,128)S(1)}, f32[4,1,1024]{2,1,0:T(1,128)S(1)}, u32[]{:S(2)}, u32[]{:S(2)}) collective-permute-start(f32[4,1,1024]{2,1,0:T(1,128)S(1)} %slice.173), channel_id=1, source_target_pairs={{0,4},{4,8},{8,12},{12,16},{16,20},{20,24},{24,28},{28,32},{32,36}... | collective-permute-start | bytes 49160 | tf_op jit(solution)/shard_map/ppermute | solution.py:41
  9.6 3.5 %collective-permute-start.2 = (f32[4,128,1]{2,1,0:T(8,128)S(1)}, f32[4,128,1]{2,1,0:T(8,128)S(1)}, u32[]{:S(2)}, u32[]{:S(2)}) collective-permute-start(f32[4,128,1]{2,1,0:T(8,128)S(1)} %slice.175), channel_id=1, source_target_pairs={{0,1},{1,2},{2,3},{4,5},{5,6},{6,7},{8,9},{9,10},{10,11},{12,13},{... | collective-permute-start | bytes 6152 | tf_op jit(solution)/shard_map/ppermute | solution.py:41
  13.2 4.7 %collective-permute-done.2 = f32[4,128,1]{2,1,0:T(8,128)S(1)} collective-permute-done((f32[4,128,1]{2,1,0:T(8,128)S(1)}, f32[4,128,1]{2,1,0:T(8,128)S(1)}, u32[]{:S(2)}, u32[]{:S(2)}) %collective-permute-start.2) | collective-permute-done | bytes 2080 | tf_op jit(solution)/shard_map/ppermute | solution.py:41
  17.9 1.8 add_add_fusion
  20.2 1.5 collective-permute-start.3
  21.6 1.5 collective-permute-done.3
  24.1 2.3 %collective-permute-start.4 = (f32[128,1024]{1,0:T(8,128)S(1)}, f32[128,1024]{1,0:T(8,128)S(1)}, u32[]{:S(2)}, u32[]{:S(2)}) collective-permute-start(f32[128,1024]{1,0:T(8,128)S(1)} %get-tuple-element.40), channel_id=1, source_target_pairs={{0,64},{1,65},{2,66},{3,67},{4,68},{5,69},{6,70},{7,71},{8,72},{9,... | collective-permute-start | bytes 1572872 | tf_op jit(solution)/shard_map/ppermute | solution.py:41
  26.4 1.5 collective-permute-done.4
  27.9 1.0 multiply_add_fusion.8
  28.9 1.3 collective-permute-start.5
  30.2 2.5 %collective-permute-done.5 = f32[128,1024]{1,0:T(8,128)S(1)} collective-permute-done((f32[128,1024]{1,0:T(8,128)S(1)}, f32[128,1024]{1,0:T(8,128)S(1)}, u32[]{:S(2)}, u32[]{:S(2)}) %collective-permute-start.5) | collective-permute-done | bytes 524320 | tf_op jit(solution)/shard_map/ppermute | solution.py:41
  33.0 2.1 %collective-permute-start.6 = (f32[1,128,1024]{2,1,0:T(8,128)S(1)}, f32[1,128,1024]{2,1,0:T(8,128)S(1)}, u32[]{:S(2)}, u32[]{:S(2)}) collective-permute-start(f32[1,128,1024]{2,1,0:T(8,128)S(1)} %bitcast.233), channel_id=1, source_target_pairs={{0,64},{1,65},{2,66},{3,67},{4,68},{5,69},{6,70},{7,71},{8,72},{9,... | collective-permute-start | bytes 1572872 | tf_op jit(solution)/shard_map/ppermute | solution.py:20
  35.1 1.5 collective-permute-done.6
  37.4 1.3 collective-permute-start.7
  39.1 4.0 %collective-permute-start.9 = (f32[4,1,1024]{2,1,0:T(1,128)S(1)}, f32[4,1,1024]{2,1,0:T(1,128)S(1)}, u32[]{:S(2)}, u32[]{:S(2)}) collective-permute-start(f32[4,1,1024]{2,1,0:T(1,128)S(1)} %get-tuple-element.54), channel_id=1, source_target_pairs={{0,4},{4,8},{8,12},{12,16},{16,20},{20,24},{24,28},{28,32},{32,36}... | collective-permute-start | bytes 49160 | tf_op jit(solution)/shard_map/ppermute | solution.py:20
  43.0 4.1 %collective-permute-start.8 = (f32[4,1,1024]{2,1,0:T(1,128)S(1)}, f32[4,1,1024]{2,1,0:T(1,128)S(1)}, u32[]{:S(2)}, u32[]{:S(2)}) collective-permute-start(f32[4,1,1024]{2,1,0:T(1,128)S(1)} %get-tuple-element.55), channel_id=1, source_target_pairs={{4,0},{8,4},{12,8},{16,12},{20,16},{24,20},{28,24},{32,28},{36,32}... | collective-permute-start | bytes 49160 | tf_op jit(solution)/shard_map/ppermute | solution.py:21
  47.3 1.3 collective-permute-start.10
  48.6 5.0 %collective-permute-start.11 = (f32[4,128,1]{2,1,0:T(8,128)S(1)}, f32[4,128,1]{2,1,0:T(8,128)S(1)}, u32[]{:S(2)}, u32[]{:S(2)}) collective-permute-start(f32[4,128,1]{2,1,0:T(8,128)S(1)} %get-tuple-element.53), channel_id=1, source_target_pairs={{0,1},{1,2},{2,3},{4,5},{5,6},{6,7},{8,9},{9,10},{10,11},{12,13},{... | collective-permute-start | bytes 6152 | tf_op jit(solution)/shard_map/ppermute | solution.py:20
  54.6 4.2 %collective-permute-done.10 = f32[4,128,1]{2,1,0:T(8,128)S(1)} collective-permute-done((f32[4,128,1]{2,1,0:T(8,128)S(1)}, f32[4,128,1]{2,1,0:T(8,128)S(1)}, u32[]{:S(2)}, u32[]{:S(2)}) %collective-permute-start.10) | collective-permute-done | bytes 2080 | tf_op jit(solution)/shard_map/ppermute | solution.py:21
  58.8 1.2 collective-permute-done.11
  60.0 9.9 %multiply_reduce_fusion.2 = (f32[]{:T(128)}, f32[]{:T(128)}, f32[4,128,1024]{2,1,0:T(8,128)}) fusion(f32[1,128,1024]{2,1,0:T(8,128)S(1)} %bitcast.235, f32[1,128,1024]{2,1,0:T(8,128)S(1)} %bitcast.245, f32[1,128,1024]{2,1,0:T(8,128)S(1)} %bitcast.242, f32[1,128,1024]{2,1,0:T(8,128)S(1)} %get-tuple-element.33, f32[4,128,1024]{2,1,0:T(8,128)S(1)} %copy-done.5, ...), kind=kLoop, calls=%fused_computation.56 | loop fusion | flops 25690112 | bytes 25219080 | tf_op jit(solution)/shard_map/reduce_sum | solution.py:92
  69.9 3.1 %all-reduce.15 = (f32[]{:T(128)}, f32[]{:T(128)}) all-reduce(f32[]{:T(128)} %get-tuple-element.5, f32[]{:T(128)} %get-tuple-element.4), channel_id=1, replica_groups=mesh['layer'=2,'px_0'=4,'px_1'=4,'py'=4] {'layer'}, use_global_device_ids=true, to_apply=%region_1.2 | all-reduce | flops 2 | bytes 16 | tf_op jit(solution)/shard_map/psum | solution.py:34
  73.0 9.3 %all-reduce.13 = (f32[]{:T(128)}, f32[]{:T(128)}) all-reduce(f32[]{:T(128)} %get-tuple-element.20, f32[]{:T(128)} %get-tuple-element.21), channel_id=1, replica_groups=mesh['layer'=2,'px_0'=4,'px_1'=4,'py'=4] {'px_0'}, use_global_device_ids=true, to_apply=%region_2.3 | all-reduce | flops 2 | bytes 16 | tf_op jit(solution)/shard_map/psum | solution.py:34
  82.3 8.7 %all-reduce.11 = (f32[]{:T(128)}, f32[]{:T(128)}) all-reduce(f32[]{:T(128)} %get-tuple-element.16, f32[]{:T(128)} %get-tuple-element.17), channel_id=1, replica_groups=mesh['layer'=2,'px_0'=4,'px_1'=4,'py'=4] {'px_1'}, use_global_device_ids=true, to_apply=%region_3.4 | all-reduce | flops 2 | bytes 16 | tf_op jit(solution)/shard_map/psum | solution.py:34
  91.0 12.8 %all-reduce.9 = (f32[]{:T(128)}, f32[]{:T(128)}) all-reduce(f32[]{:T(128)} %get-tuple-element.12, f32[]{:T(128)} %get-tuple-element.13), channel_id=1, replica_groups=mesh['layer'=2,'px_0'=4,'px_1'=4,'py'=4] {'py'}, use_global_device_ids=true, to_apply=%region_4.5 | all-reduce | flops 2 | bytes 16 | tf_op jit(solution)/shard_map/psum | solution.py:34
  105.3 2.8 %multiply_subtract_fusion.1 = f32[4,128,1024]{2,1,0:T(8,128)S(1)} fusion(f32[4,128,1024]{2,1,0:T(8,128)} %param.6, f32[4,128,1024]{2,1,0:T(8,128)} %get-tuple-element.31, f32[]{:T(128)S(6)} %div.44), kind=kLoop, calls=%fused_computation.55 | loop fusion | flops 1048576 | bytes 6291460 | tf_op jit(solution)/shard_map/sub | solution.py:152
  108.8 1.6 collective-permute-start.12
  110.5 1.3 collective-permute-done.12
  112.8 1.3 collective-permute-start.13
  114.1 2.5 %collective-permute-done.13 = f32[128,1024]{1,0:T(8,128)S(1)} collective-permute-done((f32[128,1024]{1,0:T(8,128)S(1)}, f32[128,1024]{1,0:T(8,128)S(1)}, u32[]{:S(2)}, u32[]{:S(2)}) %collective-permute-start.13) | collective-permute-done | bytes 524320 | tf_op jit(solution)/shard_map/ppermute | solution.py:41
  116.9 2.1 %collective-permute-start.14 = (f32[1,128,1024]{2,1,0:T(8,128)S(1)}, f32[1,128,1024]{2,1,0:T(8,128)S(1)}, u32[]{:S(2)}, u32[]{:S(2)}) collective-permute-start(f32[1,128,1024]{2,1,0:T(8,128)S(1)} %bitcast.237), channel_id=1, source_target_pairs={{0,64},{1,65},{2,66},{3,67},{4,68},{5,69},{6,70},{7,71},{8,72},{9,... | collective-permute-start | bytes 1572872 | tf_op jit(solution)/shard_map/ppermute | solution.py:20
  119.0 1.5 collective-permute-done.14
  121.3 1.3 constant_dynamic-update-slice_fusion.10
  122.6 1.3 collective-permute-start.15
  125.8 3.9 %collective-permute-start.17 = (f32[4,1,1024]{2,1,0:T(1,128)S(1)}, f32[4,1,1024]{2,1,0:T(1,128)S(1)}, u32[]{:S(2)}, u32[]{:S(2)}) collective-permute-start(f32[4,1,1024]{2,1,0:T(1,128)S(1)} %get-tuple-element.50), channel_id=1, source_target_pairs={{0,4},{4,8},{8,12},{12,16},{16,20},{20,24},{24,28},{28,32},{32,36}... | collective-permute-start | bytes 49160 | tf_op jit(solution)/shard_map/ppermute | solution.py:20
  129.7 4.3 %collective-permute-start.16 = (f32[4,1,1024]{2,1,0:T(1,128)S(1)}, f32[4,1,1024]{2,1,0:T(1,128)S(1)}, u32[]{:S(2)}, u32[]{:S(2)}) collective-permute-start(f32[4,1,1024]{2,1,0:T(1,128)S(1)} %get-tuple-element.51), channel_id=1, source_target_pairs={{4,0},{8,4},{12,8},{16,12},{20,16},{24,20},{28,24},{32,28},{36,32}... | collective-permute-start | bytes 49160 | tf_op jit(solution)/shard_map/ppermute | solution.py:21
  135.1 1.3 collective-permute-start.18
  136.4 4.6 %collective-permute-start.19 = (f32[4,128,1]{2,1,0:T(8,128)S(1)}, f32[4,128,1]{2,1,0:T(8,128)S(1)}, u32[]{:S(2)}, u32[]{:S(2)}) collective-permute-start(f32[4,128,1]{2,1,0:T(8,128)S(1)} %get-tuple-element.49), channel_id=1, source_target_pairs={{0,1},{1,2},{2,3},{4,5},{5,6},{6,7},{8,9},{9,10},{10,11},{12,13},{... | collective-permute-start | bytes 6152 | tf_op jit(solution)/shard_map/ppermute | solution.py:20
  141.8 3.9 %collective-permute-done.18 = f32[4,128,1]{2,1,0:T(8,128)S(1)} collective-permute-done((f32[4,128,1]{2,1,0:T(8,128)S(1)}, f32[4,128,1]{2,1,0:T(8,128)S(1)}, u32[]{:S(2)}, u32[]{:S(2)}) %collective-permute-start.18) | collective-permute-done | bytes 2080 | tf_op jit(solution)/shard_map/ppermute | solution.py:21
  145.8 1.2 collective-permute-done.19
  147.0 10.1 %multiply_reduce_fusion = (f32[]{:T(128)}, f32[]{:T(128)}, f32[4,128,1024]{2,1,0:T(8,128)}) fusion(f32[1,128,1024]{2,1,0:T(8,128)S(1)} %bitcast.239, f32[1,128,1024]{2,1,0:T(8,128)S(1)} %bitcast.251, f32[1,128,1024]{2,1,0:T(8,128)S(1)} %bitcast.248, f32[1,128,1024]{2,1,0:T(8,128)S(1)} %get-tuple-element.24, f32[4,128,1024]{2,1,0:T(8,128)S(1)} %multiply_subtract_fusion.1, ...), kind=kLoop, calls=%fused_computation.53 | loop fusion | flops 25690112 | bytes 25219080 | tf_op jit(solution)/shard_map/reduce_sum | solution.py:92
  157.1 3.1 %all-reduce.14 = (f32[]{:T(128)}, f32[]{:T(128)}) all-reduce(f32[]{:T(128)} %get-tuple-element.3, f32[]{:T(128)} %get-tuple-element.2), channel_id=1, replica_groups=mesh['layer'=2,'px_0'=4,'px_1'=4,'py'=4] {'layer'}, use_global_device_ids=true, to_apply=%region_11.12 | all-reduce | flops 2 | bytes 16 | tf_op jit(solution)/shard_map/psum | solution.py:34
  160.2 9.0 %all-reduce.12 = (f32[]{:T(128)}, f32[]{:T(128)}) all-reduce(f32[]{:T(128)} %get-tuple-element.18, f32[]{:T(128)} %get-tuple-element.19), channel_id=1, replica_groups=mesh['layer'=2,'px_0'=4,'px_1'=4,'py'=4] {'px_0'}, use_global_device_ids=true, to_apply=%region_12.13 | all-reduce | flops 2 | bytes 16 | tf_op jit(solution)/shard_map/psum | solution.py:34
  169.1 9.8 %all-reduce.10 = (f32[]{:T(128)}, f32[]{:T(128)}) all-reduce(f32[]{:T(128)} %get-tuple-element.14, f32[]{:T(128)} %get-tuple-element.15), channel_id=1, replica_groups=mesh['layer'=2,'px_0'=4,'px_1'=4,'py'=4] {'px_1'}, use_global_device_ids=true, to_apply=%region_13.14 | all-reduce | flops 2 | bytes 16 | tf_op jit(solution)/shard_map/psum | solution.py:34
  178.9 10.9 %all-reduce.8 = (f32[]{:T(128)}, f32[]{:T(128)}) all-reduce(f32[]{:T(128)} %get-tuple-element.10, f32[]{:T(128)} %get-tuple-element.11), channel_id=1, replica_groups=mesh['layer'=2,'px_0'=4,'px_1'=4,'py'=4] {'py'}, use_global_device_ids=true, to_apply=%region_14.15 | all-reduce | flops 2 | bytes 16 | tf_op jit(solution)/shard_map/psum | solution.py:34
  194.4 6.0 %multiply_subtract_fusion = (f32[4,128,1024]{2,1,0:T(8,128)}, f32[4,128,1024]{2,1,0:T(8,128)}) fusion(f32[4,128,1024]{2,1,0:T(8,128)} %copy-done.4, f32[4,128,1024]{2,1,0:T(8,128)} %get-tuple-element.22, f32[4,128,1024]{2,1,0:T(8,128)} %get-tuple-element.31, f32[]{:T(128)S(6)} %div.45, f32[]{:T(128)S(6)} %div.47, f32[1,128,1024]{2,1,0:T(8,128)} %bitcast.240, ...), kind=kLoop, calls=%fused_computation.51 | loop fusion | flops 7864320 | bytes 14680076 | tf_op jit(solution)/shard_map/sub | solution.py:152
  (108 shorter events, 10.7 us)
Async XLA Ops:
  0.6 5.0 %copy-start.2 = (f32[4,128,1024]{2,1,0:T(8,128)S(1)}, f32[4,128,1024]{2,1,0:T(8,128)}, u32[]{:S(2)}) copy-start(f32[4,128,1024]{2,1,0:T(8,128)} %param.7) | copy-start | bytes 6291460
  0.7 8.8 %copy-start = (f32[4,128,1024]{2,1,0:T(8,128)S(1)}, f32[4,128,1024]{2,1,0:T(8,128)}, u32[]{:S(2)}) copy-start(f32[4,128,1024]{2,1,0:T(8,128)} %param.8) | copy-start | bytes 6291460
  3.7 14.2 %copy-start.8 = (f32[4,128,1024]{2,1,0:T(8,128)S(1)}, f32[4,128,1024]{2,1,0:T(8,128)}, u32[]{:S(2)}) copy-start(f32[4,128,1024]{2,1,0:T(8,128)} %param.11) | copy-start | bytes 6291460
  3.7 14.2 %collective-permute-start = (f32[1,128,1024]{2,1,0:T(8,128)S(1)}, f32[1,128,1024]{2,1,0:T(8,128)S(1)}, u32[]{:S(2)}, u32[]{:S(2)}) collective-permute-start(f32[1,128,1024]{2,1,0:T(8,128)S(1)} %slice.202), channel_id=1, source_target_pairs={{0,64},{1,65},{2,66},{3,67},{4,68},{5,69},{6,70},{7,71},{8,72},{9,... | collective-permute-start | bytes 1572872 | tf_op jit(solution)/shard_map/ppermute | solution.py:41
  5.6 12.3 %collective-permute-start.1 = (f32[4,1,1024]{2,1,0:T(1,128)S(1)}, f32[4,1,1024]{2,1,0:T(1,128)S(1)}, u32[]{:S(2)}, u32[]{:S(2)}) collective-permute-start(f32[4,1,1024]{2,1,0:T(1,128)S(1)} %slice.173), channel_id=1, source_target_pairs={{0,4},{4,8},{8,12},{12,16},{16,20},{20,24},{24,28},{28,32},{32,36}... | collective-permute-start | bytes 49160 | tf_op jit(solution)/shard_map/ppermute | solution.py:41
  9.6 8.3 %collective-permute-start.2 = (f32[4,128,1]{2,1,0:T(8,128)S(1)}, f32[4,128,1]{2,1,0:T(8,128)S(1)}, u32[]{:S(2)}, u32[]{:S(2)}) collective-permute-start(f32[4,128,1]{2,1,0:T(8,128)S(1)} %slice.175), channel_id=1, source_target_pairs={{0,1},{1,2},{2,3},{4,5},{5,6},{6,7},{8,9},{9,10},{10,11},{12,13},{... | collective-permute-start | bytes 6152 | tf_op jit(solution)/shard_map/ppermute | solution.py:41
  13.2 46.7 %copy-start.6 = (f32[3,128,1024]{2,1,0:T(8,128)}, f32[3,128,1024]{2,1,0:T(8,128)S(1)}, u32[]{:S(2)}) copy-start(f32[3,128,1024]{2,1,0:T(8,128)S(1)} %slice.206) | copy-start | bytes 4718596
  19.7 3.4 %copy-start.5 = (f32[4,128,1024]{2,1,0:T(8,128)S(1)}, f32[4,128,1024]{2,1,0:T(8,128)}, u32[]{:S(2)}) copy-start(f32[4,128,1024]{2,1,0:T(8,128)} %param.6) | copy-start | bytes 6291460
  20.2 2.9 %collective-permute-start.3 = (f32[128,1024]{1,0:T(8,128)S(1)}, f32[128,1024]{1,0:T(8,128)S(1)}, u32[]{:S(2)}, u32[]{:S(2)}) collective-permute-start(f32[128,1024]{1,0:T(8,128)S(1)} %fusion.30), channel_id=1, source_target_pairs={{0,64},{1,65},{2,66},{3,67},{4,68},{5,69},{6,70},{7,71},{8,72},{9,... | collective-permute-start | bytes 1572872 | tf_op jit(solution)/shard_map/ppermute | solution.py:41
  24.0 4.9 %copy-start.25 = (f32[128,1024]{1,0:T(8,128)}, f32[128,1024]{1,0:T(8,128)S(1)}, u32[]{:S(2)}) copy-start(f32[128,1024]{1,0:T(8,128)S(1)} %get-tuple-element.43) | copy-start | bytes 1572868
  24.0 4.9 %copy-start.27 = (f32[128,1024]{1,0:T(8,128)}, f32[128,1024]{1,0:T(8,128)S(1)}, u32[]{:S(2)}) copy-start(f32[128,1024]{1,0:T(8,128)S(1)} %get-tuple-element.45) | copy-start | bytes 1572868
  24.0 4.9 %copy-start.29 = (f32[128,1024]{1,0:T(8,128)}, f32[128,1024]{1,0:T(8,128)S(1)}, u32[]{:S(2)}) copy-start(f32[128,1024]{1,0:T(8,128)S(1)} %get-tuple-element.47) | copy-start | bytes 1572868
  24.0 8.7 %copy-start.11 = (f32[128,1024]{1,0:T(8,128)}, f32[128,1024]{1,0:T(8,128)S(1)}, u32[]{:S(2)}) copy-start(f32[128,1024]{1,0:T(8,128)S(1)} %get-tuple-element.41) | copy-start | bytes 1572868
  24.0 12.6 %copy-start.17 = (f32[128,1024]{1,0:T(8,128)}, f32[128,1024]{1,0:T(8,128)S(1)}, u32[]{:S(2)}) copy-start(f32[128,1024]{1,0:T(8,128)S(1)} %get-tuple-element.42) | copy-start | bytes 1572868
  24.1 12.6 %copy-start.19 = (f32[128,1024]{1,0:T(8,128)}, f32[128,1024]{1,0:T(8,128)S(1)}, u32[]{:S(2)}) copy-start(f32[128,1024]{1,0:T(8,128)S(1)} %get-tuple-element.44) | copy-start | bytes 1572868
  24.1 12.6 %copy-start.21 = (f32[128,1024]{1,0:T(8,128)}, f32[128,1024]{1,0:T(8,128)S(1)}, u32[]{:S(2)}) copy-start(f32[128,1024]{1,0:T(8,128)S(1)} %get-tuple-element.46) | copy-start | bytes 1572868
  24.1 3.8 %collective-permute-start.4 = (f32[128,1024]{1,0:T(8,128)S(1)}, f32[128,1024]{1,0:T(8,128)S(1)}, u32[]{:S(2)}, u32[]{:S(2)}) collective-permute-start(f32[128,1024]{1,0:T(8,128)S(1)} %get-tuple-element.40), channel_id=1, source_target_pairs={{0,64},{1,65},{2,66},{3,67},{4,68},{5,69},{6,70},{7,71},{8,72},{9,... | collective-permute-start | bytes 1572872 | tf_op jit(solution)/shard_map/ppermute | solution.py:41
  28.9 3.8 %collective-permute-start.5 = (f32[128,1024]{1,0:T(8,128)S(1)}, f32[128,1024]{1,0:T(8,128)S(1)}, u32[]{:S(2)}, u32[]{:S(2)}) collective-permute-start(f32[128,1024]{1,0:T(8,128)S(1)} %get-tuple-element.36), channel_id=1, source_target_pairs={{64,0},{65,1},{66,2},{67,3},{68,4},{69,5},{70,6},{71,7},{72,8},{73... | collective-permute-start | bytes 1572872 | tf_op jit(solution)/shard_map/ppermute | solution.py:41
  33.0 3.6 %collective-permute-start.6 = (f32[1,128,1024]{2,1,0:T(8,128)S(1)}, f32[1,128,1024]{2,1,0:T(8,128)S(1)}, u32[]{:S(2)}, u32[]{:S(2)}) collective-permute-start(f32[1,128,1024]{2,1,0:T(8,128)S(1)} %bitcast.233), channel_id=1, source_target_pairs={{0,64},{1,65},{2,66},{3,67},{4,68},{5,69},{6,70},{7,71},{8,72},{9,... | collective-permute-start | bytes 1572872 | tf_op jit(solution)/shard_map/ppermute | solution.py:20
  37.4 22.6 %copy-start.13 = (f32[128,1024]{1,0:T(8,128)}, f32[128,1024]{1,0:T(8,128)S(1)}, u32[]{:S(2)}) copy-start(f32[128,1024]{1,0:T(8,128)S(1)} %get-tuple-element.34) | copy-start | bytes 1572868
  37.4 22.6 %copy-start.14 = (f32[128,1024]{1,0:T(8,128)}, f32[128,1024]{1,0:T(8,128)S(1)}, u32[]{:S(2)}) copy-start(f32[128,1024]{1,0:T(8,128)S(1)} %get-tuple-element.35) | copy-start | bytes 1572868
  37.4 22.6 %copy-start.23 = (f32[1,128,1024]{2,1,0:T(8,128)}, f32[1,128,1024]{2,1,0:T(8,128)S(1)}, u32[]{:S(2)}) copy-start(f32[1,128,1024]{2,1,0:T(8,128)S(1)} %get-tuple-element.33) | copy-start | bytes 1572868
  37.4 16.4 %collective-permute-start.7 = (f32[1,128,1024]{2,1,0:T(8,128)S(1)}, f32[1,128,1024]{2,1,0:T(8,128)S(1)}, u32[]{:S(2)}, u32[]{:S(2)}) collective-permute-start(f32[1,128,1024]{2,1,0:T(8,128)S(1)} %get-tuple-element.33), channel_id=1, source_target_pairs={{64,0},{65,1},{66,2},{67,3},{68,4},{69,5},{70,6},{71,7},{72,8},{73... | collective-permute-start | bytes 1572872 | tf_op jit(solution)/shard_map/ppermute | solution.py:21
  39.0 21.0 %copy-start.32 = (f32[1,128,1024]{2,1,0:T(8,128)S(1)}, f32[1,128,1024]{2,1,0:T(8,128)}, u32[]{:S(2)}) copy-start(f32[1,128,1024]{2,1,0:T(8,128)} %copy-done.31) | copy-start | bytes 1572868
  39.1 14.6 %collective-permute-start.9 = (f32[4,1,1024]{2,1,0:T(1,128)S(1)}, f32[4,1,1024]{2,1,0:T(1,128)S(1)}, u32[]{:S(2)}, u32[]{:S(2)}) collective-permute-start(f32[4,1,1024]{2,1,0:T(1,128)S(1)} %get-tuple-element.54), channel_id=1, source_target_pairs={{0,4},{4,8},{8,12},{12,16},{16,20},{20,24},{24,28},{28,32},{32,36}... | collective-permute-start | bytes 49160 | tf_op jit(solution)/shard_map/ppermute | solution.py:20
  43.0 10.7 %collective-permute-start.8 = (f32[4,1,1024]{2,1,0:T(1,128)S(1)}, f32[4,1,1024]{2,1,0:T(1,128)S(1)}, u32[]{:S(2)}, u32[]{:S(2)}) collective-permute-start(f32[4,1,1024]{2,1,0:T(1,128)S(1)} %get-tuple-element.55), channel_id=1, source_target_pairs={{4,0},{8,4},{12,8},{16,12},{20,16},{24,20},{28,24},{32,28},{36,32}... | collective-permute-start | bytes 49160 | tf_op jit(solution)/shard_map/ppermute | solution.py:21
  47.3 11.4 %collective-permute-start.10 = (f32[4,128,1]{2,1,0:T(8,128)S(1)}, f32[4,128,1]{2,1,0:T(8,128)S(1)}, u32[]{:S(2)}, u32[]{:S(2)}) collective-permute-start(f32[4,128,1]{2,1,0:T(8,128)S(1)} %get-tuple-element.52), channel_id=1, source_target_pairs={{1,0},{2,1},{3,2},{5,4},{6,5},{7,6},{9,8},{10,9},{11,10},{13,12},{... | collective-permute-start | bytes 6152 | tf_op jit(solution)/shard_map/ppermute | solution.py:21
  48.6 11.3 %collective-permute-start.11 = (f32[4,128,1]{2,1,0:T(8,128)S(1)}, f32[4,128,1]{2,1,0:T(8,128)S(1)}, u32[]{:S(2)}, u32[]{:S(2)}) collective-permute-start(f32[4,128,1]{2,1,0:T(8,128)S(1)} %get-tuple-element.53), channel_id=1, source_target_pairs={{0,1},{1,2},{2,3},{4,5},{5,6},{6,7},{8,9},{9,10},{10,11},{12,13},{... | collective-permute-start | bytes 6152 | tf_op jit(solution)/shard_map/ppermute | solution.py:20
  108.1 38.8 %copy-start.4 = (f32[4,128,1024]{2,1,0:T(8,128)}, f32[4,128,1024]{2,1,0:T(8,128)S(1)}, u32[]{:S(2)}) copy-start(f32[4,128,1024]{2,1,0:T(8,128)S(1)} %multiply_subtract_fusion.1) | copy-start | bytes 6291460
  108.1 3.6 %copy-start.18 = (f32[128,1024]{1,0:T(8,128)S(1)}, f32[128,1024]{1,0:T(8,128)}, u32[]{:S(2)}) copy-start(f32[128,1024]{1,0:T(8,128)} %copy-done.17) | copy-start | bytes 1572868
  108.1 3.6 %copy-start.20 = (f32[128,1024]{1,0:T(8,128)S(1)}, f32[128,1024]{1,0:T(8,128)}, u32[]{:S(2)}) copy-start(f32[128,1024]{1,0:T(8,128)} %copy-done.19) | copy-start | bytes 1572868
  108.2 3.6 %copy-start.22 = (f32[128,1024]{1,0:T(8,128)S(1)}, f32[128,1024]{1,0:T(8,128)}, u32[]{:S(2)}) copy-start(f32[128,1024]{1,0:T(8,128)} %copy-done.21) | copy-start | bytes 1572868
  108.8 2.9 %collective-permute-start.12 = (f32[128,1024]{1,0:T(8,128)S(1)}, f32[128,1024]{1,0:T(8,128)S(1)}, u32[]{:S(2)}, u32[]{:S(2)}) collective-permute-start(f32[128,1024]{1,0:T(8,128)S(1)} %add_multiply_fusion.3), channel_id=1, source_target_pairs={{0,64},{1,65},{2,66},{3,67},{4,68},{5,69},{6,70},{7,71},{8,72},{9,... | collective-permute-start | bytes 1572872 | tf_op jit(solution)/shard_map/ppermute | solution.py:41
  112.8 3.8 %collective-permute-start.13 = (f32[128,1024]{1,0:T(8,128)S(1)}, f32[128,1024]{1,0:T(8,128)S(1)}, u32[]{:S(2)}, u32[]{:S(2)}) collective-permute-start(f32[128,1024]{1,0:T(8,128)S(1)} %get-tuple-element.27), channel_id=1, source_target_pairs={{64,0},{65,1},{66,2},{67,3},{68,4},{69,5},{70,6},{71,7},{72,8},{73... | collective-permute-start | bytes 1572872 | tf_op jit(solution)/shard_map/ppermute | solution.py:41
  116.9 30.1 %copy-start.10 = (f32[128,1024]{1,0:T(8,128)}, f32[128,1024]{1,0:T(8,128)S(1)}, u32[]{:S(2)}) copy-start(f32[128,1024]{1,0:T(8,128)S(1)} %multiply_add_fusion.3) | copy-start | bytes 1572868
  116.9 3.6 %collective-permute-start.14 = (f32[1,128,1024]{2,1,0:T(8,128)S(1)}, f32[1,128,1024]{2,1,0:T(8,128)S(1)}, u32[]{:S(2)}, u32[]{:S(2)}) collective-permute-start(f32[1,128,1024]{2,1,0:T(8,128)S(1)} %bitcast.237), channel_id=1, source_target_pairs={{0,64},{1,65},{2,66},{3,67},{4,68},{5,69},{6,70},{7,71},{8,72},{9,... | collective-permute-start | bytes 1572872 | tf_op jit(solution)/shard_map/ppermute | solution.py:20
  122.6 24.4 %copy-start.15 = (f32[128,1024]{1,0:T(8,128)}, f32[128,1024]{1,0:T(8,128)S(1)}, u32[]{:S(2)}) copy-start(f32[128,1024]{1,0:T(8,128)S(1)} %get-tuple-element.25) | copy-start | bytes 1572868
  122.6 24.4 %copy-start.16 = (f32[128,1024]{1,0:T(8,128)}, f32[128,1024]{1,0:T(8,128)S(1)}, u32[]{:S(2)}) copy-start(f32[128,1024]{1,0:T(8,128)S(1)} %get-tuple-element.26) | copy-start | bytes 1572868
  122.6 24.4 %copy-start.24 = (f32[1,128,1024]{2,1,0:T(8,128)}, f32[1,128,1024]{2,1,0:T(8,128)S(1)}, u32[]{:S(2)}) copy-start(f32[1,128,1024]{2,1,0:T(8,128)S(1)} %get-tuple-element.24) | copy-start | bytes 1572868
  122.6 18.4 %collective-permute-start.15 = (f32[1,128,1024]{2,1,0:T(8,128)S(1)}, f32[1,128,1024]{2,1,0:T(8,128)S(1)}, u32[]{:S(2)}, u32[]{:S(2)}) collective-permute-start(f32[1,128,1024]{2,1,0:T(8,128)S(1)} %get-tuple-element.24), channel_id=1, source_target_pairs={{64,0},{65,1},{66,2},{67,3},{68,4},{69,5},{70,6},{71,7},{72,8},{73... | collective-permute-start | bytes 1572872 | tf_op jit(solution)/shard_map/ppermute | solution.py:21
  124.7 22.3 %copy-start.9 = (f32[4,128,1024]{2,1,0:T(8,128)S(1)}, f32[4,128,1024]{2,1,0:T(8,128)}, u32[]{:S(2)}) copy-start(f32[4,128,1024]{2,1,0:T(8,128)} %param.11) | copy-start | bytes 6291460
  125.5 21.4 %copy-start.3 = (f32[4,128,1024]{2,1,0:T(8,128)S(1)}, f32[4,128,1024]{2,1,0:T(8,128)}, u32[]{:S(2)}) copy-start(f32[4,128,1024]{2,1,0:T(8,128)} %param.7) | copy-start | bytes 6291460
  125.5 21.4 %copy-start.7 = (f32[3,128,1024]{2,1,0:T(8,128)S(1)}, f32[3,128,1024]{2,1,0:T(8,128)}, u32[]{:S(2)}) copy-start(f32[3,128,1024]{2,1,0:T(8,128)} %copy-done.6) | copy-start | bytes 4718596
  125.8 21.2 %copy-start.1 = (f32[4,128,1024]{2,1,0:T(8,128)S(1)}, f32[4,128,1024]{2,1,0:T(8,128)}, u32[]{:S(2)}) copy-start(f32[4,128,1024]{2,1,0:T(8,128)} %param.8) | copy-start | bytes 6291460
  125.8 15.1 %collective-permute-start.17 = (f32[4,1,1024]{2,1,0:T(1,128)S(1)}, f32[4,1,1024]{2,1,0:T(1,128)S(1)}, u32[]{:S(2)}, u32[]{:S(2)}) collective-permute-start(f32[4,1,1024]{2,1,0:T(1,128)S(1)} %get-tuple-element.50), channel_id=1, source_target_pairs={{0,4},{4,8},{8,12},{12,16},{16,20},{20,24},{24,28},{28,32},{32,36}... | collective-permute-start | bytes 49160 | tf_op jit(solution)/shard_map/ppermute | solution.py:20
  129.7 11.2 %collective-permute-start.16 = (f32[4,1,1024]{2,1,0:T(1,128)S(1)}, f32[4,1,1024]{2,1,0:T(1,128)S(1)}, u32[]{:S(2)}, u32[]{:S(2)}) collective-permute-start(f32[4,1,1024]{2,1,0:T(1,128)S(1)} %get-tuple-element.51), channel_id=1, source_target_pairs={{4,0},{8,4},{12,8},{16,12},{20,16},{24,20},{28,24},{32,28},{36,32}... | collective-permute-start | bytes 49160 | tf_op jit(solution)/shard_map/ppermute | solution.py:21
  135.1 10.7 %collective-permute-start.18 = (f32[4,128,1]{2,1,0:T(8,128)S(1)}, f32[4,128,1]{2,1,0:T(8,128)S(1)}, u32[]{:S(2)}, u32[]{:S(2)}) collective-permute-start(f32[4,128,1]{2,1,0:T(8,128)S(1)} %get-tuple-element.48), channel_id=1, source_target_pairs={{1,0},{2,1},{3,2},{5,4},{6,5},{7,6},{9,8},{10,9},{11,10},{13,12},{... | collective-permute-start | bytes 6152 | tf_op jit(solution)/shard_map/ppermute | solution.py:21
  136.4 10.6 %collective-permute-start.19 = (f32[4,128,1]{2,1,0:T(8,128)S(1)}, f32[4,128,1]{2,1,0:T(8,128)S(1)}, u32[]{:S(2)}, u32[]{:S(2)}) collective-permute-start(f32[4,128,1]{2,1,0:T(8,128)S(1)} %get-tuple-element.49), channel_id=1, source_target_pairs={{0,1},{1,2},{2,3},{4,5},{5,6},{6,7},{8,9},{9,10},{10,11},{12,13},{... | collective-permute-start | bytes 6152 | tf_op jit(solution)/shard_map/ppermute | solution.py:20
  (6 other events, 13.0 us)
where the time goes:
time: 201 us
  blocking collectives  66.7 us (33%)
  starting transfers between devices  52.4 us (26%)
  other arithmetic  40.2 us (20%)
  waiting for transfers between devices  27.4 us (14%)
  between operations  7.53 us (4%)
  local copies, waits for them, and re-layouts  6.31 us (3%)
    psum x8, blocking collectives, by_axis(): value = lax.psum(value, axis)  66.7 us
    ppermute x6, starting transfers between devices, extended(): lax.ppermute(last, axis, up)  21.6 us
    reduce_sum x2, other arithmetic, paired_sums(): jnp.sum(image * precond)  20 us
    ppermute x8, starting transfers between devices, from_behind(): return lax.ppermute(value, axis, pairs)  17.2 us
    ppermute x8, waiting for transfers between devices, from_behind(): return lax.ppermute(value, axis, pairs)  13.9 us
    ppermute x6, starting transfers between devices, extended(): lax.ppermute(initial, axis, [(b, a) for a, b in up])  13.6 us
    sub x2, other arithmetic, shards(): residual = residual - alpha * along  8.84 us
    ppermute x6, waiting for transfers between devices, extended(): lax.ppermute(initial, axis, [(b, a) for a, b in up])  8.16 us
  transfers between devices with their start and end apart: 20, of which 12 were waited for; matrix products, arithmetic and copies ran while one was open for 2% of the time, Pallas kernels for 0%

commit v1 on v0

v1 whole, which is shorter than its diff:
```python
import functools

import jax
import jax.numpy as jnp
from jax import lax
from jax.experimental import pallas as pl
from jax.experimental.pallas import tpu as pltpu
from jax.sharding import Mesh
from jax.sharding import PartitionSpec as P

RIGHT, ROW, COL, VIA, GROUND = range(5)
FIELDS = 5
SUB, LANE = 8, 128
PX = ("px_0", "px_1")
ALL = ("layer", "px_0", "px_1", "py")


def lanes(shape):
    return lax.broadcasted_iota(jnp.int32, shape, len(shape) - 1)


def sublanes(shape):
    return lax.broadcasted_iota(jnp.int32, shape, len(shape) - 2)


def tile(index):
    return pl.ds(pl.multiple_of(index * SUB, SUB), SUB)


def position():
    px = lax.axis_index("px_0") * lax.axis_size("px_1") + lax.axis_index("px_1")
    return (lax.axis_index("layer"), px, lax.axis_index("py"))


def spec_of(kind):
    return pl.BlockSpec(memory_space=kind)


def call(body, operands, kinds, outs, scratch=(), alias=None, flops=0, moved=0, limit=8 << 20):
    shapes = [
        pltpu.VMEM(o, jnp.float32) if isinstance(o, tuple) else o for o in outs
    ]
    operands = [
        pltpu.with_memory_space_constraint(o, pltpu.VMEM) if k == pltpu.VMEM else o
        for o, k in zip(operands, kinds)
    ]
    return pl.pallas_call(
        body,
        out_shape=shapes,
        in_specs=[spec_of(k) for k in kinds],
        out_specs=[spec_of(pltpu.VMEM if isinstance(o, tuple) else pl.ANY) for o in outs],
        scratch_shapes=list(scratch),
        input_output_aliases=alias or {},
        compiler_params=pltpu.CompilerParams(vmem_limit_bytes=limit),
        cost_estimate=pl.CostEstimate(flops=flops, bytes_accessed=moved, transcendentals=0),
    )(*operands)


def layer_of(core, k, depth):
    return jnp.where(core == 0, k, depth - 1 - k)


def link_of(core, k, depth):
    upper = depth - 1 if k == depth - 1 else depth - 2 - k
    return jnp.where(core == 0, k, upper)


def load_kernel(depth, rows, cols, *refs):
    (right, row, col, via, mask, ground, e0, e1, e2, e3, e4, msg_right, msg_left, masks, pack, sem) = refs
    core, _, _ = position()
    fields = (e0, e1, e2, e3, e4)
    copies = []
    for k in range(depth):
        at = layer_of(core, k, depth)
        link = link_of(core, k, depth)
        for index, (source, layer, target) in enumerate(
            (
                (right, at, e0),
                (row, at, e1),
                (col, at, e2),
                (via, link, e3),
                (ground, at, e4),
                (mask, link, None),
            )
        ):
            into = masks.at[k] if target is None else target.at[k, 0:rows, 0:cols]
            copies.append(pltpu.make_async_copy(source.at[layer], into, sem.at[index, k]))
    for copy in copies:
        copy.start()
    for copy in copies:
        copy.wait()
    below = jnp.where(core == 0, 1.0, 0.0).astype(jnp.float32)
    last = cols - LANE
    lane = lanes((SUB, LANE))

    def step(t, _):
        for k in range(depth):
            value = e3[k, tile(t), 0:cols] * masks[k, tile(t), :].astype(jnp.float32)
            if k == depth - 1:
                value = value * below
            e3[k, tile(t), 0:cols] = value
        to_right = jnp.zeros((SUB, LANE), jnp.float32)
        to_left = jnp.zeros((SUB, LANE), jnp.float32)
        for f in range(FIELDS):
            for k in range(depth):
                q = f * depth + k
                tail = fields[f][k, tile(t), last:cols]
                head = fields[f][k, tile(t), 0:LANE]
                if f == GROUND:
                    across = pltpu.roll(e2[k, tile(t), last:cols], 1, 1)
                    tail = tail + jnp.where(lane == LANE - 2, across, 0.0)
                shift = 4 * q + 2
                to_right = jnp.where((lane // 2) == 2 * q, pltpu.roll(tail, shift, 1), to_right)
                to_left = jnp.where((lane // 2) == 2 * q + 1, pltpu.roll(head, shift, 1), to_left)
        pack[0, tile(t), :] = to_right
        pack[1, tile(t), :] = to_left
        return 0

    lax.fori_loop(0, rows // SUB, step, 0)
    used = msg_right.shape[0]
    msg_right[...] = pack[0].T[0:used]
    msg_left[...] = pack[1].T[0:used]


def column_kernel(depth, rows, cols, places, *refs):
    e_in, (from_left, from_right) = refs[0:5], refs[5:7]
    e = refs[7:12]
    msg_down, msg_up, both = refs[12:15]
    _, _, py = position()
    used = from_left.shape[0]
    both[...] = jnp.zeros_like(both)
    both[0:used] = from_left[...] + from_right[...]
    both[...] = both[...].T
    lane = lanes((SUB, LANE))
    keep = ((lane < 2) & (py < places - 1)) | ((lane >= LANE - 2) & (py > 0))

    def step(t, _):
        value = both[tile(t), :]
        for f in range(FIELDS):
            for k in range(depth):
                q = f * depth + k
                shift = (LANE - (4 * q + 2)) % LANE
                got = pltpu.roll(value, shift, 1)
                e[f][k, tile(t), cols : cols + LANE] = jnp.where(
                    keep, got, 1.0 if f == GROUND else 0.0
                )
        return 0

    lax.fori_loop(0, rows // SUB, step, 0)
    wide = cols + LANE
    sub = sublanes((SUB, wide))
    end = rows - SUB
    down = up = None
    for f in range(FIELDS):
        for k in range(depth):
            q = f * depth + k
            i = q % 4
            tail = e[f][k, end:rows, :]
            head = e[f][k, 0:SUB, :]
            if f == GROUND:
                across = pltpu.roll(e[ROW][k, end:rows, :], 1, 0)
                tail = tail + jnp.where(sub == SUB - 2, across, 0.0)
            tail = pltpu.roll(tail, (2 * i + 2) % SUB, 0)
            head = pltpu.roll(head, (2 * i) % SUB, 0)
            if i == 0:
                down, up = tail, head
            else:
                down = jnp.where(sub // 2 == i, tail, down)
                up = jnp.where(sub // 2 == i, head, up)
            if i == 3:
                msg_down[(q // 4) * SUB : (q // 4 + 1) * SUB, :] = down
                msg_up[(q // 4) * SUB : (q // 4 + 1) * SUB, :] = up


def row_kernel(depth, rows, cols, places, *refs):
    e_in, (from_above, from_below) = refs[0:5], refs[5:7]
    e = refs[7:12]
    fwd, gain, inv, out = refs[12:16]
    core, px, _ = position()
    wide = cols + LANE
    sub = sublanes((SUB, wide))
    top = (sub >= SUB - 2) & (px > 0)
    low = (sub < 2) & (px < places - 1)
    for f in range(FIELDS):
        for k in range(depth):
            q = f * depth + k
            i = q % 4
            m = (q // 4) * SUB
            above = pltpu.roll(from_above[m : m + SUB, :], (SUB - 2 - 2 * i) % SUB, 0)
            under = pltpu.roll(from_below[m : m + SUB, :], (SUB - 2 * i) % SUB, 0)
            fill = 1.0 if f == GROUND else 0.0
            e[f][k, rows : rows + SUB, :] = jnp.where(top, above, jnp.where(low, under, fill))
    count = rows // SUB + 1
    upper = core == 1

    def step(t, _):
        before = jnp.where(t == 0, count - 1, t - 1)
        g = f = v = None
        for k in range(depth):
            row = e[ROW][k, tile(t), :]
            col = e[COL][k, tile(t), :]
            row_upper = pltpu.roll(jnp.where(sub == SUB - 1, e[ROW][k, tile(before), :], row), 1, 0)
            pivot = e[GROUND][k, tile(t), :] + row + row_upper + col + pltpu.roll(col, 1, 1)
            value = e[RIGHT][k, tile(t), :]
            if k:
                pivot = pivot + v * (1.0 - g)
                value = value + v * f
            v = e[VIA][k, tile(t), :]
            if k < depth - 1:
                inverse = 1.0 / (pivot + v)
                f = value * inverse
                g = v * inverse
                fwd[k, tile(t), :] = f
                gain[k, tile(t), :] = g
                inv[k, tile(t), :] = inverse
            else:
                inverse = 1.0 / (pivot + v)
                g = v * inverse
                inverse = jnp.where(upper, 0.0, inverse)
                fwd[k, tile(t), :] = value * inverse
                inv[k, tile(t), :] = inverse
                out[1, tile(t), :] = jnp.where(upper, pivot, v * (1.0 - g))
                g = jnp.where(upper, 1.0, g)
                gain[k, tile(t), :] = g
                out[0, tile(t), :] = g * value
        return 0

    lax.fori_loop(0, count, step, 0)


def back(depth, t, fwd, gain, middle, out):
    value = middle
    for k in range(depth - 1, -1, -1):
        value = fwd[k, tile(t), :] + gain[k, tile(t), :] * value
        out[k, tile(t), :] = value


def neighbours(k, t, count, sub, wide, field, row, col, z, flow):
    nxt = jnp.where(t == count - 1, 0, t + 1)
    r = row[k, tile(t), :]
    c = col[k, tile(t), :]
    after = field[k, tile(nxt), :]
    down = pltpu.roll(jnp.where(sub == 0, after, z), SUB - 1, 0)
    here = r * z
    up = pltpu.roll(jnp.where(sub == SUB - 1, flow, here), 1, 0)
    total = r * down + up + c * pltpu.roll(z, wide - 1, 1) + pltpu.roll(c * z, 1, 1)
    return (total, after, here)


def image_kernel(depth, rows, cols, places, *refs):
    (right, row, col, via, fwd, gain, inv, mine, theirs, z, w, fwd2, out, inv4) = refs
    _, px, py = position()
    wide = cols + LANE
    count = rows // SUB + 1
    sub = sublanes((SUB, wide))

    def first(t, _):
        ratio = 1.0 / (mine[1, tile(t), :] + theirs[1, tile(t), :])
        inv4[tile(t), :] = ratio
        back(depth, t, fwd, gain, (mine[0, tile(t), :] + theirs[0, tile(t), :]) * ratio, z)
        return 0

    lax.fori_loop(0, count, first, 0)
    lane = lanes((SUB, wide))
    beyond = (lane >= cols) & (lane < cols + LANE // 2) & (py == places[1] - 1)

    for k in range(depth):

        def second(t, carry, k=k):
            flow, here = carry
            total, after, flow = neighbours(k, t, count, sub, wide, z, row, col, here, flow)
            value = right[k, tile(t), :] - total
            outside = beyond | ((t == count - 1) & (sub < SUB // 2) & (px == places[0] - 1))
            value = jnp.where(outside, 0.0, value)
            w[k, tile(t), :] = value
            if k:
                value = value + via[k - 1, tile(t), :] * fwd2[k - 1, tile(t), :]
            fwd2[k, tile(t), :] = value * inv[k, tile(t), :]
            if k == depth - 1:
                out[tile(t), :] = gain[k, tile(t), :] * value
            return (flow, after)

        end = tile(count - 1)
        lax.fori_loop(0, count, second, (row[k, end, :] * z[k, end, :], z[k, tile(0), :]))


def dots_kernel(depth, rows, cols, *refs):
    (row, col, fwd2, gain, mine, theirs, inv4, right, z, w, y, v, sums) = refs
    wide = cols + LANE
    count = rows // SUB + 1
    sub = sublanes((SUB, wide))

    def first(t, _):
        back(depth, t, fwd2, gain, (mine[tile(t), :] + theirs[tile(t), :]) * inv4[tile(t), :], y)
        return 0

    lax.fori_loop(0, count, first, 0)
    zero = jnp.zeros((SUB, cols), jnp.float32)
    acc = (zero,) * 4
    for k in range(depth):

        def second(t, carry, k=k):
            flow, here, rho, c, e, g = carry
            total, after, flow = neighbours(k, t, count, sub, wide, y, row, col, here, flow)
            ww = w[k, tile(t), 0:cols]
            zz = z[k, tile(t), 0:cols]
            yy = here[:, 0:cols]
            vv = ww - total[:, 0:cols]
            v[k, tile(t), :] = vv
            rho = rho + right[k, tile(t), 0:cols] * zz
            return (flow, after, rho, c + zz * ww, e + ww * yy, g + yy * vv)

        end = tile(count - 1)
        carry = lax.fori_loop(
            0, count - 1, second, (row[k, end, :] * y[k, end, :], y[k, tile(0), :]) + acc
        )
        acc = carry[2:]
    lane = lanes(sums.shape)
    result = jnp.zeros(sums.shape, jnp.float32)
    for i, part in enumerate(acc):
        total = jnp.sum(jnp.sum(part, axis=0, keepdims=True), axis=1, keepdims=True)
        result = jnp.where(lane == i, total, result)
    sums[...] = result


def final_kernel(depth, rows, cols, *refs):
    (sums, right, z, w, y, v, x_out, r_out, x, r, sem) = refs
    core, _, _ = position()
    total = jnp.sum(sums[...], axis=0, keepdims=True)
    lane = lanes(total.shape)
    rho, c, e, g = (
        jnp.sum(jnp.where(lane == i, total, 0.0), axis=1, keepdims=True) for i in range(4)
    )
    alpha = rho / c
    rho1 = alpha * (alpha * e - c)
    beta = rho1 / rho
    curvature = c - 2.0 * alpha * e + alpha * alpha * g
    alpha1 = rho1 / (curvature - beta * rho1 / alpha)
    near = jnp.broadcast_to(alpha + alpha1 * (1.0 + beta), (SUB, cols))
    far = jnp.broadcast_to(alpha1 * alpha, (SUB, cols))
    copies = []
    for k in range(depth):

        def step(t, _, k=k):
            x[k, tile(t), :] = near * z[k, tile(t), 0:cols] - far * y[k, tile(t), 0:cols]
            r[k, tile(t), :] = (
                right[k, tile(t), 0:cols] - near * w[k, tile(t), 0:cols] + far * v[k, tile(t), :]
            )
            return 0

        lax.fori_loop(0, rows // SUB, step, 0)
        at = layer_of(core, k, depth)
        for index, (value, target) in enumerate(((x, x_out), (r, r_out))):
            copy = pltpu.make_async_copy(value.at[k], target.at[at], sem.at[index, k])
            copy.start()
            copies.append(copy)
    for copy in copies:
        copy.wait()


def shift(value, axis, by):
    count = lax.axis_size(axis)
    return lax.ppermute(value, axis, [(i, (i + by) % count) for i in range(count)])


def shards(right_side, row_conduct, column_conduct, via_conduct, via_mask, ground_conduct):
    depth, rows, cols = right_side.shape
    places = (lax.axis_size(PX), lax.axis_size("py"))
    devices = lax.axis_size(ALL)
    tall, wide = rows + SUB, cols + LANE
    ext = (depth, tall, wide)
    vmem, hbm = pltpu.VMEM, pl.ANY
    size = depth * tall * wide
    part = functools.partial

    strips = (FIELDS * depth * 4, LANE)
    *e, msg_right, msg_left = call(
        part(load_kernel, depth, rows, cols),
        [right_side, row_conduct, column_conduct, via_conduct, via_mask, ground_conduct],
        [hbm] * 6,
        [ext] * FIELDS + [strips] * 2,
        [
            pltpu.VMEM((depth, rows, cols), jnp.int32),
            pltpu.VMEM((2, rows, LANE), jnp.float32),
            pltpu.SemaphoreType.DMA((6, depth)),
        ],
        flops=size,
        moved=24 * size,
    )
    from_left = shift(msg_right, "py", 1)
    from_right = shift(msg_left, "py", -1)
    strips = (FIELDS * depth * 2, wide)
    *e, msg_down, msg_up = call(
        part(column_kernel, depth, rows, cols, places[1]),
        [*e, from_left, from_right],
        [vmem] * 7,
        [ext] * FIELDS + [strips] * 2,
        [pltpu.VMEM((rows, LANE), jnp.float32)],
        alias={i: i for i in range(FIELDS)},
        flops=size,
    )
    from_above = shift(msg_down, PX, 1)
    from_below = shift(msg_up, PX, -1)
    *e, fwd, gain, inv, mine = call(
        part(row_kernel, depth, rows, cols, places[0]),
        [*e, from_above, from_below],
        [vmem] * 7,
        [ext] * FIELDS + [ext] * 3 + [(2, tall, wide)],
        alias={i: i for i in range(FIELDS)},
        flops=30 * size,
    )
    right, row, col, via, _ = e
    theirs = shift(mine, "layer", 1)
    z, w, fwd2, mine2, inv4 = call(
        part(image_kernel, depth, rows, cols, places),
        [right, row, col, via, fwd, gain, inv, mine, theirs],
        [vmem] * 9,
        [ext] * 3 + [(tall, wide)] * 2,
        flops=30 * size,
    )
    theirs2 = shift(mine2, "layer", 1)
    y, v, sums = call(
        part(dots_kernel, depth, rows, cols),
        [row, col, fwd2, gain, mine2, theirs2, inv4, right, z, w],
        [vmem] * 10,
        [ext, (depth, rows, cols), (devices, LANE)],
        flops=30 * size,
    )
    sums = lax.all_to_all(sums.reshape(devices, 1, LANE), ALL, 0, 0).reshape(devices, LANE)
    block = jax.ShapeDtypeStruct((depth, rows, cols), jnp.float32)
    return call(
        part(final_kernel, depth, rows, cols),
        [sums, right, z, w, y, v],
        [vmem] * 6,
        [block] * 2,
        [
            pltpu.VMEM((depth, rows, cols), jnp.float32),
            pltpu.VMEM((depth, rows, cols), jnp.float32),
            pltpu.SemaphoreType.DMA((2, depth)),
        ],
        flops=10 * size,
    )


def solution(mesh):
    count = mesh.shape["px"]
    inner = 4 if count % 4 == 0 else 1
    split = Mesh(
        mesh.devices.reshape(mesh.shape["layer"], count // inner, inner, mesh.shape["py"]),
        ALL,
    )
    spec = P("layer", PX, "py")
    return jax.shard_map(
        lambda *a: tuple(shards(*a)),
        mesh=split,
        in_specs=(spec,) * 6,
        out_specs=(spec, spec),
        check_vma=False,
    )
```

time: 201 us -> 74.1 us (0.37)
  the two profiles are of different devices: /device:TPU:2 before, /device:TPU:1 now
where the time goes in v1:
time: 74.1 us; the launch traced here: 73.8 us
  Pallas kernels  23.5 us (32%)
  blocking collectives  18.3 us (25%)
  starting transfers between devices  13.3 us (18%)
  local copies, waits for them, and re-layouts  9.54 us (13%)
  waiting for transfers between devices  8.44 us (11%)
    pallas_call x6, Pallas kernels, call(): pl.pallas_call(body, out_shape=shapes, in_specs=[spec_of(k) for k in kind...  23.5 us
    all_to_all x1, blocking collectives, shards(): lax.all_to_all(sums.reshape(devices, 1, LANE), ALL, 0, 0)  18.3 us
    ppermute x6, starting transfers between devices, shift(): lax.ppermute(value, axis, [(i, (i + by) % count) for i in range(count)])  13.3 us
    unnamed x12, local copies, waits for them, and re-layouts  9.54 us
    ppermute x6, waiting for transfers between devices, shift(): lax.ppermute(value, axis, [(i, (i + by) % count) for i in range(count)])  8.44 us
  transfers between devices with their start and end apart: 6, of which 4 were waited for; matrix products, arithmetic and copies ran while one was open for 0% of the time, Pallas kernels for 0%

profile of v1, /device:TPU:1, one launch (start us, length us, event | category | flops | bytes accessed | tf_op | source)
XLA Modules:
  0.0 73.8 jit_solution(16290384782735381087)
XLA Ops:
  0.6 0.0 copy-start
  0.6 1.6 %copy-done = f32[4,128,1024]{2,1,0:T(8,128)S(1)} copy-done((f32[4,128,1024]{2,1,0:T(8,128)S(1)}, f32[4,128,1024]{2,1,0:T(8,128)}, u32[]{:S(2)}) %copy-start) | copy-done | bytes 2097176
  2.2 0.0 copy-start.1
  2.2 1.6 %copy-done.1 = f32[4,128,1024]{2,1,0:T(8,128)S(1)} copy-done((f32[4,128,1024]{2,1,0:T(8,128)S(1)}, f32[4,128,1024]{2,1,0:T(8,128)}, u32[]{:S(2)}) %copy-start.1) | copy-done | bytes 2097176
  3.8 0.0 copy-start.2
  3.8 1.6 %copy-done.2 = f32[4,128,1024]{2,1,0:T(8,128)S(1)} copy-done((f32[4,128,1024]{2,1,0:T(8,128)S(1)}, f32[4,128,1024]{2,1,0:T(8,128)}, u32[]{:S(2)}) %copy-start.2) | copy-done | bytes 2097176
  5.4 0.0 copy-start.3
  5.4 1.6 %copy-done.3 = f32[4,128,1024]{2,1,0:T(8,128)S(1)} copy-done((f32[4,128,1024]{2,1,0:T(8,128)S(1)}, f32[4,128,1024]{2,1,0:T(8,128)}, u32[]{:S(2)}) %copy-start.3) | copy-done | bytes 2097176
  7.0 0.0 copy-start.4
  7.0 1.6 %copy-done.4 = s32[4,128,1024]{2,1,0:T(8,128)S(1)} copy-done((s32[4,128,1024]{2,1,0:T(8,128)S(1)}, s32[4,128,1024]{2,1,0:T(8,128)}, u32[]{:S(2)}) %copy-start.4) | copy-done | bytes 2097176
  8.6 0.0 copy-start.5
  8.6 1.6 %copy-done.5 = f32[4,128,1024]{2,1,0:T(8,128)S(1)} copy-done((f32[4,128,1024]{2,1,0:T(8,128)S(1)}, f32[4,128,1024]{2,1,0:T(8,128)}, u32[]{:S(2)}) %copy-start.5) | copy-done | bytes 2097176
  10.2 3.6 %shard_map.77 = (f32[4,136,1152]{2,1,0:T(8,128)S(1)}, f32[4,136,1152]{2,1,0:T(8,128)S(1)}, f32[4,136,1152]{2,1,0:T(8,128)S(1)}, f32[4,136,1152]{2,1,0:T(8,128)S(...) custom-call(f32[4,128,1024]{2,1,0:T(8,128)S(1)} %copy-done, ...), custom_call_target="tpu_custom_call" | custom-call | flops 626688 | bytes 15040512 | tf_op jit(solution)/shard_map/pallas_call | solution.py:47
  13.8 2.2 %collective-permute-start = (f32[80,128]{1,0:T(8,128)S(1)}, f32[80,128]{1,0:T(8,128)S(1)}, u32[]{:S(2)}, u32[]{:S(2)}) collective-permute-start(f32[80,128]{1,0:T(8,128)S(1)} %get-tuple-element.37), channel_id=1, source_target_pairs={{0,1},{1,2},{2,3},{3,0},{4,5},{5,6},{6,7},{7,4},{8,9},{9,10},{10,1... | collective-permute-start | bytes 122888 | tf_op jit(solution)/shard_map/ppermute | solution.py:363
  16.0 1.5 %collective-permute-start.1 = (f32[80,128]{1,0:T(8,128)S(1)}, f32[80,128]{1,0:T(8,128)S(1)}, u32[]{:S(2)}, u32[]{:S(2)}) collective-permute-start(f32[80,128]{1,0:T(8,128)S(1)} %get-tuple-element.38), channel_id=1, source_target_pairs={{0,3},{1,0},{2,1},{3,2},{4,7},{5,4},{6,5},{7,6},{8,11},{9,8},{10,9... | collective-permute-start | bytes 122888 | tf_op jit(solution)/shard_map/ppermute | solution.py:363
  17.5 1.3 %collective-permute-done.refs_5_ = f32[80,128]{1,0:T(8,128)S(1)} collective-permute-done((f32[80,128]{1,0:T(8,128)S(1)}, f32[80,128]{1,0:T(8,128)S(1)}, u32[]{:S(2)}, u32[]{:S(2)}) %collective-permute-start) | collective-permute-done | bytes 40992 | tf_op jit(solution)/shard_map/ppermute | solution.py:363
  18.8 0.0 collective-permute-done.1.refs_6_
  18.9 1.6 %shard_map.78 = (f32[4,136,1152]{2,1,0:T(8,128)S(1)}, f32[4,136,1152]{2,1,0:T(8,128)S(1)}, f32[4,136,1152]{2,1,0:T(8,128)S(1)}, f32[4,136,1152]{2,1,0:T(8,128)S(...) custom-call(f32[4,136,1152]{2,1,0:T(8,128)S(1)} %get-tuple-element.3, ...), custom_call_target="tpu_custom_call", output_to_operand_aliasing={{0}: (0, {}), {1}: (1, {}), {2}: (2, {}), {3}: (3, {}), {4}... | custom-call | flops 626688 | tf_op jit(solution)/shard_map/pallas_call | solution.py:47
  20.4 1.7 %collective-permute-start.2 = (f32[40,1152]{1,0:T(8,128)S(1)}, f32[40,1152]{1,0:T(8,128)S(1)}, u32[]{:S(2)}, u32[]{:S(2)}) collective-permute-start(f32[40,1152]{1,0:T(8,128)S(1)} %get-tuple-element.44), channel_id=1, source_target_pairs={{0,4},{4,8},{8,12},{12,16},{16,20},{20,24},{24,28},{28,32},{32,36}... | collective-permute-start | bytes 552968 | tf_op jit(solution)/shard_map/ppermute | solution.py:363
  22.1 4.4 %collective-permute-start.3 = (f32[40,1152]{1,0:T(8,128)S(1)}, f32[40,1152]{1,0:T(8,128)S(1)}, u32[]{:S(2)}, u32[]{:S(2)}) collective-permute-start(f32[40,1152]{1,0:T(8,128)S(1)} %get-tuple-element.45), channel_id=1, source_target_pairs={{0,60},{4,0},{8,4},{12,8},{16,12},{20,16},{24,20},{28,24},{32,28},... | collective-permute-start | bytes 552968 | tf_op jit(solution)/shard_map/ppermute | solution.py:363
  26.5 2.8 %collective-permute-done.2.refs_5_ = f32[40,1152]{1,0:T(8,128)S(1)} collective-permute-done((f32[40,1152]{1,0:T(8,128)S(1)}, f32[40,1152]{1,0:T(8,128)S(1)}, u32[]{:S(2)}, u32[]{:S(2)}) %collective-permute-start.2) | collective-permute-done | bytes 184352 | tf_op jit(solution)/shard_map/ppermute | solution.py:363
  29.4 0.0 collective-permute-done.3.refs_6_
  29.4 2.6 %shard_map.79 = (f32[4,136,1152]{2,1,0:T(8,128)S(1)}, f32[4,136,1152]{2,1,0:T(8,128)S(1)}, f32[4,136,1152]{2,1,0:T(8,128)S(1)}, f32[4,136,1152]{2,1,0:T(8,128)S(...) custom-call(f32[4,136,1152]{2,1,0:T(8,128)S(1)} %get-tuple-element.3, ...), custom_call_target="tpu_custom_call", output_to_operand_aliasing={{0}: (0, {}), {1}: (1, {}), {2}: (2, {}), {3}: (3, {}), {4}... | custom-call | flops 18800640 | tf_op jit(solution)/shard_map/pallas_call | solution.py:47
  32.0 3.1 %collective-permute-start.4 = (f32[2,136,1152]{2,1,0:T(8,128)S(1)}, f32[2,136,1152]{2,1,0:T(8,128)S(1)}, u32[]{:S(2)}, u32[]{:S(2)}) collective-permute-start(f32[2,136,1152]{2,1,0:T(8,128)S(1)} %get-tuple-element.53.refs_7_), channel_id=1, source_target_pairs={{0,64},{64,0},{1,65},{65,1},{2,66},{66,2},{3,67},{67,3},{4,68},{68... | collective-permute-start | bytes 3760136 | tf_op jit(solution)/shard_map/ppermute | solution.py:363
  35.0 2.6 %collective-permute-done.4.refs_8_ = f32[2,136,1152]{2,1,0:T(8,128)S(1)} collective-permute-done((f32[2,136,1152]{2,1,0:T(8,128)S(1)}, f32[2,136,1152]{2,1,0:T(8,128)S(1)}, u32[]{:S(2)}, u32[]{:S(2)}) %collective-permute-start.4) | collective-permute-done | bytes 1253408 | tf_op jit(solution)/shard_map/ppermute | solution.py:363
  37.6 6.8 %shard_map.80 = (f32[4,136,1152]{2,1,0:T(8,128)S(1)}, f32[4,136,1152]{2,1,0:T(8,128)S(1)}, f32[4,136,1152]{2,1,0:T(8,128)S(1)}, f32[136,1152]{1,0:T(8,128)S(1)}, f32[136,1152]{1,0:T(8,128)S(1)}) custom-call(f32[4,136,1152]{2,1,0:T(8,128)S(1)} %get-tuple-element.48.refs_0_.refs_7_.refs_1_, f32[4,136,1152]{2,1,0:T(8,128)S(1)} %get-tuple-element.46.refs_1_.refs_0_, ...), custom_call_target="tpu_custom_call" | custom-call | flops 18800640 | tf_op jit(solution)/shard_map/pallas_call | solution.py:47
  44.4 0.5 collective-permute-start.5
  44.9 1.7 %collective-permute-done.5.refs_5_ = f32[136,1152]{1,0:T(8,128)S(1)} collective-permute-done((f32[136,1152]{1,0:T(8,128)S(1)}, f32[136,1152]{1,0:T(8,128)S(1)}, u32[]{:S(2)}, u32[]{:S(2)}) %collective-permute-start.5) | collective-permute-done | bytes 626720 | tf_op jit(solution)/shard_map/ppermute | solution.py:363
  46.5 6.5 %shard_map.81 = (f32[4,136,1152]{2,1,0:T(8,128)S(1)}, f32[4,128,1024]{2,1,0:T(8,128)S(1)}, f32[128,128]{1,0:T(8,128)S(1)}) custom-call(f32[4,136,1152]{2,1,0:T(8,128)S(1)} %get-tuple-element.46.refs_1_.refs_0_, f32[4,136,1152]{2,1,0:T(8,128)S(1)} %get-tuple-element.47.refs_2_.refs_1_, f32[4,136,1152]{2,1,0:T(8,128)S(1)} %get-tuple-element.54.refs_2_, ...), custom_call_target="tpu_custom_call" | custom-call | flops 18800640 | tf_op jit(solution)/shard_map/pallas_call | solution.py:47
  53.1 18.3 %all_to_all.5 = f32[128,1,128]{2,1,0:T(1,128)S(1)} all-to-all(f32[128,1,128]{2,1,0:T(1,128)S(1)} %bitcast.5), channel_id=1, replica_groups=mesh['layer'=2,'px_0'=4,'px_1'=4,'py'=4] {'layer','px_0','px_1','py'}, dimensions={0} | all-to-all | bytes 131072 | tf_op jit(solution)/shard_map/all_to_all | solution.py:429
  71.4 2.4 %shard_map.82 = (f32[4,128,1024]{2,1,0:T(8,128)}, f32[4,128,1024]{2,1,0:T(8,128)}) custom-call(f32[128,128]{1,0:T(8,128)S(1)} %bitcast.4, f32[4,136,1152]{2,1,0:T(8,128)S(1)} %get-tuple-element.48.refs_0_.refs_7_.refs_1_, f32[4,136,1152]{2,1,0:T(8,128)S(1)} %get-tuple-element.57.refs_8_.refs_2_, f32[4,136,1152]{2,1,0:T(8,128)S(1)} %get-tuple-element.58.refs_9_.refs_3_, ...), custom_call_target="tpu_custom_call" | custom-call | flops 6266880 | tf_op jit(solution)/shard_map/pallas_call | solution.py:47
Async XLA Ops:
  0.6 1.6 %copy-start = (f32[4,128,1024]{2,1,0:T(8,128)S(1)}, f32[4,128,1024]{2,1,0:T(8,128)}, u32[]{:S(2)}) copy-start(f32[4,128,1024]{2,1,0:T(8,128)} %refs_0_.1) | copy-start | bytes 6291460
  2.2 1.6 %copy-start.1 = (f32[4,128,1024]{2,1,0:T(8,128)S(1)}, f32[4,128,1024]{2,1,0:T(8,128)}, u32[]{:S(2)}) copy-start(f32[4,128,1024]{2,1,0:T(8,128)} %refs_1_.1) | copy-start | bytes 6291460
  3.8 1.6 %copy-start.2 = (f32[4,128,1024]{2,1,0:T(8,128)S(1)}, f32[4,128,1024]{2,1,0:T(8,128)}, u32[]{:S(2)}) copy-start(f32[4,128,1024]{2,1,0:T(8,128)} %refs_2_.1) | copy-start | bytes 6291460
  5.4 1.6 %copy-start.3 = (f32[4,128,1024]{2,1,0:T(8,128)S(1)}, f32[4,128,1024]{2,1,0:T(8,128)}, u32[]{:S(2)}) copy-start(f32[4,128,1024]{2,1,0:T(8,128)} %refs_3_.1) | copy-start | bytes 6291460
  7.0 1.6 %copy-start.4 = (s32[4,128,1024]{2,1,0:T(8,128)S(1)}, s32[4,128,1024]{2,1,0:T(8,128)}, u32[]{:S(2)}) copy-start(s32[4,128,1024]{2,1,0:T(8,128)} %refs_4_.1) | copy-start | bytes 6291460
  8.6 1.6 %copy-start.5 = (f32[4,128,1024]{2,1,0:T(8,128)S(1)}, f32[4,128,1024]{2,1,0:T(8,128)}, u32[]{:S(2)}) copy-start(f32[4,128,1024]{2,1,0:T(8,128)} %refs_5_.1) | copy-start | bytes 6291460
  13.8 5.0 %collective-permute-start = (f32[80,128]{1,0:T(8,128)S(1)}, f32[80,128]{1,0:T(8,128)S(1)}, u32[]{:S(2)}, u32[]{:S(2)}) collective-permute-start(f32[80,128]{1,0:T(8,128)S(1)} %get-tuple-element.37), channel_id=1, source_target_pairs={{0,1},{1,2},{2,3},{3,0},{4,5},{5,6},{6,7},{7,4},{8,9},{9,10},{10,1... | collective-permute-start | bytes 122888 | tf_op jit(solution)/shard_map/ppermute | solution.py:363
  16.0 2.9 %collective-permute-start.1 = (f32[80,128]{1,0:T(8,128)S(1)}, f32[80,128]{1,0:T(8,128)S(1)}, u32[]{:S(2)}, u32[]{:S(2)}) collective-permute-start(f32[80,128]{1,0:T(8,128)S(1)} %get-tuple-element.38), channel_id=1, source_target_pairs={{0,3},{1,0},{2,1},{3,2},{4,7},{5,4},{6,5},{7,6},{8,11},{9,8},{10,9... | collective-permute-start | bytes 122888 | tf_op jit(solution)/shard_map/ppermute | solution.py:363
  20.4 8.9 %collective-permute-start.2 = (f32[40,1152]{1,0:T(8,128)S(1)}, f32[40,1152]{1,0:T(8,128)S(1)}, u32[]{:S(2)}, u32[]{:S(2)}) collective-permute-start(f32[40,1152]{1,0:T(8,128)S(1)} %get-tuple-element.44), channel_id=1, source_target_pairs={{0,4},{4,8},{8,12},{12,16},{16,20},{20,24},{24,28},{28,32},{32,36}... | collective-permute-start | bytes 552968 | tf_op jit(solution)/shard_map/ppermute | solution.py:363
  22.1 7.2 %collective-permute-start.3 = (f32[40,1152]{1,0:T(8,128)S(1)}, f32[40,1152]{1,0:T(8,128)S(1)}, u32[]{:S(2)}, u32[]{:S(2)}) collective-permute-start(f32[40,1152]{1,0:T(8,128)S(1)} %get-tuple-element.45), channel_id=1, source_target_pairs={{0,60},{4,0},{8,4},{12,8},{16,12},{20,16},{24,20},{28,24},{32,28},... | collective-permute-start | bytes 552968 | tf_op jit(solution)/shard_map/ppermute | solution.py:363
  32.0 5.6 %collective-permute-start.4 = (f32[2,136,1152]{2,1,0:T(8,128)S(1)}, f32[2,136,1152]{2,1,0:T(8,128)S(1)}, u32[]{:S(2)}, u32[]{:S(2)}) collective-permute-start(f32[2,136,1152]{2,1,0:T(8,128)S(1)} %get-tuple-element.53.refs_7_), channel_id=1, source_target_pairs={{0,64},{64,0},{1,65},{65,1},{2,66},{66,2},{3,67},{67,3},{4,68},{68... | collective-permute-start | bytes 3760136 | tf_op jit(solution)/shard_map/ppermute | solution.py:363
  44.4 2.1 %collective-permute-start.5 = (f32[136,1152]{1,0:T(8,128)S(1)}, f32[136,1152]{1,0:T(8,128)S(1)}, u32[]{:S(2)}, u32[]{:S(2)}) collective-permute-start(f32[136,1152]{1,0:T(8,128)S(1)} %get-tuple-element.55.refs_4_), channel_id=1, source_target_pairs={{0,64},{64,0},{1,65},{65,1},{2,66},{66,2},{3,67},{67,3},{4,68},{68... | collective-permute-start | bytes 1880072 | tf_op jit(solution)/shard_map/ppermute | solution.py:363

commit v2 on v1

v2 whole, which is shorter than its diff:
```python
import functools

import jax
import jax.numpy as jnp
from jax import lax
from jax.experimental import pallas as pl
from jax.experimental.pallas import tpu as pltpu
from jax.sharding import Mesh
from jax.sharding import PartitionSpec as P

RIGHT, ROW, COL, VIA, GROUND = range(5)
FIELDS = 5
SUB, LANE = 8, 128
PX = ("px_0", "px_1")
ALL = ("layer", "px_0", "px_1", "py")


def lanes(shape):
    return lax.broadcasted_iota(jnp.int32, shape, len(shape) - 1)


def sublanes(shape):
    return lax.broadcasted_iota(jnp.int32, shape, len(shape) - 2)


def tile(index):
    return pl.ds(pl.multiple_of(index * SUB, SUB), SUB)


def position():
    px = lax.axis_index("px_0") * lax.axis_size("px_1") + lax.axis_index("px_1")
    return (lax.axis_index("layer"), px, lax.axis_index("py"))


def spec_of(kind):
    return pl.BlockSpec(memory_space=kind)


def call(body, operands, kinds, outs, scratch=(), alias=None, flops=0, moved=0, limit=8 << 20):
    shapes = [
        pltpu.VMEM(o, jnp.float32) if isinstance(o, tuple) else o for o in outs
    ]
    operands = [
        pltpu.with_memory_space_constraint(o, k) for o, k in zip(operands, kinds)
    ]
    return pl.pallas_call(
        body,
        out_shape=shapes,
        in_specs=[spec_of(k) for k in kinds],
        out_specs=[spec_of(pltpu.VMEM if isinstance(o, tuple) else pltpu.HBM) for o in outs],
        scratch_shapes=list(scratch),
        input_output_aliases=alias or {},
        compiler_params=pltpu.CompilerParams(vmem_limit_bytes=limit),
        cost_estimate=pl.CostEstimate(flops=flops, bytes_accessed=moved, transcendentals=0),
    )(*operands)


def layer_of(core, k, depth):
    return jnp.where(core == 0, k, depth - 1 - k)


def link_of(core, k, depth):
    upper = depth - 1 if k == depth - 1 else depth - 2 - k
    return jnp.where(core == 0, k, upper)


def copies_in(core, depth, rows, sources, targets, masks, sem, spans):
    copies = []
    for s, (low, high) in enumerate(spans):
        for k in range(depth):
            at, link = layer_of(core, k, depth), link_of(core, k, depth)
            for f, source in enumerate(sources):
                layer = link if f in (VIA, FIELDS) else at
                into = (
                    masks.at[k, :, s * (high - low) : (s + 1) * (high - low)]
                    if f == FIELDS
                    else targets[f].at[k, 0:rows, low:high]
                )
                copy = pltpu.make_async_copy(
                    source.at[layer, :, low:high], into, sem.at[s, f, k]
                )
                copy.start()
                copies.append(copy)
    return copies


def masked(core, depth, t, via, masks, low, high, start):
    for k in range(depth):
        value = via[k, tile(t), low:high] * masks[k, tile(t), start : start + high - low].astype(
            jnp.float32
        )
        if k == depth - 1:
            value = value * jnp.where(core == 0, 1.0, 0.0).astype(jnp.float32)
        via[k, tile(t), low:high] = value


def load_kernel(depth, rows, cols, *refs):
    sources, e = refs[0:6], refs[6:11]
    msg_right, msg_left, masks, pack, sem = refs[11:]
    core, _, _ = position()
    last = cols - LANE
    for copy in copies_in(core, depth, rows, sources, e, masks, sem, ((0, LANE), (last, cols))):
        copy.wait()
    lane = lanes((SUB, LANE))

    def step(t, _):
        masked(core, depth, t, e[VIA], masks, 0, LANE, 0)
        masked(core, depth, t, e[VIA], masks, last, cols, LANE)
        to_right = jnp.zeros((SUB, LANE), jnp.float32)
        to_left = jnp.zeros((SUB, LANE), jnp.float32)
        for f in range(FIELDS):
            for k in range(depth):
                q = f * depth + k
                tail = e[f][k, tile(t), last:cols]
                head = e[f][k, tile(t), 0:LANE]
                if f == GROUND:
                    across = pltpu.roll(e[COL][k, tile(t), last:cols], 1, 1)
                    tail = tail + jnp.where(lane == LANE - 2, across, 0.0)
                shift = 4 * q + 2
                to_right = jnp.where((lane // 2) == 2 * q, pltpu.roll(tail, shift, 1), to_right)
                to_left = jnp.where((lane // 2) == 2 * q + 1, pltpu.roll(head, shift, 1), to_left)
        pack[0, tile(t), :] = to_right
        pack[1, tile(t), :] = to_left
        return 0

    lax.fori_loop(0, rows // SUB, step, 0)
    used = msg_right.shape[0]
    msg_right[...] = pack[0].T[0:used]
    msg_left[...] = pack[1].T[0:used]


def middle_kernel(depth, rows, cols, *refs):
    sources, e, masks, sem = refs[0:6], refs[11:16], refs[16], refs[17]
    core, _, _ = position()
    low, high = LANE, cols - LANE
    for copy in copies_in(core, depth, rows, sources, e, masks, sem, ((low, high),)):
        copy.wait()

    def step(t, _):
        masked(core, depth, t, e[VIA], masks, low, high, 0)
        return 0

    lax.fori_loop(0, rows // SUB, step, 0)


def unpack_columns(depth, cols, keep, t, both, e):
    value = both[tile(t), :]
    for f in range(FIELDS):
        for k in range(depth):
            got = pltpu.roll(value, (LANE - (4 * (f * depth + k) + 2)) % LANE, 1)
            fill = 1.0 if f == GROUND else 0.0
            e[f][k, tile(t), cols : cols + LANE] = jnp.where(keep, got, fill)


def kept_columns(places):
    _, _, py = position()
    lane = lanes((SUB, LANE))
    return ((lane < 2) & (py < places - 1)) | ((lane >= LANE - 2) & (py > 0))


def column_kernel(depth, rows, cols, places, *refs):
    from_left, from_right = refs[5:7]
    e = refs[7:12]
    msg_down, msg_up, both = refs[12:15]
    used = from_left.shape[0]
    both[...] = jnp.zeros_like(both)
    both[0:used] = from_left[...] + from_right[...]
    both[...] = both[...].T
    keep = kept_columns(places)
    unpack_columns(depth, cols, keep, 0, both, e)
    unpack_columns(depth, cols, keep, rows // SUB - 1, both, e)
    wide = cols + LANE
    sub = sublanes((SUB, wide))
    end = rows - SUB
    down = up = None
    for f in range(FIELDS):
        for k in range(depth):
            q = f * depth + k
            i = q % 4
            tail = e[f][k, end:rows, :]
            head = e[f][k, 0:SUB, :]
            if f == GROUND:
                across = pltpu.roll(e[ROW][k, end:rows, :], 1, 0)
                tail = tail + jnp.where(sub == SUB - 2, across, 0.0)
            tail = pltpu.roll(tail, (2 * i + 2) % SUB, 0)
            head = pltpu.roll(head, (2 * i) % SUB, 0)
            if i == 0:
                down, up = tail, head
            else:
                down = jnp.where(sub // 2 == i, tail, down)
                up = jnp.where(sub // 2 == i, head, up)
            if i == 3:
                msg_down[(q // 4) * SUB : (q // 4 + 1) * SUB, :] = down
                msg_up[(q // 4) * SUB : (q // 4 + 1) * SUB, :] = up


def eliminate(depth, rows, cols, places, t, e, fwd, gain, inv, out):
    core, px, py = position()
    upper = core == 1
    count = rows // SUB + 1
    sub = sublanes((SUB, cols + LANE))
    before = jnp.where(t == 0, count - 1, t - 1)
    g = f = v = None
    for k in range(depth):
        row = e[ROW][k, tile(t), :]
        col = e[COL][k, tile(t), :]
        row_upper = pltpu.roll(jnp.where(sub == SUB - 1, e[ROW][k, tile(before), :], row), 1, 0)
        pivot = e[GROUND][k, tile(t), :] + row + row_upper + col + pltpu.roll(col, 1, 1)
        value = e[RIGHT][k, tile(t), :]
        if k:
            pivot = pivot + v * (1.0 - g)
            value = value + v * f
        v = e[VIA][k, tile(t), :]
        inverse = 1.0 / (pivot + v)
        g = v * inverse
        if k < depth - 1:
            f = value * inverse
            fwd[k, tile(t), :] = f
            gain[k, tile(t), :] = g
            inv[k, tile(t), :] = inverse
        else:
            inverse = jnp.where(upper, 0.0, inverse)
            fwd[k, tile(t), :] = value * inverse
            inv[k, tile(t), :] = inverse
            out[1, tile(t), :] = jnp.where(upper, pivot, v * (1.0 - g))
            g = jnp.where(upper, 1.0, g)
            gain[k, tile(t), :] = g
            out[0, tile(t), :] = g * value
    edge = (lanes((SUB, LANE)) == LANE - 1) & (py == places[1] - 1)
    for k in range(depth):
        part = e[COL][k, tile(t), cols - LANE : cols]
        e[COL][k, tile(t), cols - LANE : cols] = jnp.where(edge, 0.0, part)


def close_rows(depth, rows, places, e):
    _, px, _ = position()
    end = slice(rows - SUB, rows)
    for k in range(depth):
        row = e[ROW][k, end, :]
        edge = (sublanes(row.shape) == SUB - 1) & (px == places[0] - 1)
        e[ROW][k, end, :] = jnp.where(edge, 0.0, row)


def inner_kernel(depth, rows, cols, places, *refs):
    both, e, (fwd, gain, inv, out) = refs[5], refs[6:11], refs[11:15]
    keep = kept_columns(places[1])
    last = rows // SUB - 1

    def step(t, _):
        @pl.when(t < last)
        def _():
            unpack_columns(depth, cols, keep, t, both, e)

        eliminate(depth, rows, cols, places, t, e, fwd, gain, inv, out)
        return 0

    lax.fori_loop(1, last + 1, step, 0)


def outer_kernel(depth, rows, cols, places, *refs):
    from_above, from_below = refs[9:11]
    e, (fwd, gain, inv, out) = refs[11:16], refs[16:20]
    _, px, _ = position()
    sub = sublanes((SUB, cols + LANE))
    top = (sub >= SUB - 2) & (px > 0)
    low = (sub < 2) & (px < places[0] - 1)
    for f in range(FIELDS):
        for k in range(depth):
            q = f * depth + k
            i = q % 4
            m = (q // 4) * SUB
            above = pltpu.roll(from_above[m : m + SUB, :], (SUB - 2 - 2 * i) % SUB, 0)
            under = pltpu.roll(from_below[m : m + SUB, :], (SUB - 2 * i) % SUB, 0)
            fill = 1.0 if f == GROUND else 0.0
            e[f][k, rows : rows + SUB, :] = jnp.where(top, above, jnp.where(low, under, fill))

    def step(i, _):
        t = jnp.where(i == 0, 0, rows // SUB)
        eliminate(depth, rows, cols, places, t, e, fwd, gain, inv, out)
        return 0

    lax.fori_loop(0, 2, step, 0)
    close_rows(depth, rows, places, e)


def back(depth, t, fwd, gain, middle, out):
    value = middle
    for k in range(depth - 1, -1, -1):
        value = fwd[k, tile(t), :] + gain[k, tile(t), :] * value
        out[k, tile(t), :] = value


def neighbours(k, t, count, sub, field, row, col):
    nxt = jnp.where(t == count - 1, 0, t + 1)
    pre = jnp.where(t == 0, count - 1, t - 1)
    r = row[k, tile(t), :]
    c = col[k, tile(t), :]
    z = field[k, tile(t), :]
    down = pltpu.roll(jnp.where(sub == 0, field[k, tile(nxt), :], z), SUB - 1, 0)
    flow = row[k, tile(pre), :] * field[k, tile(pre), :]
    up = pltpu.roll(jnp.where(sub == SUB - 1, flow, r * z), 1, 0)
    total = r * down + up + c * pltpu.roll(z, z.shape[1] - 1, 1) + pltpu.roll(c * z, 1, 1)
    return (total, z)


def image_kernel(depth, rows, cols, *refs):
    (right, row, col, via, fwd, gain, inv, mine, theirs, z, w, fwd2, out, inv4) = refs
    count = rows // SUB + 1
    sub = sublanes((SUB, cols + LANE))

    def solve(t):
        ratio = 1.0 / (mine[1, tile(t), :] + theirs[1, tile(t), :])
        inv4[tile(t), :] = ratio
        back(depth, t, fwd, gain, (mine[0, tile(t), :] + theirs[0, tile(t), :]) * ratio, z)

    solve(count - 1)
    solve(0)

    def step(t, _):
        solve(jnp.minimum(t + 1, count - 1))
        f = None
        for k in range(depth):
            total, _ = neighbours(k, t, count, sub, z, row, col)
            value = right[k, tile(t), :] - total
            w[k, tile(t), :] = value
            if k:
                value = value + via[k - 1, tile(t), :] * f
            f = value * inv[k, tile(t), :]
            fwd2[k, tile(t), :] = f
            if k == depth - 1:
                out[tile(t), :] = gain[k, tile(t), :] * value
        return 0

    lax.fori_loop(0, count, step, 0)


def gathered(sums, parts):
    lane = lanes(sums.shape)
    result = jnp.zeros(sums.shape, jnp.float32)
    for i, part in enumerate(parts):
        total = jnp.sum(jnp.sum(part, axis=0, keepdims=True), axis=1, keepdims=True)
        result = jnp.where(lane == i, total, result)
    return result


def early_kernel(depth, rows, cols, *refs):
    (right, z, w, acc) = refs

    def step(t, carry):
        rho, c = carry
        for k in range(depth):
            zz = z[k, tile(t), 0:cols]
            rho = rho + right[k, tile(t), 0:cols] * zz
            c = c + zz * w[k, tile(t), 0:cols]
        return (rho, c)

    zero = jnp.zeros((SUB, cols), jnp.float32)
    acc[0], acc[1] = lax.fori_loop(0, rows // SUB, step, (zero, zero))


def dots_kernel(depth, rows, cols, *refs):
    (row, col, fwd2, gain, mine, theirs, inv4, w, early, y, v, sums) = refs
    count = rows // SUB + 1
    sub = sublanes((SUB, cols + LANE))

    def solve(t):
        back(depth, t, fwd2, gain, (mine[tile(t), :] + theirs[tile(t), :]) * inv4[tile(t), :], y)

    solve(count - 1)
    solve(0)

    def step(t, carry):
        e, g = carry
        solve(t + 1)
        for k in range(depth):
            total, yy = neighbours(k, t, count, sub, y, row, col)
            ww = w[k, tile(t), 0:cols]
            yy = yy[:, 0:cols]
            vv = ww - total[:, 0:cols]
            v[k, tile(t), :] = vv
            e = e + ww * yy
            g = g + yy * vv
        return (e, g)

    zero = jnp.zeros((SUB, cols), jnp.float32)
    e, g = lax.fori_loop(0, count - 1, step, (zero, zero))
    sums[...] = gathered(sums, (early[0], early[1], e, g))


def final_kernel(depth, rows, cols, *refs):
    (sums, right, z, w, y, v, x_out, r_out, x, r, sem) = refs
    core, _, _ = position()
    total = jnp.sum(sums[...], axis=0, keepdims=True)
    lane = lanes(total.shape)
    rho, c, e, g = (
        jnp.sum(jnp.where(lane == i, total, 0.0), axis=1, keepdims=True) for i in range(4)
    )
    alpha = rho / c
    rho1 = alpha * (alpha * e - c)
    beta = rho1 / rho
    curvature = c - 2.0 * alpha * e + alpha * alpha * g
    alpha1 = rho1 / (curvature - beta * rho1 / alpha)
    near = jnp.broadcast_to(alpha + alpha1 * (1.0 + beta), (SUB, cols))
    far = jnp.broadcast_to(alpha1 * alpha, (SUB, cols))
    copies = []
    for k in range(depth):

        def step(t, _, k=k):
            x[k, tile(t), :] = near * z[k, tile(t), 0:cols] - far * y[k, tile(t), 0:cols]
            r[k, tile(t), :] = (
                right[k, tile(t), 0:cols] - near * w[k, tile(t), 0:cols] + far * v[k, tile(t), :]
            )
            return 0

        lax.fori_loop(0, rows // SUB, step, 0)
        at = layer_of(core, k, depth)
        for index, (value, target) in enumerate(((x, x_out), (r, r_out))):
            copy = pltpu.make_async_copy(value.at[k], target.at[at], sem.at[index, k])
            copy.start()
            copies.append(copy)
    for copy in copies:
        copy.wait()


def shift(value, axis, by):
    count = lax.axis_size(axis)
    return lax.ppermute(value, axis, [(i, (i + by) % count) for i in range(count)])


def shards(right_side, row_conduct, column_conduct, via_conduct, via_mask, ground_conduct):
    depth, rows, cols = right_side.shape
    places = (lax.axis_size(PX), lax.axis_size("py"))
    devices = lax.axis_size(ALL)
    tall, wide = rows + SUB, cols + LANE
    ext = (depth, tall, wide)
    vmem, hbm = pltpu.VMEM, pltpu.HBM
    size = depth * tall * wide
    part = functools.partial

    inputs = [right_side, row_conduct, column_conduct, via_conduct, ground_conduct, via_mask]
    strips = (FIELDS * depth * 4, LANE)
    *e, msg_right, msg_left = call(
        part(load_kernel, depth, rows, cols),
        inputs,
        [hbm] * 6,
        [ext] * FIELDS + [strips] * 2,
        [
            pltpu.VMEM((depth, rows, 2 * LANE), jnp.int32),
            pltpu.VMEM((2, rows, LANE), jnp.float32),
            pltpu.SemaphoreType.DMA((2, 6, depth)),
        ],
        flops=size,
        moved=6 * size,
    )
    from_left = shift(msg_right, "py", 1)
    from_right = shift(msg_left, "py", -1)
    e = call(
        part(middle_kernel, depth, rows, cols),
        [*inputs, *e],
        [hbm] * 6 + [vmem] * FIELDS,
        [ext] * FIELDS,
        [
            pltpu.VMEM((depth, rows, cols - 2 * LANE), jnp.int32),
            pltpu.SemaphoreType.DMA((1, 6, depth)),
        ],
        alias={6 + i: i for i in range(FIELDS)},
        flops=10 * size,
        moved=18 * size,
    )
    strips = (FIELDS * depth * 2, wide)
    *e, msg_down, msg_up, both = call(
        part(column_kernel, depth, rows, cols, places[1]),
        [*e, from_left, from_right],
        [vmem] * 7,
        [ext] * FIELDS + [strips] * 2 + [(rows, LANE)],
        alias={i: i for i in range(FIELDS)},
        flops=size,
    )
    from_above = shift(msg_down, PX, 1)
    from_below = shift(msg_up, PX, -1)
    state = call(
        part(inner_kernel, depth, rows, cols, places),
        [*e, both],
        [vmem] * 6,
        [ext] * FIELDS + [ext] * 3 + [(2, tall, wide)],
        alias={i: i for i in range(FIELDS)},
        flops=30 * size,
    )
    *e, fwd, gain, inv, mine = call(
        part(outer_kernel, depth, rows, cols, places),
        [*state, from_above, from_below],
        [vmem] * 11,
        [ext] * FIELDS + [ext] * 3 + [(2, tall, wide)],
        alias={i: i for i in range(FIELDS + 4)},
        flops=3 * size,
    )
    right, row, col, via, _ = e
    theirs = shift(mine, "layer", 1)
    z, w, fwd2, mine2, inv4 = call(
        part(image_kernel, depth, rows, cols),
        [right, row, col, via, fwd, gain, inv, mine, theirs],
        [vmem] * 9,
        [ext] * 3 + [(tall, wide)] * 2,
        flops=30 * size,
    )
    theirs2 = shift(mine2, "layer", 1)
    (early,) = call(
        part(early_kernel, depth, rows, cols),
        [right, z, w],
        [vmem] * 3,
        [(2, SUB, cols)],
        flops=4 * size,
    )
    y, v, sums = call(
        part(dots_kernel, depth, rows, cols),
        [row, col, fwd2, gain, mine2, theirs2, inv4, w, early],
        [vmem] * 9,
        [ext, (depth, rows, cols), (devices, LANE)],
        flops=30 * size,
    )
    sums = lax.all_to_all(sums.reshape(devices, 1, LANE), ALL, 0, 0).reshape(devices, LANE)
    block = jax.ShapeDtypeStruct((depth, rows, cols), jnp.float32)
    return call(
        part(final_kernel, depth, rows, cols),
        [sums, right, z, w, y, v],
        [vmem] * 6,
        [block] * 2,
        [
            pltpu.VMEM((depth, rows, cols), jnp.float32),
            pltpu.VMEM((depth, rows, cols), jnp.float32),
            pltpu.SemaphoreType.DMA((2, depth)),
        ],
        flops=10 * size,
    )


def solution(mesh):
    count = mesh.shape["px"]
    inner = 4 if count % 4 == 0 else 1
    split = Mesh(
        mesh.devices.reshape(mesh.shape["layer"], count // inner, inner, mesh.shape["py"]),
        ALL,
    )
    spec = P("layer", PX, "py")
    return jax.shard_map(
        lambda *a: tuple(shards(*a)),
        mesh=split,
        in_specs=(spec,) * 6,
        out_specs=(spec, spec),
        check_vma=False,
    )
```

time: 74.1 us -> 56.9 us (0.77)
  local copies, waits for them, and re-layouts: 9.54 us -> 0 us
  waiting for transfers between devices: 8.44 us -> 4.26 us
  blocking collectives: 18.3 us -> 17 us
  starting transfers between devices: 13.3 us -> 12 us
    unnamed x12 -> x0, local copies, waits for them, and re-layouts: 9.54 us -> none
    ppermute x6, waiting for transfers between devices: 8.44 us -> 4.26 us  [shift(): lax.ppermute(value, axis, [(i, (i + by) % count) for i in range(count)])]
    all_to_all x1, blocking collectives: 18.3 us -> 17 us  [shards(): lax.all_to_all(sums.reshape(devices, 1, LANE), ALL, 0, 0)]
    ppermute x6, starting transfers between devices: 13.3 us -> 12 us  [shift(): lax.ppermute(value, axis, [(i, (i + by) % count) for i in range(count)])]
    pallas_call x6 -> x9, Pallas kernels: 23.5 us -> 22.8 us  [call(): pl.pallas_call(body, out_shape=shapes, in_specs=[spec_of(k) for k in kind...]
  transfers between devices with their start and end apart: 6 -> 6, of which waited for: 4 -> 3; matrix products, arithmetic and copies ran while one was open for 0% -> 0% of each run, Pallas kernels for 0% -> 14%
where the time goes in v2:
time: 56.9 us; the launch traced here: 56.7 us
  Pallas kernels  22.8 us (40%)
  blocking collectives  17 us (30%)
  starting transfers between devices  12 us (21%)
  waiting for transfers between devices  4.26 us (7%)
  between operations  0.7 us (1%)
    pallas_call x9, Pallas kernels, call(): pl.pallas_call(body, out_shape=shapes, in_specs=[spec_of(k) for k in kind...  22.8 us
    all_to_all x1, blocking collectives, shards(): lax.all_to_all(sums.reshape(devices, 1, LANE), ALL, 0, 0)  17 us
    ppermute x6, starting transfers between devices, shift(): lax.ppermute(value, axis, [(i, (i + by) % count) for i in range(count)])  12 us
    ppermute x6, waiting for transfers between devices, shift(): lax.ppermute(value, axis, [(i, (i + by) % count) for i in range(count)])  4.26 us
  transfers between devices with their start and end apart: 6, of which 3 were waited for; matrix products, arithmetic and copies ran while one was open for 0% of the time, Pallas kernels for 14%

profile of v2, /device:TPU:1, one launch (start us, length us, event | category | flops | bytes accessed | tf_op | source)
XLA Modules:
  0.0 56.7 jit_solution(10153354474569793843)
XLA Ops:
  0.6 4.8 %shard_map.77 = (f32[4,136,1152]{2,1,0:T(8,128)S(1)}, f32[4,136,1152]{2,1,0:T(8,128)S(1)}, f32[4,136,1152]{2,1,0:T(8,128)S(1)}, f32[4,136,1152]{2,1,0:T(8,128)S(...) custom-call(f32[4,128,1024]{2,1,0:T(8,128)} %refs_0_.3, f32[4,128,1024]{2,1,0:T(8,128)} %refs_1_.3, ...), custom_call_target="tpu_custom_call" | custom-call | flops 626688 | bytes 3760128 | tf_op jit(solution)/shard_map/pallas_call | solution.py:46
  5.5 2.2 %collective-permute-start = (f32[80,128]{1,0:T(8,128)S(1)}, f32[80,128]{1,0:T(8,128)S(1)}, u32[]{:S(2)}, u32[]{:S(2)}) collective-permute-start(f32[80,128]{1,0:T(8,128)S(1)} %get-tuple-element.57), channel_id=1, source_target_pairs={{0,1},{1,2},{2,3},{3,0},{4,5},{5,6},{6,7},{7,4},{8,9},{9,10},{10,1... | collective-permute-start | bytes 122888 | tf_op jit(solution)/shard_map/ppermute | solution.py:427
  7.7 1.5 %collective-permute-start.1 = (f32[80,128]{1,0:T(8,128)S(1)}, f32[80,128]{1,0:T(8,128)S(1)}, u32[]{:S(2)}, u32[]{:S(2)}) collective-permute-start(f32[80,128]{1,0:T(8,128)S(1)} %get-tuple-element.58), channel_id=1, source_target_pairs={{0,3},{1,0},{2,1},{3,2},{4,7},{5,4},{6,5},{7,6},{8,11},{9,8},{10,9... | collective-permute-start | bytes 122888 | tf_op jit(solution)/shard_map/ppermute | solution.py:427
  9.2 4.1 %shard_map.78 = (f32[4,136,1152]{2,1,0:T(8,128)S(1)}, f32[4,136,1152]{2,1,0:T(8,128)S(1)}, f32[4,136,1152]{2,1,0:T(8,128)S(1)}, f32[4,136,1152]{2,1,0:T(8,128)S(1)}, f32[4,136,1152]{2,1,0:T(8,128)S(1)}) custom-call(f32[4,128,1024]{2,1,0:T(8,128)} %refs_0_.3, ...), custom_call_target="tpu_custom_call", output_to_operand_aliasing={{0}: (6, {}), {1}: (7, {}), {2}: (8, {}), {3}: (9, {}), {4}... | custom-call | flops 6266880 | bytes 11280384 | tf_op jit(solution)/shard_map/pallas_call | solution.py:46
  13.3 0.0 collective-permute-done.refs_5_
  13.3 0.0 collective-permute-done.1.refs_6_
  13.3 0.2 shard_map.79
  13.6 1.7 %collective-permute-start.2 = (f32[40,1152]{1,0:T(8,128)S(1)}, f32[40,1152]{1,0:T(8,128)S(1)}, u32[]{:S(2)}, u32[]{:S(2)}) collective-permute-start(f32[40,1152]{1,0:T(8,128)S(1)} %get-tuple-element.74), channel_id=1, source_target_pairs={{0,4},{4,8},{8,12},{12,16},{16,20},{20,24},{24,28},{28,32},{32,36}... | collective-permute-start | bytes 552968 | tf_op jit(solution)/shard_map/ppermute | solution.py:427
  15.3 4.4 %collective-permute-start.3 = (f32[40,1152]{1,0:T(8,128)S(1)}, f32[40,1152]{1,0:T(8,128)S(1)}, u32[]{:S(2)}, u32[]{:S(2)}) collective-permute-start(f32[40,1152]{1,0:T(8,128)S(1)} %get-tuple-element.75), channel_id=1, source_target_pairs={{0,60},{4,0},{8,4},{12,8},{16,12},{20,16},{24,20},{28,24},{32,28},... | collective-permute-start | bytes 552968 | tf_op jit(solution)/shard_map/ppermute | solution.py:427
  19.7 3.4 %shard_map.80 = (f32[4,136,1152]{2,1,0:T(8,128)S(1)}, f32[4,136,1152]{2,1,0:T(8,128)S(1)}, f32[4,136,1152]{2,1,0:T(8,128)S(1)}, f32[4,136,1152]{2,1,0:T(8,128)S(...) custom-call(f32[4,136,1152]{2,1,0:T(8,128)S(1)} %get-tuple-element.5, ...), custom_call_target="tpu_custom_call", output_to_operand_aliasing={{0}: (0, {}), {1}: (1, {}), {2}: (2, {}), {3}: (3, {}), {4}... | custom-call | flops 18800640 | tf_op jit(solution)/shard_map/pallas_call | solution.py:46
  23.1 0.4 collective-permute-done.2.refs_9_
  23.5 0.0 collective-permute-done.3.refs_10_
  23.5 0.4 shard_map.81
  23.9 1.8 %collective-permute-start.4 = (f32[2,136,1152]{2,1,0:T(8,128)S(1)}, f32[2,136,1152]{2,1,0:T(8,128)S(1)}, u32[]{:S(2)}, u32[]{:S(2)}) collective-permute-start(f32[2,136,1152]{2,1,0:T(8,128)S(1)} %get-tuple-element.83.refs_7_), channel_id=1, source_target_pairs={{0,64},{64,0},{1,65},{65,1},{2,66},{66,2},{3,67},{67,3},{4,68},{68... | collective-permute-start | bytes 3760136 | tf_op jit(solution)/shard_map/ppermute | solution.py:427
  25.7 2.6 %collective-permute-done.4.refs_8_ = f32[2,136,1152]{2,1,0:T(8,128)S(1)} collective-permute-done((f32[2,136,1152]{2,1,0:T(8,128)S(1)}, f32[2,136,1152]{2,1,0:T(8,128)S(1)}, u32[]{:S(2)}, u32[]{:S(2)}) %collective-permute-start.4) | collective-permute-done | bytes 1253408 | tf_op jit(solution)/shard_map/ppermute | solution.py:427
  28.3 3.7 %shard_map.82 = (f32[4,136,1152]{2,1,0:T(8,128)S(1)}, f32[4,136,1152]{2,1,0:T(8,128)S(1)}, f32[4,136,1152]{2,1,0:T(8,128)S(1)}, f32[136,1152]{1,0:T(8,128)S(1)}, f32[136,1152]{1,0:T(8,128)S(1)}) custom-call(f32[4,136,1152]{2,1,0:T(8,128)S(1)} %get-tuple-element.78.refs_0_.refs_1_, f32[4,136,1152]{2,1,0:T(8,128)S(1)} %get-tuple-element.76.refs_1_.refs_0_, ...), custom_call_target="tpu_custom_call" | custom-call | flops 18800640 | tf_op jit(solution)/shard_map/pallas_call | solution.py:46
  32.0 0.5 collective-permute-start.5
  32.4 0.4 shard_map.83.refs_8_
  32.8 1.3 %collective-permute-done.5.refs_5_ = f32[136,1152]{1,0:T(8,128)S(1)} collective-permute-done((f32[136,1152]{1,0:T(8,128)S(1)}, f32[136,1152]{1,0:T(8,128)S(1)}, u32[]{:S(2)}, u32[]{:S(2)}) %collective-permute-start.5) | collective-permute-done | bytes 626720 | tf_op jit(solution)/shard_map/ppermute | solution.py:427
  34.1 3.3 %shard_map.84 = (f32[4,136,1152]{2,1,0:T(8,128)S(1)}, f32[4,128,1024]{2,1,0:T(8,128)S(1)}, f32[128,128]{1,0:T(8,128)S(1)}) custom-call(f32[4,136,1152]{2,1,0:T(8,128)S(1)} %get-tuple-element.76.refs_1_.refs_0_, f32[4,136,1152]{2,1,0:T(8,128)S(1)} %get-tuple-element.77.refs_2_.refs_1_, f32[4,136,1152]{2,1,0:T(8,128)S(1)} %get-tuple-element.84.refs_2_, ...), custom_call_target="tpu_custom_call" | custom-call | flops 18800640 | tf_op jit(solution)/shard_map/pallas_call | solution.py:46
  37.4 17.0 %all_to_all.5 = f32[128,1,128]{2,1,0:T(1,128)S(1)} all-to-all(f32[128,1,128]{2,1,0:T(1,128)S(1)} %bitcast.5), channel_id=1, replica_groups=mesh['layer'=2,'px_0'=4,'px_1'=4,'py'=4] {'layer','px_0','px_1','py'}, dimensions={0} | all-to-all | bytes 131072 | tf_op jit(solution)/shard_map/all_to_all | solution.py:521
  54.3 2.4 %shard_map.85 = (f32[4,128,1024]{2,1,0:T(8,128)}, f32[4,128,1024]{2,1,0:T(8,128)}) custom-call(f32[128,128]{1,0:T(8,128)S(1)} %bitcast.4, f32[4,136,1152]{2,1,0:T(8,128)S(1)} %get-tuple-element.78.refs_0_.refs_1_, f32[4,136,1152]{2,1,0:T(8,128)S(1)} %get-tuple-element.88.refs_1_.refs_2_, f32[4,136,1152]{2,1,0:T(8,128)S(1)} %get-tuple-element.87.refs_2_.refs_7_.refs_3_, ...), custom_call_target="tpu_custom_call" | custom-call | flops 6266880 | tf_op jit(solution)/shard_map/pallas_call | solution.py:46
Async XLA Ops:
  5.5 7.8 %collective-permute-start = (f32[80,128]{1,0:T(8,128)S(1)}, f32[80,128]{1,0:T(8,128)S(1)}, u32[]{:S(2)}, u32[]{:S(2)}) collective-permute-start(f32[80,128]{1,0:T(8,128)S(1)} %get-tuple-element.57), channel_id=1, source_target_pairs={{0,1},{1,2},{2,3},{3,0},{4,5},{5,6},{6,7},{7,4},{8,9},{9,10},{10,1... | collective-permute-start | bytes 122888 | tf_op jit(solution)/shard_map/ppermute | solution.py:427
  7.7 5.7 %collective-permute-start.1 = (f32[80,128]{1,0:T(8,128)S(1)}, f32[80,128]{1,0:T(8,128)S(1)}, u32[]{:S(2)}, u32[]{:S(2)}) collective-permute-start(f32[80,128]{1,0:T(8,128)S(1)} %get-tuple-element.58), channel_id=1, source_target_pairs={{0,3},{1,0},{2,1},{3,2},{4,7},{5,4},{6,5},{7,6},{8,11},{9,8},{10,9... | collective-permute-start | bytes 122888 | tf_op jit(solution)/shard_map/ppermute | solution.py:427
  13.6 9.9 %collective-permute-start.2 = (f32[40,1152]{1,0:T(8,128)S(1)}, f32[40,1152]{1,0:T(8,128)S(1)}, u32[]{:S(2)}, u32[]{:S(2)}) collective-permute-start(f32[40,1152]{1,0:T(8,128)S(1)} %get-tuple-element.74), channel_id=1, source_target_pairs={{0,4},{4,8},{8,12},{12,16},{16,20},{20,24},{24,28},{28,32},{32,36}... | collective-permute-start | bytes 552968 | tf_op jit(solution)/shard_map/ppermute | solution.py:427
  15.3 8.2 %collective-permute-start.3 = (f32[40,1152]{1,0:T(8,128)S(1)}, f32[40,1152]{1,0:T(8,128)S(1)}, u32[]{:S(2)}, u32[]{:S(2)}) collective-permute-start(f32[40,1152]{1,0:T(8,128)S(1)} %get-tuple-element.75), channel_id=1, source_target_pairs={{0,60},{4,0},{8,4},{12,8},{16,12},{20,16},{24,20},{28,24},{32,28},... | collective-permute-start | bytes 552968 | tf_op jit(solution)/shard_map/ppermute | solution.py:427
  23.9 4.3 %collective-permute-start.4 = (f32[2,136,1152]{2,1,0:T(8,128)S(1)}, f32[2,136,1152]{2,1,0:T(8,128)S(1)}, u32[]{:S(2)}, u32[]{:S(2)}) collective-permute-start(f32[2,136,1152]{2,1,0:T(8,128)S(1)} %get-tuple-element.83.refs_7_), channel_id=1, source_target_pairs={{0,64},{64,0},{1,65},{65,1},{2,66},{66,2},{3,67},{67,3},{4,68},{68... | collective-permute-start | bytes 3760136 | tf_op jit(solution)/shard_map/ppermute | solution.py:427
  32.0 2.1 %collective-permute-start.5 = (f32[136,1152]{1,0:T(8,128)S(1)}, f32[136,1152]{1,0:T(8,128)S(1)}, u32[]{:S(2)}, u32[]{:S(2)}) collective-permute-start(f32[136,1152]{1,0:T(8,128)S(1)} %get-tuple-element.85.refs_4_), channel_id=1, source_target_pairs={{0,64},{64,0},{1,65},{65,1},{2,66},{66,2},{3,67},{67,3},{4,68},{68... | collective-permute-start | bytes 1880072 | tf_op jit(solution)/shard_map/ppermute | solution.py:427

commit v3 on v2

--- a/solution.py
+++ b/solution.py
@@ -8,9 +8,12 @@
 from jax.sharding import Mesh
 from jax.sharding import PartitionSpec as P
 
+
 RIGHT, ROW, COL, VIA, GROUND = range(5)
 FIELDS = 5
+EARLY = (RIGHT, ROW, COL)
 SUB, LANE = 8, 128
+INNER, IMAGE, DOTS, FINAL = 3, 2, 2, 4
 PX = ("px_0", "px_1")
 ALL = ("layer", "px_0", "px_1", "py")
 
@@ -24,12 +27,28 @@
 
 
 def tile(index):
+    if isinstance(index, int):
+        return slice(index * SUB, (index + 1) * SUB)
     return pl.ds(pl.multiple_of(index * SUB, SUB), SUB)
 
 
 def position():
     px = lax.axis_index("px_0") * lax.axis_size("px_1") + lax.axis_index("px_1")
     return (lax.axis_index("layer"), px, lax.axis_index("py"))
+
+
+def sweep(low, high, several, body, carry=()):
+    steps = (high - low) // several
+
+    def step(i, carry):
+        for j in range(several):
+            carry = body(low + i * several + j, carry)
+        return carry
+
+    carry = lax.fori_loop(0, steps, step, carry)
+    for t in range(low + steps * several, high):
+        carry = body(t, carry)
+    return carry
 
 
 def spec_of(kind):
@@ -64,28 +83,25 @@
     return jnp.where(core == 0, k, upper)
 
 
-def copies_in(core, depth, rows, sources, targets, masks, sem, spans):
+def start_copies(core, depth, rows, sources, targets, masks, sem, slot, low, high, start, fields):
     copies = []
-    for s, (low, high) in enumerate(spans):
-        for k in range(depth):
-            at, link = layer_of(core, k, depth), link_of(core, k, depth)
-            for f, source in enumerate(sources):
-                layer = link if f in (VIA, FIELDS) else at
-                into = (
-                    masks.at[k, :, s * (high - low) : (s + 1) * (high - low)]
-                    if f == FIELDS
-                    else targets[f].at[k, 0:rows, low:high]
-                )
-                copy = pltpu.make_async_copy(
-                    source.at[layer, :, low:high], into, sem.at[s, f, k]
-                )
-                copy.start()
-                copies.append(copy)
+    for k in range(depth):
+        at, link = layer_of(core, k, depth), link_of(core, k, depth)
+        for f in fields:
+            into = (
+                masks.at[k, :, start : start + high - low]
+                if f == FIELDS
+                else targets[f].at[k, 0:rows, low:high]
+            )
+            source = sources[f].at[link if f in (VIA, FIELDS) else at, :, low:high]
+            copy = pltpu.make_async_copy(source, into, sem.at[slot, f, k])
+            copy.start()
+            copies.append(copy)
     return copies
 
 
-def masked(core, depth, t, via, masks, low, high, start):
-    for k in range(depth):
+def masked(core, depth, layers, t, via, masks, low, high, start):
+    for k in layers:
         value = via[k, tile(t), low:high] * masks[k, tile(t), start : start + high - low].astype(
             jnp.float32
         )
@@ -99,13 +115,17 @@
     msg_right, msg_left, masks, pack, sem = refs[11:]
     core, _, _ = position()
     last = cols - LANE
-    for copy in copies_in(core, depth, rows, sources, e, masks, sem, ((0, LANE), (last, cols))):
+    every = range(FIELDS + 1)
+    begin = functools.partial(start_copies, core, depth, rows, sources, e, masks, sem)
+    edges = begin(0, 0, LANE, 0, every) + begin(1, last, cols, LANE, every)
+    others = begin(2, LANE, last, 0, EARLY)
+    for copy in edges:
         copy.wait()
     lane = lanes((SUB, LANE))
 
-    def step(t, _):
-        masked(core, depth, t, e[VIA], masks, 0, LANE, 0)
-        masked(core, depth, t, e[VIA], masks, last, cols, LANE)
+    def body(t, carry):
+        masked(core, depth, range(depth), t, e[VIA], masks, 0, LANE, 0)
+        masked(core, depth, range(depth), t, e[VIA], masks, last, cols, LANE)
         to_right = jnp.zeros((SUB, LANE), jnp.float32)
         to_left = jnp.zeros((SUB, LANE), jnp.float32)
         for f in range(FIELDS):
@@ -121,26 +141,34 @@
                 to_left = jnp.where((lane // 2) == 2 * q + 1, pltpu.roll(head, shift, 1), to_left)
         pack[0, tile(t), :] = to_right
         pack[1, tile(t), :] = to_left
-        return 0
-
-    lax.fori_loop(0, rows // SUB, step, 0)
+        return carry
+
+    sweep(0, rows // SUB, 4, body)
     used = msg_right.shape[0]
     msg_right[...] = pack[0].T[0:used]
     msg_left[...] = pack[1].T[0:used]
+    for copy in others:
+        copy.wait()
 
 
 def middle_kernel(depth, rows, cols, *refs):
     sources, e, masks, sem = refs[0:6], refs[11:16], refs[16], refs[17]
     core, _, _ = position()
     low, high = LANE, cols - LANE
-    for copy in copies_in(core, depth, rows, sources, e, masks, sem, ((low, high),)):
+    begin = functools.partial(start_copies, core, depth, rows, sources, e, masks, sem, 0, low, high, 0)
+    vias = begin((VIA, FIELDS))
+    others = begin([f for f in range(FIELDS) if f not in EARLY and f != VIA])
+    for k in range(depth):
+        for copy in vias[2 * k : 2 * k + 2]:
+            copy.wait()
+
+        def body(t, carry, k=k):
+            masked(core, depth, (k,), t, e[VIA], masks, low, high, 0)
+            return carry
+
+        sweep(0, rows // SUB, 4, body)
+    for copy in others:
         copy.wait()
-
-    def step(t, _):
-        masked(core, depth, t, e[VIA], masks, low, high, 0)
-        return 0
-
-    lax.fori_loop(0, rows // SUB, step, 0)
 
 
 def unpack_columns(depth, cols, keep, t, both, e):
@@ -194,8 +222,8 @@
                 msg_up[(q // 4) * SUB : (q // 4 + 1) * SUB, :] = up
 
 
-def eliminate(depth, rows, cols, places, t, e, fwd, gain, inv, out):
-    core, px, py = position()
+def eliminate(depth, rows, cols, places, t, e, fwd, gain, inv, out, slot):
+    core, _, py = position()
     upper = core == 1
     count = rows // SUB + 1
     sub = sublanes((SUB, cols + LANE))
@@ -222,10 +250,10 @@
             inverse = jnp.where(upper, 0.0, inverse)
             fwd[k, tile(t), :] = value * inverse
             inv[k, tile(t), :] = inverse
-            out[1, tile(t), :] = jnp.where(upper, pivot, v * (1.0 - g))
+            out[1, tile(slot), :] = jnp.where(upper, pivot, v * (1.0 - g))
             g = jnp.where(upper, 1.0, g)
             gain[k, tile(t), :] = g
-            out[0, tile(t), :] = g * value
+            out[0, tile(slot), :] = g * value
     edge = (lanes((SUB, LANE)) == LANE - 1) & (py == places[1] - 1)
     for k in range(depth):
         part = e[COL][k, tile(t), cols - LANE : cols]
@@ -246,20 +274,21 @@
     keep = kept_columns(places[1])
     last = rows // SUB - 1
 
-    def step(t, _):
-        @pl.when(t < last)
-        def _():
-            unpack_columns(depth, cols, keep, t, both, e)
-
-        eliminate(depth, rows, cols, places, t, e, fwd, gain, inv, out)
-        return 0
-
-    lax.fori_loop(1, last + 1, step, 0)
+    def unpack(t, carry):
+        unpack_columns(depth, cols, keep, t, both, e)
+        return carry
+
+    def body(t, carry):
+        eliminate(depth, rows, cols, places, t, e, fwd, gain, inv, out, t - 1)
+        return carry
+
+    sweep(1, last, 2, unpack)
+    sweep(1, last + 1, INNER, body)
 
 
 def outer_kernel(depth, rows, cols, places, *refs):
-    from_above, from_below = refs[9:11]
-    e, (fwd, gain, inv, out) = refs[11:16], refs[16:20]
+    from_above, from_below = refs[8:10]
+    e, (fwd, gain, inv, out) = refs[10:15], refs[15:19]
     _, px, _ = position()
     sub = sublanes((SUB, cols + LANE))
     top = (sub >= SUB - 2) & (px > 0)
@@ -274,12 +303,8 @@
             fill = 1.0 if f == GROUND else 0.0
             e[f][k, rows : rows + SUB, :] = jnp.where(top, above, jnp.where(low, under, fill))
 
-    def step(i, _):
-        t = jnp.where(i == 0, 0, rows // SUB)
-        eliminate(depth, rows, cols, places, t, e, fwd, gain, inv, out)
-        return 0
-
-    lax.fori_loop(0, 2, step, 0)
+    eliminate(depth, rows, cols, places, 0, e, fwd, gain, inv, out, 0)
+    eliminate(depth, rows, cols, places, rows // SUB, e, fwd, gain, inv, out, 1)
     close_rows(depth, rows, places, e)
 
 
@@ -303,21 +328,30 @@
     return (total, z)
 
 
+def join(depth, t, slot, fwd, gain, mine, theirs, inv4, z):
+    ratio = 1.0 / (mine[1, tile(slot), :] + theirs[1, tile(slot), :])
+    inv4[tile(t), :] = ratio
+    back(depth, t, fwd, gain, (mine[0, tile(slot), :] + theirs[0, tile(slot), :]) * ratio, z)
+
+
+def inner_solve_kernel(depth, rows, *refs):
+    (fwd, gain, mine, theirs, z, inv4) = refs
+
+    def body(t, carry):
+        join(depth, t, t - 1, fwd, gain, mine, theirs, inv4, z)
+        return carry
+
+    sweep(1, rows // SUB, 3, body)
+
+
 def image_kernel(depth, rows, cols, *refs):
-    (right, row, col, via, fwd, gain, inv, mine, theirs, z, w, fwd2, out, inv4) = refs
+    (right, row, col, via, fwd, gain, inv, mine, theirs, _, _, z, inv4, w, fwd2, out) = refs
     count = rows // SUB + 1
     sub = sublanes((SUB, cols + LANE))
-
-    def solve(t):
-        ratio = 1.0 / (mine[1, tile(t), :] + theirs[1, tile(t), :])
-        inv4[tile(t), :] = ratio
-        back(depth, t, fwd, gain, (mine[0, tile(t), :] + theirs[0, tile(t), :]) * ratio, z)
-
-    solve(count - 1)
-    solve(0)
-
-    def step(t, _):
-        solve(jnp.minimum(t + 1, count - 1))
+    join(depth, 0, 0, fwd, gain, mine, theirs, inv4, z)
+    join(depth, count - 1, 1, fwd, gain, mine, theirs, inv4, z)
+
+    def body(t, carry):
         f = None
         for k in range(depth):
             total, _ = neighbours(k, t, count, sub, z, row, col)
@@ -329,9 +363,9 @@
             fwd2[k, tile(t), :] = f
             if k == depth - 1:
                 out[tile(t), :] = gain[k, tile(t), :] * value
-        return 0
-
-    lax.fori_loop(0, count, step, 0)
+        return carry
+
+    sweep(0, count, IMAGE, body)
 
 
 def gathered(sums, parts):
@@ -346,7 +380,7 @@
 def early_kernel(depth, rows, cols, *refs):
     (right, z, w, acc) = refs
 
-    def step(t, carry):
+    def body(t, carry):
         rho, c = carry
         for k in range(depth):
             zz = z[k, tile(t), 0:cols]
@@ -355,13 +389,14 @@
         return (rho, c)
 
     zero = jnp.zeros((SUB, cols), jnp.float32)
-    acc[0], acc[1] = lax.fori_loop(0, rows // SUB, step, (zero, zero))
+    acc[0], acc[1] = sweep(0, rows // SUB, 2, body, (zero, zero))
 
 
 def dots_kernel(depth, rows, cols, *refs):
     (row, col, fwd2, gain, mine, theirs, inv4, w, early, y, v, sums) = refs
     count = rows // SUB + 1
-    sub = sublanes((SUB, cols + LANE))
+    wide = cols + LANE
+    sub = sublanes((SUB, wide))
 
     def solve(t):
         back(depth, t, fwd2, gain, (mine[tile(t), :] + theirs[tile(t), :]) * inv4[tile(t), :], y)
@@ -369,21 +404,21 @@
     solve(count - 1)
     solve(0)
 
-    def step(t, carry):
+    def body(t, carry):
         e, g = carry
         solve(t + 1)
         for k in range(depth):
             total, yy = neighbours(k, t, count, sub, y, row, col)
-            ww = w[k, tile(t), 0:cols]
             yy = yy[:, 0:cols]
-            vv = ww - total[:, 0:cols]
-            v[k, tile(t), :] = vv
-            e = e + ww * yy
-            g = g + yy * vv
+            first = w[k, tile(t), 0:cols]
+            second = first - total[:, 0:cols]
+            v[k, tile(t), :] = second
+            e = e + first * yy
+            g = g + yy * second
         return (e, g)
 
     zero = jnp.zeros((SUB, cols), jnp.float32)
-    e, g = lax.fori_loop(0, count - 1, step, (zero, zero))
+    e, g = sweep(0, count - 1, DOTS, body, (zero, zero))
     sums[...] = gathered(sums, (early[0], early[1], e, g))
 
 
@@ -405,17 +440,17 @@
     copies = []
     for k in range(depth):
 
-        def step(t, _, k=k):
+        def body(t, carry, k=k):
             x[k, tile(t), :] = near * z[k, tile(t), 0:cols] - far * y[k, tile(t), 0:cols]
             r[k, tile(t), :] = (
                 right[k, tile(t), 0:cols] - near * w[k, tile(t), 0:cols] + far * v[k, tile(t), :]
             )
-            return 0
-
-        lax.fori_loop(0, rows // SUB, step, 0)
+            return carry
+
+        sweep(0, rows // SUB, FINAL, body)
         at = layer_of(core, k, depth)
-        for index, (value, target) in enumerate(((x, x_out), (r, r_out))):
-            copy = pltpu.make_async_copy(value.at[k], target.at[at], sem.at[index, k])
+        for slot, (value, target) in enumerate(((x, x_out), (r, r_out))):
+            copy = pltpu.make_async_copy(value.at[k], target.at[at], sem.at[slot, k])
             copy.start()
             copies.append(copy)
     for copy in copies:
@@ -447,7 +482,7 @@
         [
             pltpu.VMEM((depth, rows, 2 * LANE), jnp.int32),
             pltpu.VMEM((2, rows, LANE), jnp.float32),
-            pltpu.SemaphoreType.DMA((2, 6, depth)),
+            pltpu.SemaphoreType.DMA((3, 6, depth)),
         ],
         flops=size,
         moved=6 * size,
@@ -478,29 +513,38 @@
     )
     from_above = shift(msg_down, PX, 1)
     from_below = shift(msg_up, PX, -1)
-    state = call(
+    *state, mine = call(
         part(inner_kernel, depth, rows, cols, places),
         [*e, both],
         [vmem] * 6,
-        [ext] * FIELDS + [ext] * 3 + [(2, tall, wide)],
+        [ext] * FIELDS + [ext] * 3 + [(2, rows - SUB, wide)],
         alias={i: i for i in range(FIELDS)},
         flops=30 * size,
     )
-    *e, fwd, gain, inv, mine = call(
+    theirs = shift(mine, "layer", 1)
+    *e, fwd, gain, inv, mine_outer = call(
         part(outer_kernel, depth, rows, cols, places),
         [*state, from_above, from_below],
+        [vmem] * 10,
+        [ext] * FIELDS + [ext] * 3 + [(2, 2 * SUB, wide)],
+        alias={i: i for i in range(FIELDS + 3)},
+        flops=3 * size,
+    )
+    right, row, col, via, _ = e
+    theirs_outer = shift(mine_outer, "layer", 1)
+    z, inv4 = call(
+        part(inner_solve_kernel, depth, rows),
+        [fwd, gain, mine, theirs],
+        [vmem] * 4,
+        [ext, (tall, wide)],
+        flops=8 * size,
+    )
+    z, inv4, w, fwd2, mine2 = call(
+        part(image_kernel, depth, rows, cols),
+        [right, row, col, via, fwd, gain, inv, mine_outer, theirs_outer, z, inv4],
         [vmem] * 11,
-        [ext] * FIELDS + [ext] * 3 + [(2, tall, wide)],
-        alias={i: i for i in range(FIELDS + 4)},
-        flops=3 * size,
-    )
-    right, row, col, via, _ = e
-    theirs = shift(mine, "layer", 1)
-    z, w, fwd2, mine2, inv4 = call(
-        part(image_kernel, depth, rows, cols),
-        [right, row, col, via, fwd, gain, inv, mine, theirs],
-        [vmem] * 9,
-        [ext] * 3 + [(tall, wide)] * 2,
+        [ext, (tall, wide)] + [ext] * 2 + [(tall, wide)],
+        alias={9: 0, 10: 1},
         flops=30 * size,
     )
     theirs2 = shift(mine2, "layer", 1)
@@ -516,7 +560,7 @@
         [row, col, fwd2, gain, mine2, theirs2, inv4, w, early],
         [vmem] * 9,
         [ext, (depth, rows, cols), (devices, LANE)],
-        flops=30 * size,
+        flops=20 * size,
     )
     sums = lax.all_to_all(sums.reshape(devices, 1, LANE), ALL, 0, 0).reshape(devices, LANE)
     block = jax.ShapeDtypeStruct((depth, rows, cols), jnp.float32)
@@ -542,8 +586,12 @@
         ALL,
     )
     spec = P("layer", PX, "py")
+
+    def step(*arrays):
+        return tuple(shards(*arrays))
+
     return jax.shard_map(
-        lambda *a: tuple(shards(*a)),
+        step,
         mesh=split,
         in_specs=(spec,) * 6,
         out_specs=(spec, spec),

time: 56.9 us -> 56.7 us (level)
  Pallas kernels: 22.8 us -> 19.3 us
  waiting for transfers between devices: 4.26 us -> 6.82 us
  blocking collectives: 17 us -> 17.7 us
    pallas_call x9 -> x10, Pallas kernels: 22.8 us -> 19.3 us  [call(): pl.pallas_call(body, out_shape=shapes, in_specs=[spec_of(k) for k in kind...]
    ppermute x6 -> x7, waiting for transfers between devices: 4.26 us -> 6.82 us  [shift(): lax.ppermute(value, axis, [(i, (i + by) % count) for i in range(count)])]
    all_to_all x1, blocking collectives: 17 us -> 17.7 us  [shards(): lax.all_to_all(sums.reshape(devices, 1, LANE), ALL, 0, 0)]
    ppermute x6 -> x7, starting transfers between devices: 12 us -> 12 us  [shift(): lax.ppermute(value, axis, [(i, (i + by) % count) for i in range(count)])]
  transfers between devices with their start and end apart: 6 -> 7, of which waited for: 3 -> 3; matrix products, arithmetic and copies ran while one was open for 0% -> 0% of each run, Pallas kernels for 14% -> 6%
where the time goes in v3:
time: 56.7 us; the launch traced here: 56.5 us
  Pallas kernels  19.3 us (34%)
  blocking collectives  17.7 us (31%)
  starting transfers between devices  12 us (21%)
  waiting for transfers between devices  6.82 us (12%)
  between operations  0.7 us (1%)
    pallas_call x10, Pallas kernels, call(): pl.pallas_call(body, out_shape=shapes, in_specs=[spec_of(k) for k in kind...  19.3 us
    all_to_all x1, blocking collectives, shards(): lax.all_to_all(sums.reshape(devices, 1, LANE), ALL, 0, 0)  17.7 us
    ppermute x7, starting transfers between devices, shift(): lax.ppermute(value, axis, [(i, (i + by) % count) for i in range(count)])  12 us
    ppermute x7, waiting for transfers between devices, shift(): lax.ppermute(value, axis, [(i, (i + by) % count) for i in range(count)])  6.82 us
  transfers between devices with their start and end apart: 7, of which 3 were waited for; matrix products, arithmetic and copies ran while one was open for 0% of the time, Pallas kernels for 6%

profile of v3, /device:TPU:1, one launch (start us, length us, event | category | flops | bytes accessed | tf_op | source)
XLA Modules:
  0.0 56.5 jit_solution(12719256014934841662)
XLA Ops:
  0.6 5.1 %shard_map.77 = (f32[4,136,1152]{2,1,0:T(8,128)S(1)}, f32[4,136,1152]{2,1,0:T(8,128)S(1)}, f32[4,136,1152]{2,1,0:T(8,128)S(1)}, f32[4,136,1152]{2,1,0:T(8,128)S(...) custom-call(f32[4,128,1024]{2,1,0:T(8,128)} %refs_0_.3, f32[4,128,1024]{2,1,0:T(8,128)} %refs_1_.3, ...), custom_call_target="tpu_custom_call" | custom-call | flops 626688 | bytes 3760128 | tf_op jit(solution)/shard_map/pallas_call | solution.py:65
  5.8 2.2 %collective-permute-start = (f32[80,128]{1,0:T(8,128)S(1)}, f32[80,128]{1,0:T(8,128)S(1)}, u32[]{:S(2)}, u32[]{:S(2)}) collective-permute-start(f32[80,128]{1,0:T(8,128)S(1)} %get-tuple-element.59), channel_id=1, source_target_pairs={{0,1},{1,2},{2,3},{3,0},{4,5},{5,6},{6,7},{7,4},{8,9},{9,10},{10,1... | collective-permute-start | bytes 122888 | tf_op jit(solution)/shard_map/ppermute | solution.py:462
  8.0 1.5 %collective-permute-start.1 = (f32[80,128]{1,0:T(8,128)S(1)}, f32[80,128]{1,0:T(8,128)S(1)}, u32[]{:S(2)}, u32[]{:S(2)}) collective-permute-start(f32[80,128]{1,0:T(8,128)S(1)} %get-tuple-element.60), channel_id=1, source_target_pairs={{0,3},{1,0},{2,1},{3,2},{4,7},{5,4},{6,5},{7,6},{8,11},{9,8},{10,9... | collective-permute-start | bytes 122888 | tf_op jit(solution)/shard_map/ppermute | solution.py:462
  9.5 2.5 %shard_map.78 = (f32[4,136,1152]{2,1,0:T(8,128)S(1)}, f32[4,136,1152]{2,1,0:T(8,128)S(1)}, f32[4,136,1152]{2,1,0:T(8,128)S(1)}, f32[4,136,1152]{2,1,0:T(8,128)S(1)}, f32[4,136,1152]{2,1,0:T(8,128)S(1)}) custom-call(f32[4,128,1024]{2,1,0:T(8,128)} %refs_0_.3, ...), custom_call_target="tpu_custom_call", output_to_operand_aliasing={{0}: (6, {}), {1}: (7, {}), {2}: (8, {}), {3}: (9, {}), {4}... | custom-call | flops 6266880 | bytes 11280384 | tf_op jit(solution)/shard_map/pallas_call | solution.py:65
  12.0 0.0 collective-permute-done.refs_5_
  12.0 0.0 collective-permute-done.1.refs_6_
  12.0 0.2 shard_map.79
  12.2 2.6 %shard_map.80 = (f32[4,136,1152]{2,1,0:T(8,128)S(1)}, f32[4,136,1152]{2,1,0:T(8,128)S(1)}, f32[4,136,1152]{2,1,0:T(8,128)S(1)}, f32[4,136,1152]{2,1,0:T(8,128)S(...) custom-call(f32[4,136,1152]{2,1,0:T(8,128)S(1)} %get-tuple-element.6, ...), custom_call_target="tpu_custom_call", output_to_operand_aliasing={{0}: (0, {}), {1}: (1, {}), {2}: (2, {}), {3}: (3, {}), {4}... | custom-call | flops 18800640 | tf_op jit(solution)/shard_map/pallas_call | solution.py:65
  14.8 1.1 %collective-permute-start.5 = (f32[2,120,1152]{2,1,0:T(8,128)S(1)}, f32[2,120,1152]{2,1,0:T(8,128)S(1)}, u32[]{:S(2)}, u32[]{:S(2)}) collective-permute-start(f32[2,120,1152]{2,1,0:T(8,128)S(1)} %get-tuple-element.85.refs_2_), channel_id=1, source_target_pairs={{0,64},{64,0},{1,65},{65,1},{2,66},{66,2},{3,67},{67,3},{4,68},{68... | collective-permute-start | bytes 3317768 | tf_op jit(solution)/shard_map/ppermute | solution.py:462
  15.9 1.7 %collective-permute-start.2 = (f32[40,1152]{1,0:T(8,128)S(1)}, f32[40,1152]{1,0:T(8,128)S(1)}, u32[]{:S(2)}, u32[]{:S(2)}) collective-permute-start(f32[40,1152]{1,0:T(8,128)S(1)} %get-tuple-element.75), channel_id=1, source_target_pairs={{0,4},{4,8},{8,12},{12,16},{16,20},{20,24},{24,28},{28,32},{32,36}... | collective-permute-start | bytes 552968 | tf_op jit(solution)/shard_map/ppermute | solution.py:462
  17.6 4.3 %collective-permute-start.3 = (f32[40,1152]{1,0:T(8,128)S(1)}, f32[40,1152]{1,0:T(8,128)S(1)}, u32[]{:S(2)}, u32[]{:S(2)}) collective-permute-start(f32[40,1152]{1,0:T(8,128)S(1)} %get-tuple-element.76), channel_id=1, source_target_pairs={{0,60},{4,0},{8,4},{12,8},{16,12},{20,16},{24,20},{28,24},{32,28},... | collective-permute-start | bytes 552968 | tf_op jit(solution)/shard_map/ppermute | solution.py:462
  21.9 4.9 %collective-permute-done.2.refs_8_ = f32[40,1152]{1,0:T(8,128)S(1)} collective-permute-done((f32[40,1152]{1,0:T(8,128)S(1)}, f32[40,1152]{1,0:T(8,128)S(1)}, u32[]{:S(2)}, u32[]{:S(2)}) %collective-permute-start.2) | collective-permute-done | bytes 184352 | tf_op jit(solution)/shard_map/ppermute | solution.py:462
  26.9 0.0 collective-permute-done.3.refs_9_
  26.9 0.3 shard_map.81
  27.2 0.7 %collective-permute-start.4 = (f32[2,16,1152]{2,1,0:T(8,128)S(1)}, f32[2,16,1152]{2,1,0:T(8,128)S(1)}, u32[]{:S(2)}, u32[]{:S(2)}) collective-permute-start(f32[2,16,1152]{2,1,0:T(8,128)S(1)} %get-tuple-element.84.refs_7_), channel_id=1, source_target_pairs={{0,64},{64,0},{1,65},{65,1},{2,66},{66,2},{3,67},{67,3},{4,68},{68... | collective-permute-start | bytes 442376 | tf_op jit(solution)/shard_map/ppermute | solution.py:462
  27.9 0.0 collective-permute-done.5.refs_3_
  27.9 0.5 shard_map.82
  28.4 0.5 collective-permute-done.4.refs_8_
  28.9 2.5 %shard_map.83 = (f32[4,136,1152]{2,1,0:T(8,128)S(1)}, f32[136,1152]{1,0:T(8,128)S(1)}, f32[4,136,1152]{2,1,0:T(8,128)S(1)}, f32[4,136,1152]{2,1,0:T(8,128)S(1)}, f32[136,1152]{1,0:T(8,128)S(1)}) custom-call(f32[4,136,1152]{2,1,0:T(8,128)S(1)} %get-tuple-element.79.refs_0_.refs_1_, ...), custom_call_target="tpu_custom_call", output_to_operand_aliasing={{0}: (9, {}), {1}: (10, {})} | custom-call | flops 18800640 | tf_op jit(solution)/shard_map/pallas_call | solution.py:65
  31.4 0.4 collective-permute-start.6
  31.8 0.3 shard_map.84.refs_8_
  32.2 1.3 %collective-permute-done.6.refs_5_ = f32[136,1152]{1,0:T(8,128)S(1)} collective-permute-done((f32[136,1152]{1,0:T(8,128)S(1)}, f32[136,1152]{1,0:T(8,128)S(1)}, u32[]{:S(2)}, u32[]{:S(2)}) %collective-permute-start.6) | collective-permute-done | bytes 626720 | tf_op jit(solution)/shard_map/ppermute | solution.py:462
  33.5 2.9 %shard_map.85 = (f32[4,136,1152]{2,1,0:T(8,128)S(1)}, f32[4,128,1024]{2,1,0:T(8,128)S(1)}, f32[128,128]{1,0:T(8,128)S(1)}) custom-call(f32[4,136,1152]{2,1,0:T(8,128)S(1)} %get-tuple-element.77.refs_1_.refs_0_, f32[4,136,1152]{2,1,0:T(8,128)S(1)} %get-tuple-element.78.refs_2_.refs_1_, f32[4,136,1152]{2,1,0:T(8,128)S(1)} %get-tuple-element.88.refs_2_, ...), custom_call_target="tpu_custom_call" | custom-call | flops 12533760 | tf_op jit(solution)/shard_map/pallas_call | solution.py:65
  36.4 17.7 %all_to_all.5 = f32[128,1,128]{2,1,0:T(1,128)S(1)} all-to-all(f32[128,1,128]{2,1,0:T(1,128)S(1)} %bitcast.5), channel_id=1, replica_groups=mesh['layer'=2,'px_0'=4,'px_1'=4,'py'=4] {'layer','px_0','px_1','py'}, dimensions={0} | all-to-all | bytes 131072 | tf_op jit(solution)/shard_map/all_to_all | solution.py:565
  54.1 2.4 %shard_map.86 = (f32[4,128,1024]{2,1,0:T(8,128)}, f32[4,128,1024]{2,1,0:T(8,128)}) custom-call(f32[128,128]{1,0:T(8,128)S(1)} %bitcast.4, f32[4,136,1152]{2,1,0:T(8,128)S(1)} %get-tuple-element.79.refs_0_.refs_1_, f32[4,136,1152]{2,1,0:T(8,128)S(1)} %get-tuple-element.92.refs_1_.refs_2_, f32[4,136,1152]{2,1,0:T(8,128)S(1)} %get-tuple-element.91.refs_2_.refs_7_.refs_3_, ...), custom_call_target="tpu_custom_call" | custom-call | flops 6266880 | tf_op jit(solution)/shard_map/pallas_call | solution.py:65
Async XLA Ops:
  5.8 6.2 %collective-permute-start = (f32[80,128]{1,0:T(8,128)S(1)}, f32[80,128]{1,0:T(8,128)S(1)}, u32[]{:S(2)}, u32[]{:S(2)}) collective-permute-start(f32[80,128]{1,0:T(8,128)S(1)} %get-tuple-element.59), channel_id=1, source_target_pairs={{0,1},{1,2},{2,3},{3,0},{4,5},{5,6},{6,7},{7,4},{8,9},{9,10},{10,1... | collective-permute-start | bytes 122888 | tf_op jit(solution)/shard_map/ppermute | solution.py:462
  8.0 4.0 %collective-permute-start.1 = (f32[80,128]{1,0:T(8,128)S(1)}, f32[80,128]{1,0:T(8,128)S(1)}, u32[]{:S(2)}, u32[]{:S(2)}) collective-permute-start(f32[80,128]{1,0:T(8,128)S(1)} %get-tuple-element.60), channel_id=1, source_target_pairs={{0,3},{1,0},{2,1},{3,2},{4,7},{5,4},{6,5},{7,6},{8,11},{9,8},{10,9... | collective-permute-start | bytes 122888 | tf_op jit(solution)/shard_map/ppermute | solution.py:462
  14.8 13.1 %collective-permute-start.5 = (f32[2,120,1152]{2,1,0:T(8,128)S(1)}, f32[2,120,1152]{2,1,0:T(8,128)S(1)}, u32[]{:S(2)}, u32[]{:S(2)}) collective-permute-start(f32[2,120,1152]{2,1,0:T(8,128)S(1)} %get-tuple-element.85.refs_2_), channel_id=1, source_target_pairs={{0,64},{64,0},{1,65},{65,1},{2,66},{66,2},{3,67},{67,3},{4,68},{68... | collective-permute-start | bytes 3317768 | tf_op jit(solution)/shard_map/ppermute | solution.py:462
  15.9 11.0 %collective-permute-start.2 = (f32[40,1152]{1,0:T(8,128)S(1)}, f32[40,1152]{1,0:T(8,128)S(1)}, u32[]{:S(2)}, u32[]{:S(2)}) collective-permute-start(f32[40,1152]{1,0:T(8,128)S(1)} %get-tuple-element.75), channel_id=1, source_target_pairs={{0,4},{4,8},{8,12},{12,16},{16,20},{20,24},{24,28},{28,32},{32,36}... | collective-permute-start | bytes 552968 | tf_op jit(solution)/shard_map/ppermute | solution.py:462
  17.6 9.2 %collective-permute-start.3 = (f32[40,1152]{1,0:T(8,128)S(1)}, f32[40,1152]{1,0:T(8,128)S(1)}, u32[]{:S(2)}, u32[]{:S(2)}) collective-permute-start(f32[40,1152]{1,0:T(8,128)S(1)} %get-tuple-element.76), channel_id=1, source_target_pairs={{0,60},{4,0},{8,4},{12,8},{16,12},{20,16},{24,20},{28,24},{32,28},... | collective-permute-start | bytes 552968 | tf_op jit(solution)/shard_map/ppermute | solution.py:462
  27.2 1.8 %collective-permute-start.4 = (f32[2,16,1152]{2,1,0:T(8,128)S(1)}, f32[2,16,1152]{2,1,0:T(8,128)S(1)}, u32[]{:S(2)}, u32[]{:S(2)}) collective-permute-start(f32[2,16,1152]{2,1,0:T(8,128)S(1)} %get-tuple-element.84.refs_7_), channel_id=1, source_target_pairs={{0,64},{64,0},{1,65},{65,1},{2,66},{66,2},{3,67},{67,3},{4,68},{68... | collective-permute-start | bytes 442376 | tf_op jit(solution)/shard_map/ppermute | solution.py:462
  31.4 2.1 %collective-permute-start.6 = (f32[136,1152]{1,0:T(8,128)S(1)}, f32[136,1152]{1,0:T(8,128)S(1)}, u32[]{:S(2)}, u32[]{:S(2)}) collective-permute-start(f32[136,1152]{1,0:T(8,128)S(1)} %get-tuple-element.89.refs_4_), channel_id=1, source_target_pairs={{0,64},{64,0},{1,65},{65,1},{2,66},{66,2},{3,67},{67,3},{4,68},{68... | collective-permute-start | bytes 1880072 | tf_op jit(solution)/shard_map/ppermute | solution.py:462

commit v4 on v3

--- a/solution.py
+++ b/solution.py
@@ -11,9 +11,9 @@
 
 RIGHT, ROW, COL, VIA, GROUND = range(5)
 FIELDS = 5
-EARLY = (RIGHT, ROW, COL)
+EARLY = (RIGHT, ROW)
 SUB, LANE = 8, 128
-INNER, IMAGE, DOTS, FINAL = 3, 2, 2, 4
+INNER, IMAGE, DOTS, FINAL = 3, 3, 3, 2
 PX = ("px_0", "px_1")
 ALL = ("layer", "px_0", "px_1", "py")
 
@@ -39,16 +39,20 @@
 
 def sweep(low, high, several, body, carry=()):
     steps = (high - low) // several
-
-    def step(i, carry):
-        for j in range(several):
-            carry = body(low + i * several + j, carry)
+    carry = lax.fori_loop(
+        0, steps, lambda i, carry: body(low + i * several, several, carry), carry
+    )
+    left = high - low - steps * several
+    return body(high - left, left, carry) if left else carry
+
+
+def each(body):
+    def run(t, n, carry):
+        for i in range(n):
+            carry = body(t + i, carry)
         return carry
 
-    carry = lax.fori_loop(0, steps, step, carry)
-    for t in range(low + steps * several, high):
-        carry = body(t, carry)
-    return carry
+    return run
 
 
 def spec_of(kind):
@@ -121,29 +125,37 @@
     others = begin(2, LANE, last, 0, EARLY)
     for copy in edges:
         copy.wait()
-    lane = lanes((SUB, LANE))
-
-    def body(t, carry):
+
+    def mask(t, carry):
         masked(core, depth, range(depth), t, e[VIA], masks, 0, LANE, 0)
         masked(core, depth, range(depth), t, e[VIA], masks, last, cols, LANE)
-        to_right = jnp.zeros((SUB, LANE), jnp.float32)
-        to_left = jnp.zeros((SUB, LANE), jnp.float32)
+        return carry
+
+    sweep(0, rows // SUB, 4, each(mask))
+    several = 2 * SUB
+    lane = lanes((several, LANE))
+    pair = lane // 2
+
+    def place(i, _):
+        at = pl.ds(pl.multiple_of(i * several, several), several)
+        to_right = jnp.zeros((several, LANE), jnp.float32)
+        to_left = jnp.zeros((several, LANE), jnp.float32)
         for f in range(FIELDS):
             for k in range(depth):
                 q = f * depth + k
-                tail = e[f][k, tile(t), last:cols]
-                head = e[f][k, tile(t), 0:LANE]
+                tail = e[f][k, at, last:cols]
+                head = e[f][k, at, 0:LANE]
                 if f == GROUND:
-                    across = pltpu.roll(e[COL][k, tile(t), last:cols], 1, 1)
+                    across = pltpu.roll(e[COL][k, at, last:cols], 1, 1)
                     tail = tail + jnp.where(lane == LANE - 2, across, 0.0)
                 shift = 4 * q + 2
-                to_right = jnp.where((lane // 2) == 2 * q, pltpu.roll(tail, shift, 1), to_right)
-                to_left = jnp.where((lane // 2) == 2 * q + 1, pltpu.roll(head, shift, 1), to_left)
-        pack[0, tile(t), :] = to_right
-        pack[1, tile(t), :] = to_left
-        return carry
-
-    sweep(0, rows // SUB, 4, body)
+                to_right = jnp.where(pair == 2 * q, pltpu.roll(tail, shift, 1), to_right)
+                to_left = jnp.where(pair == 2 * q + 1, pltpu.roll(head, shift, 1), to_left)
+        pack[0, at, :] = to_right
+        pack[1, at, :] = to_left
+        return 0
+
+    lax.fori_loop(0, rows // several, place, 0)
     used = msg_right.shape[0]
     msg_right[...] = pack[0].T[0:used]
     msg_left[...] = pack[1].T[0:used]
@@ -166,7 +178,7 @@
             masked(core, depth, (k,), t, e[VIA], masks, low, high, 0)
             return carry
 
-        sweep(0, rows // SUB, 4, body)
+        sweep(0, rows // SUB, 4, each(body))
     for copy in others:
         copy.wait()
 
@@ -269,21 +281,20 @@
         e[ROW][k, end, :] = jnp.where(edge, 0.0, row)
 
 
-def inner_kernel(depth, rows, cols, places, *refs):
-    both, e, (fwd, gain, inv, out) = refs[5], refs[6:11], refs[11:15]
+def inner_kernel(depth, rows, cols, places, low, high, held, *refs):
+    both, e, (fwd, gain, inv, out) = refs[FIELDS + held], refs[-9:-4], refs[-4:]
     keep = kept_columns(places[1])
-    last = rows // SUB - 1
 
     def unpack(t, carry):
         unpack_columns(depth, cols, keep, t, both, e)
         return carry
 
     def body(t, carry):
-        eliminate(depth, rows, cols, places, t, e, fwd, gain, inv, out, t - 1)
+        eliminate(depth, rows, cols, places, t, e, fwd, gain, inv, out, t - low)
         return carry
 
-    sweep(1, last, 2, unpack)
-    sweep(1, last + 1, INNER, body)
+    sweep(low, min(high, rows // SUB - 1), 2, each(unpack))
+    sweep(low, high, INNER, each(body))
 
 
 def outer_kernel(depth, rows, cols, places, *refs):
@@ -315,17 +326,20 @@
         out[k, tile(t), :] = value
 
 
-def neighbours(k, t, count, sub, field, row, col):
-    nxt = jnp.where(t == count - 1, 0, t + 1)
-    pre = jnp.where(t == 0, count - 1, t - 1)
-    r = row[k, tile(t), :]
-    c = col[k, tile(t), :]
-    z = field[k, tile(t), :]
-    down = pltpu.roll(jnp.where(sub == 0, field[k, tile(nxt), :], z), SUB - 1, 0)
-    flow = row[k, tile(pre), :] * field[k, tile(pre), :]
-    up = pltpu.roll(jnp.where(sub == SUB - 1, flow, r * z), 1, 0)
-    total = r * down + up + c * pltpu.roll(z, z.shape[1] - 1, 1) + pltpu.roll(c * z, 1, 1)
-    return (total, z)
+def stencil(k, t, n, count, sub, field, row, col):
+    wrap = lambda i: i % count if isinstance(i, int) else i
+    z = [field[k, tile(wrap(t + i)), :] for i in range(-1, n + 1)]
+    r = [row[k, tile(wrap(t + i)), :] for i in range(-1, n)]
+    flows = [a * b for a, b in zip(r, z)]
+    totals = []
+    for i in range(1, n + 1):
+        here = z[i]
+        c = col[k, tile(wrap(t + i - 1)), :]
+        down = pltpu.roll(jnp.where(sub == 0, z[i + 1], here), SUB - 1, 0)
+        up = pltpu.roll(jnp.where(sub == SUB - 1, flows[i - 1], flows[i]), 1, 0)
+        across = pltpu.roll(here, here.shape[1] - 1, 1)
+        totals.append(r[i] * down + up + c * across + pltpu.roll(c * here, 1, 1))
+    return totals, z[1 : n + 1]
 
 
 def join(depth, t, slot, fwd, gain, mine, theirs, inv4, z):
@@ -334,38 +348,58 @@
     back(depth, t, fwd, gain, (mine[0, tile(slot), :] + theirs[0, tile(slot), :]) * ratio, z)
 
 
-def inner_solve_kernel(depth, rows, *refs):
-    (fwd, gain, mine, theirs, z, inv4) = refs
-
-    def body(t, carry):
-        join(depth, t, t - 1, fwd, gain, mine, theirs, inv4, z)
+def image_of(depth, t, n, count, sub, slots, refs):
+    right, row, col, via, gain, inv, z, w, fwd2, out = refs
+    wrap = lambda i: i % count if isinstance(i, int) else i
+    f = [None] * n
+    for k in range(depth):
+        totals, _ = stencil(k, t, n, count, sub, z, row, col)
+        for i in range(n):
+            at = tile(wrap(t + i))
+            value = right[k, at, :] - totals[i]
+            w[k, at, :] = value
+            if k:
+                value = value + via[k - 1, at, :] * f[i]
+            f[i] = value * inv[k, at, :]
+            fwd2[k, at, :] = f[i]
+            if k == depth - 1:
+                out[tile(slots + i), :] = gain[k, at, :] * value
+
+
+def inner_image_kernel(depth, rows, cols, low, high, first, *refs):
+    right, row, col, via, fwd, gain, inv, mine, theirs = refs[0:9]
+    z, inv4, w, fwd2, out = refs[-5:]
+    count = rows // SUB + 1
+    sub = sublanes((SUB, cols + LANE))
+
+    def solve(t):
+        join(depth, t, t - low, fwd, gain, mine, theirs, inv4, z)
+
+    begin = low + 1 if first else low - 1
+    for t in range(low, begin + 1):
+        solve(t)
+
+    def body(t, n, carry):
+        for i in range(n):
+            solve(t + 1 + i)
+        image_of(
+            depth, t, n, count, sub, t - 2, (right, row, col, via, gain, inv, z, w, fwd2, out)
+        )
         return carry
 
-    sweep(1, rows // SUB, 3, body)
-
-
-def image_kernel(depth, rows, cols, *refs):
-    (right, row, col, via, fwd, gain, inv, mine, theirs, _, _, z, inv4, w, fwd2, out) = refs
+    sweep(begin, high - 1, IMAGE, body)
+
+
+def outer_image_kernel(depth, rows, cols, *refs):
+    (right, row, col, via, fwd, gain, inv, mine, theirs) = refs[0:9]
+    z, inv4, w, fwd2, out = refs[13:18]
     count = rows // SUB + 1
     sub = sublanes((SUB, cols + LANE))
     join(depth, 0, 0, fwd, gain, mine, theirs, inv4, z)
     join(depth, count - 1, 1, fwd, gain, mine, theirs, inv4, z)
-
-    def body(t, carry):
-        f = None
-        for k in range(depth):
-            total, _ = neighbours(k, t, count, sub, z, row, col)
-            value = right[k, tile(t), :] - total
-            w[k, tile(t), :] = value
-            if k:
-                value = value + via[k - 1, tile(t), :] * f
-            f = value * inv[k, tile(t), :]
-            fwd2[k, tile(t), :] = f
-            if k == depth - 1:
-                out[tile(t), :] = gain[k, tile(t), :] * value
-        return carry
-
-    sweep(0, count, IMAGE, body)
+    image_of(
+        depth, count - 2, 4, count, sub, 0, (right, row, col, via, gain, inv, z, w, fwd2, out)
+    )
 
 
 def gathered(sums, parts):
@@ -389,37 +423,57 @@
         return (rho, c)
 
     zero = jnp.zeros((SUB, cols), jnp.float32)
-    acc[0], acc[1] = sweep(0, rows // SUB, 2, body, (zero, zero))
-
-
-def dots_kernel(depth, rows, cols, *refs):
-    (row, col, fwd2, gain, mine, theirs, inv4, w, early, y, v, sums) = refs
-    count = rows // SUB + 1
-    wide = cols + LANE
-    sub = sublanes((SUB, wide))
-
-    def solve(t):
-        back(depth, t, fwd2, gain, (mine[tile(t), :] + theirs[tile(t), :]) * inv4[tile(t), :], y)
-
-    solve(count - 1)
-    solve(0)
-
-    def body(t, carry):
-        e, g = carry
-        solve(t + 1)
-        for k in range(depth):
-            total, yy = neighbours(k, t, count, sub, y, row, col)
-            yy = yy[:, 0:cols]
-            first = w[k, tile(t), 0:cols]
-            second = first - total[:, 0:cols]
-            v[k, tile(t), :] = second
+    acc[0], acc[1] = sweep(0, rows // SUB, 2, each(body), (zero, zero))
+
+
+def second_image_of(depth, cols, t, n, count, sub, refs, carry):
+    row, col, w, y, v = refs
+    e, g = carry
+    for k in range(depth):
+        totals, fields = stencil(k, t, n, count, sub, y, row, col)
+        for i in range(n):
+            yy = fields[i][:, 0:cols]
+            first = w[k, tile(t + i), 0:cols]
+            second = first - totals[i][:, 0:cols]
+            v[k, tile(t + i), :] = second
             e = e + first * yy
             g = g + yy * second
-        return (e, g)
+    return e, g
+
+
+def inner_dots_kernel(depth, rows, cols, *refs):
+    (row, col, fwd2, gain, mine, theirs, inv4, w, y, v, acc) = refs
+    count = rows // SUB + 1
+    sub = sublanes((SUB, cols + LANE))
+
+    def solve(t):
+        middle = (mine[tile(t - 2), :] + theirs[tile(t - 2), :]) * inv4[tile(t), :]
+        back(depth, t, fwd2, gain, middle, y)
+
+    solve(2)
+    solve(3)
+
+    def body(t, n, carry):
+        for i in range(n):
+            solve(t + 1 + i)
+        return second_image_of(depth, cols, t, n, count, sub, (row, col, w, y, v), carry)
 
     zero = jnp.zeros((SUB, cols), jnp.float32)
-    e, g = sweep(0, count - 1, DOTS, body, (zero, zero))
-    sums[...] = gathered(sums, (early[0], early[1], e, g))
+    acc[0], acc[1] = sweep(3, count - 3, DOTS, body, (zero, zero))
+
+
+def outer_dots_kernel(depth, rows, cols, *refs):
+    (row, col, fwd2, gain, mine, theirs, inv4, w, early, acc) = refs[0:10]
+    y, v, sums = refs[12:15]
+    count = rows // SUB + 1
+    sub = sublanes((SUB, cols + LANE))
+    for slot, t in enumerate((count - 2, count - 1, 0, 1)):
+        middle = (mine[tile(slot), :] + theirs[tile(slot), :]) * inv4[tile(t), :]
+        back(depth, t, fwd2, gain, middle, y)
+    carry = (acc[0], acc[1])
+    for t, n in ((count - 3, 2), (0, 3)):
+        carry = second_image_of(depth, cols, t, n, count, sub, (row, col, w, y, v), carry)
+    sums[...] = gathered(sums, (early[0], early[1], *carry))
 
 
 def final_kernel(depth, rows, cols, *refs):
@@ -447,7 +501,7 @@
             )
             return carry
 
-        sweep(0, rows // SUB, FINAL, body)
+        sweep(0, rows // SUB, FINAL, each(body))
         at = layer_of(core, k, depth)
         for slot, (value, target) in enumerate(((x, x_out), (r, r_out))):
             copy = pltpu.make_async_copy(value.at[k], target.at[at], sem.at[slot, k])
@@ -513,15 +567,44 @@
     )
     from_above = shift(msg_down, PX, 1)
     from_below = shift(msg_up, PX, -1)
+    end = rows // SUB
+    split = end // 2 + 1
+    flops = 15 * size
     *state, mine = call(
-        part(inner_kernel, depth, rows, cols, places),
+        part(inner_kernel, depth, rows, cols, places, 1, split, 0),
         [*e, both],
         [vmem] * 6,
-        [ext] * FIELDS + [ext] * 3 + [(2, rows - SUB, wide)],
+        [ext] * FIELDS + [ext] * 3 + [(2, (split - 1) * SUB, wide)],
         alias={i: i for i in range(FIELDS)},
-        flops=30 * size,
+        flops=flops,
     )
     theirs = shift(mine, "layer", 1)
+    *state, mine_rest = call(
+        part(inner_kernel, depth, rows, cols, places, split, end, 3),
+        [*state, both],
+        [vmem] * 9,
+        [ext] * FIELDS + [ext] * 3 + [(2, (end - split) * SUB, wide)],
+        alias={i: i for i in range(FIELDS + 3)},
+        flops=flops,
+    )
+    theirs_rest = shift(mine_rest, "layer", 1)
+    right, row, col, via, _, fwd, gain, inv = state
+    images = [ext, (tall, wide), ext, ext, (tall - 4 * SUB, wide)]
+    images = call(
+        part(inner_image_kernel, depth, rows, cols, 1, split, True),
+        [right, row, col, via, fwd, gain, inv, mine, theirs],
+        [vmem] * 9,
+        images,
+        flops=flops,
+    )
+    z, inv4, w, fwd2, mine2 = call(
+        part(inner_image_kernel, depth, rows, cols, split, end, False),
+        [right, row, col, via, fwd, gain, inv, mine_rest, theirs_rest, *images],
+        [vmem] * 14,
+        [ext, (tall, wide), ext, ext, (tall - 4 * SUB, wide)],
+        alias={9 + i: i for i in range(5)},
+        flops=flops,
+    )
     *e, fwd, gain, inv, mine_outer = call(
         part(outer_kernel, depth, rows, cols, places),
         [*state, from_above, from_below],
@@ -532,22 +615,16 @@
     )
     right, row, col, via, _ = e
     theirs_outer = shift(mine_outer, "layer", 1)
-    z, inv4 = call(
-        part(inner_solve_kernel, depth, rows),
-        [fwd, gain, mine, theirs],
-        [vmem] * 4,
-        [ext, (tall, wide)],
+    theirs2 = shift(mine2, "layer", 1)
+    z, inv4, w, fwd2, mine2_outer = call(
+        part(outer_image_kernel, depth, rows, cols),
+        [right, row, col, via, fwd, gain, inv, mine_outer, theirs_outer, z, inv4, w, fwd2],
+        [vmem] * 13,
+        [ext, (tall, wide), ext, ext, (4 * SUB, wide)],
+        alias={9: 0, 10: 1, 11: 2, 12: 3},
         flops=8 * size,
     )
-    z, inv4, w, fwd2, mine2 = call(
-        part(image_kernel, depth, rows, cols),
-        [right, row, col, via, fwd, gain, inv, mine_outer, theirs_outer, z, inv4],
-        [vmem] * 11,
-        [ext, (tall, wide)] + [ext] * 2 + [(tall, wide)],
-        alias={9: 0, 10: 1},
-        flops=30 * size,
-    )
-    theirs2 = shift(mine2, "layer", 1)
+    theirs2_outer = shift(mine2_outer, "layer", 1)
     (early,) = call(
         part(early_kernel, depth, rows, cols),
         [right, z, w],
@@ -555,20 +632,29 @@
         [(2, SUB, cols)],
         flops=4 * size,
     )
+    block = (depth, rows, cols)
+    y, v, acc = call(
+        part(inner_dots_kernel, depth, rows, cols),
+        [row, col, fwd2, gain, mine2, theirs2, inv4, w],
+        [vmem] * 8,
+        [ext, block, (2, SUB, cols)],
+        flops=20 * size,
+    )
     y, v, sums = call(
-        part(dots_kernel, depth, rows, cols),
-        [row, col, fwd2, gain, mine2, theirs2, inv4, w, early],
-        [vmem] * 9,
-        [ext, (depth, rows, cols), (devices, LANE)],
-        flops=20 * size,
+        part(outer_dots_kernel, depth, rows, cols),
+        [row, col, fwd2, gain, mine2_outer, theirs2_outer, inv4, w, early, acc, y, v],
+        [vmem] * 12,
+        [ext, block, (devices, LANE)],
+        alias={10: 0, 11: 1},
+        flops=8 * size,
     )
     sums = lax.all_to_all(sums.reshape(devices, 1, LANE), ALL, 0, 0).reshape(devices, LANE)
-    block = jax.ShapeDtypeStruct((depth, rows, cols), jnp.float32)
+    result = jax.ShapeDtypeStruct(block, jnp.float32)
     return call(
         part(final_kernel, depth, rows, cols),
         [sums, right, z, w, y, v],
         [vmem] * 6,
-        [block] * 2,
+        [result] * 2,
         [
             pltpu.VMEM((depth, rows, cols), jnp.float32),
             pltpu.VMEM((depth, rows, cols), jnp.float32),

time: 56.7 us -> 52.1 us (0.919)
  waiting for transfers between devices: 6.82 us -> 2.46 us
  starting transfers between devices: 12 us -> 13.3 us
  Pallas kernels: 19.3 us -> 18.4 us
  blocking collectives: 17.7 us -> 17.1 us
    ppermute x7 -> x9, waiting for transfers between devices: 6.82 us -> 2.46 us  [shift(): lax.ppermute(value, axis, [(i, (i + by) % count) for i in range(count)])]
    ppermute x7 -> x9, starting transfers between devices: 12 us -> 13.3 us  [shift(): lax.ppermute(value, axis, [(i, (i + by) % count) for i in range(count)])]
    pallas_call x10 -> x13, Pallas kernels: 19.3 us -> 18.4 us  [call(): pl.pallas_call(body, out_shape=shapes, in_specs=[spec_of(k) for k in kind...]
    all_to_all x1, blocking collectives: 17.7 us -> 17.1 us  [shards(): lax.all_to_all(sums.reshape(devices, 1, LANE), ALL, 0, 0)]
  transfers between devices with their start and end apart: 7 -> 9, of which waited for: 3 -> 2; matrix products, arithmetic and copies ran while one was open for 0% -> 0% of each run, Pallas kernels for 6% -> 18%
where the time goes in v4:
time: 52.1 us; the launch traced here: 52 us
  Pallas kernels  18.4 us (35%)
  blocking collectives  17.1 us (33%)
  starting transfers between devices  13.3 us (26%)
  waiting for transfers between devices  2.46 us (5%)
  between operations  0.75 us (1%)
    pallas_call x13, Pallas kernels, call(): pl.pallas_call(body, out_shape=shapes, in_specs=[spec_of(k) for k in kind...  18.4 us
    all_to_all x1, blocking collectives, shards(): lax.all_to_all(sums.reshape(devices, 1, LANE), ALL, 0, 0)  17.1 us
    ppermute x9, starting transfers between devices, shift(): lax.ppermute(value, axis, [(i, (i + by) % count) for i in range(count)])  13.3 us
    ppermute x9, waiting for transfers between devices, shift(): lax.ppermute(value, axis, [(i, (i + by) % count) for i in range(count)])  2.46 us
  transfers between devices with their start and end apart: 9, of which 2 were waited for; matrix products, arithmetic and copies ran while one was open for 0% of the time, Pallas kernels for 18%

profile of v4, /device:TPU:1, one launch (start us, length us, event | category | flops | bytes accessed | tf_op | source)
XLA Modules:
  0.0 52.0 jit_solution(16168174367929923221)
XLA Ops:
  0.6 4.2 %shard_map.77 = (f32[4,136,1152]{2,1,0:T(8,128)S(1)}, f32[4,136,1152]{2,1,0:T(8,128)S(1)}, f32[4,136,1152]{2,1,0:T(8,128)S(1)}, f32[4,136,1152]{2,1,0:T(8,128)S(...) custom-call(f32[4,128,1024]{2,1,0:T(8,128)} %refs_0_.3, f32[4,128,1024]{2,1,0:T(8,128)} %refs_1_.3, ...), custom_call_target="tpu_custom_call" | custom-call | flops 626688 | bytes 3760128 | tf_op jit(solution)/shard_map/pallas_call | solution.py:69
  4.8 2.2 %collective-permute-start = (f32[80,128]{1,0:T(8,128)S(1)}, f32[80,128]{1,0:T(8,128)S(1)}, u32[]{:S(2)}, u32[]{:S(2)}) collective-permute-start(f32[80,128]{1,0:T(8,128)S(1)} %get-tuple-element.79), channel_id=1, source_target_pairs={{0,1},{1,2},{2,3},{3,0},{4,5},{5,6},{6,7},{7,4},{8,9},{9,10},{10,1... | collective-permute-start | bytes 122888 | tf_op jit(solution)/shard_map/ppermute | solution.py:516
  7.0 1.5 %collective-permute-start.1 = (f32[80,128]{1,0:T(8,128)S(1)}, f32[80,128]{1,0:T(8,128)S(1)}, u32[]{:S(2)}, u32[]{:S(2)}) collective-permute-start(f32[80,128]{1,0:T(8,128)S(1)} %get-tuple-element.80), channel_id=1, source_target_pairs={{0,3},{1,0},{2,1},{3,2},{4,7},{5,4},{6,5},{7,6},{8,11},{9,8},{10,9... | collective-permute-start | bytes 122888 | tf_op jit(solution)/shard_map/ppermute | solution.py:516
  8.5 3.0 %shard_map.78 = (f32[4,136,1152]{2,1,0:T(8,128)S(1)}, f32[4,136,1152]{2,1,0:T(8,128)S(1)}, f32[4,136,1152]{2,1,0:T(8,128)S(1)}, f32[4,136,1152]{2,1,0:T(8,128)S(1)}, f32[4,136,1152]{2,1,0:T(8,128)S(1)}) custom-call(f32[4,128,1024]{2,1,0:T(8,128)} %refs_0_.3, ...), custom_call_target="tpu_custom_call", output_to_operand_aliasing={{0}: (6, {}), {1}: (7, {}), {2}: (8, {}), {3}: (9, {}), {4}... | custom-call | flops 6266880 | bytes 11280384 | tf_op jit(solution)/shard_map/pallas_call | solution.py:69
  11.5 0.0 collective-permute-done.refs_5_
  11.5 0.0 collective-permute-done.1.refs_6_
  11.5 0.2 shard_map.79
  11.7 1.4 %shard_map.80 = (f32[4,136,1152]{2,1,0:T(8,128)S(1)}, f32[4,136,1152]{2,1,0:T(8,128)S(1)}, f32[4,136,1152]{2,1,0:T(8,128)S(1)}, f32[4,136,1152]{2,1,0:T(8,128)S(...) custom-call(f32[4,136,1152]{2,1,0:T(8,128)S(1)} %get-tuple-element.8, ...), custom_call_target="tpu_custom_call", output_to_operand_aliasing={{0}: (0, {}), {1}: (1, {}), {2}: (2, {}), {3}: (3, {}), {4}... | custom-call | flops 9400320 | tf_op jit(solution)/shard_map/pallas_call | solution.py:69
  13.1 1.1 %collective-permute-start.6 = (f32[2,64,1152]{2,1,0:T(8,128)S(1)}, f32[2,64,1152]{2,1,0:T(8,128)S(1)}, u32[]{:S(2)}, u32[]{:S(2)}) collective-permute-start(f32[2,64,1152]{2,1,0:T(8,128)S(1)} %get-tuple-element.114.refs_7_), channel_id=1, source_target_pairs={{0,64},{64,0},{1,65},{65,1},{2,66},{66,2},{3,67},{67,3},{4,68},{68... | collective-permute-start | bytes 1769480 | tf_op jit(solution)/shard_map/ppermute | solution.py:516
  14.2 1.2 %shard_map.81 = (f32[4,136,1152]{2,1,0:T(8,128)S(1)}, f32[4,136,1152]{2,1,0:T(8,128)S(1)}, f32[4,136,1152]{2,1,0:T(8,128)S(1)}, f32[4,136,1152]{2,1,0:T(8,128)S(...) custom-call(f32[4,136,1152]{2,1,0:T(8,128)S(1)} %get-tuple-element.8, ...), custom_call_target="tpu_custom_call", output_to_operand_aliasing={{0}: (0, {}), {1}: (1, {}), {2}: (2, {}), {3}: (3, {}), {4}... | custom-call | flops 9400320 | tf_op jit(solution)/shard_map/pallas_call | solution.py:69
  15.4 0.1 collective-permute-start.5
  15.5 1.8 %collective-permute-start.2 = (f32[40,1152]{1,0:T(8,128)S(1)}, f32[40,1152]{1,0:T(8,128)S(1)}, u32[]{:S(2)}, u32[]{:S(2)}) collective-permute-start(f32[40,1152]{1,0:T(8,128)S(1)} %get-tuple-element.103), channel_id=1, source_target_pairs={{0,4},{4,8},{8,12},{12,16},{16,20},{20,24},{24,28},{28,32},{32,36}... | collective-permute-start | bytes 552968 | tf_op jit(solution)/shard_map/ppermute | solution.py:516
  17.3 4.4 %collective-permute-start.3 = (f32[40,1152]{1,0:T(8,128)S(1)}, f32[40,1152]{1,0:T(8,128)S(1)}, u32[]{:S(2)}, u32[]{:S(2)}) collective-permute-start(f32[40,1152]{1,0:T(8,128)S(1)} %get-tuple-element.104), channel_id=1, source_target_pairs={{0,60},{4,0},{8,4},{12,8},{16,12},{20,16},{24,20},{28,24},{32,28},... | collective-permute-start | bytes 552968 | tf_op jit(solution)/shard_map/ppermute | solution.py:516
  21.7 0.0 collective-permute-done.6.refs_8_
  21.7 1.1 %shard_map.83 = (f32[4,136,1152]{2,1,0:T(8,128)S(1)}, f32[136,1152]{1,0:T(8,128)S(1)}, f32[4,136,1152]{2,1,0:T(8,128)S(1)}, f32[4,136,1152]{2,1,0:T(8,128)S(1)}, f32[104,1152]{1,0:T(8,128)S(1)}) custom-call(f32[4,136,1152]{2,1,0:T(8,128)S(1)} %get-tuple-element.95.refs_0_, f32[4,136,1152]{2,1,0:T(8,128)S(1)} %get-tuple-element.96.refs_1_, ...), custom_call_target="tpu_custom_call" | custom-call | flops 9400320 | tf_op jit(solution)/shard_map/pallas_call | solution.py:69
  22.8 0.0 collective-permute-done.5.refs_8_
  22.8 1.2 %shard_map.84 = (f32[4,136,1152]{2,1,0:T(8,128)S(1)}, f32[136,1152]{1,0:T(8,128)S(1)}, f32[4,136,1152]{2,1,0:T(8,128)S(1)}, f32[4,136,1152]{2,1,0:T(8,128)S(1)}, f32[104,1152]{1,0:T(8,128)S(1)}) custom-call(f32[4,136,1152]{2,1,0:T(8,128)S(1)} %get-tuple-element.95.refs_0_, ...), custom_call_target="tpu_custom_call", output_to_operand_aliasing={{0}: (9, {}), {1}: (10, {}), {2}: (11, {}), {3}: (12, {}), ... | custom-call | flops 9400320 | tf_op jit(solution)/shard_map/pallas_call | solution.py:69
  24.1 0.7 %collective-permute-start.8 = (f32[104,1152]{1,0:T(8,128)S(1)}, f32[104,1152]{1,0:T(8,128)S(1)}, u32[]{:S(2)}, u32[]{:S(2)}) collective-permute-start(f32[104,1152]{1,0:T(8,128)S(1)} %get-tuple-element.129.refs_4_), channel_id=1, source_target_pairs={{0,64},{64,0},{1,65},{65,1},{2,66},{66,2},{3,67},{67,3},{4,68},{68... | collective-permute-start | bytes 1437704 | tf_op jit(solution)/shard_map/ppermute | solution.py:516
  24.8 1.4 %collective-permute-done.2.refs_8_ = f32[40,1152]{1,0:T(8,128)S(1)} collective-permute-done((f32[40,1152]{1,0:T(8,128)S(1)}, f32[40,1152]{1,0:T(8,128)S(1)}, u32[]{:S(2)}, u32[]{:S(2)}) %collective-permute-start.2) | collective-permute-done | bytes 184352 | tf_op jit(solution)/shard_map/ppermute | solution.py:516
  26.2 0.0 collective-permute-done.3.refs_9_
  26.2 0.3 shard_map.82
  26.5 1.1 %collective-permute-start.4 = (f32[2,16,1152]{2,1,0:T(8,128)S(1)}, f32[2,16,1152]{2,1,0:T(8,128)S(1)}, u32[]{:S(2)}, u32[]{:S(2)}) collective-permute-start(f32[2,16,1152]{2,1,0:T(8,128)S(1)} %get-tuple-element.112.refs_7_), channel_id=1, source_target_pairs={{0,64},{64,0},{1,65},{65,1},{2,66},{66,2},{3,67},{67,3},{4,68},{68... | collective-permute-start | bytes 442376 | tf_op jit(solution)/shard_map/ppermute | solution.py:516
  27.6 1.0 %collective-permute-done.4.refs_8_ = f32[2,16,1152]{2,1,0:T(8,128)S(1)} collective-permute-done((f32[2,16,1152]{2,1,0:T(8,128)S(1)}, f32[2,16,1152]{2,1,0:T(8,128)S(1)}, u32[]{:S(2)}, u32[]{:S(2)}) %collective-permute-start.4) | collective-permute-done | bytes 147488 | tf_op jit(solution)/shard_map/ppermute | solution.py:516
  28.6 0.6 %shard_map.85 = (f32[4,136,1152]{2,1,0:T(8,128)S(1)}, f32[136,1152]{1,0:T(8,128)S(1)}, f32[4,136,1152]{2,1,0:T(8,128)S(1)}, f32[4,136,1152]{2,1,0:T(8,128)S(1)}, f32[32,1152]{1,0:T(8,128)S(1)}) custom-call(f32[4,136,1152]{2,1,0:T(8,128)S(1)} %get-tuple-element.107.refs_0_.refs_1_, ...), custom_call_target="tpu_custom_call", output_to_operand_aliasing={{0}: (9, {}), {1}: (10, {}), {2}: (11, {}), {3}: (12, {})} | custom-call | flops 5013504 | tf_op jit(solution)/shard_map/pallas_call | solution.py:69
  29.2 0.4 collective-permute-start.7
  29.6 0.3 shard_map.86.refs_8_
  29.9 0.0 collective-permute-done.8.refs_5_
  29.9 1.8 %shard_map.87 = (f32[4,136,1152]{2,1,0:T(8,128)S(1)}, f32[4,128,1024]{2,1,0:T(8,128)S(1)}, f32[2,8,1024]{2,1,0:T(8,128)S(1)}) custom-call(f32[4,136,1152]{2,1,0:T(8,128)S(1)} %get-tuple-element.105.refs_1_.refs_0_, f32[4,136,1152]{2,1,0:T(8,128)S(1)} %get-tuple-element.106.refs_2_.refs_1_, f32[4,136,1152]{2,1,0:T(8,128)S(1)} %get-tuple-element.124.refs_2_, ...), custom_call_target="tpu_custom_call" | custom-call | flops 12533760 | tf_op jit(solution)/shard_map/pallas_call | solution.py:69
  31.7 0.0 collective-permute-done.7.refs_5_
  31.7 0.8 %shard_map.88 = (f32[4,136,1152]{2,1,0:T(8,128)S(1)}, f32[4,128,1024]{2,1,0:T(8,128)S(1)}, f32[128,128]{1,0:T(8,128)S(1)}) custom-call(f32[4,136,1152]{2,1,0:T(8,128)S(1)} %get-tuple-element.105.refs_1_.refs_0_, f32[4,136,1152]{2,1,0:T(8,128)S(1)} %get-tuple-element.106.refs_2_.refs_1_, ...), custom_call_target="tpu_custom_call", output_to_operand_aliasing={{0}: (10, {}), {1}: (11, {})} | custom-call | flops 5013504 | tf_op jit(solution)/shard_map/pallas_call | solution.py:69
  32.5 17.1 %all_to_all.5 = f32[128,1,128]{2,1,0:T(1,128)S(1)} all-to-all(f32[128,1,128]{2,1,0:T(1,128)S(1)} %bitcast.5), channel_id=1, replica_groups=mesh['layer'=2,'px_0'=4,'px_1'=4,'py'=4] {'layer','px_0','px_1','py'}, dimensions={0} | all-to-all | bytes 131072 | tf_op jit(solution)/shard_map/all_to_all | solution.py:651
  49.6 2.4 %shard_map.89 = (f32[4,128,1024]{2,1,0:T(8,128)}, f32[4,128,1024]{2,1,0:T(8,128)}) custom-call(f32[128,128]{1,0:T(8,128)S(1)} %bitcast.4, f32[4,136,1152]{2,1,0:T(8,128)S(1)} %get-tuple-element.107.refs_0_.refs_1_, f32[4,136,1152]{2,1,0:T(8,128)S(1)} %get-tuple-element.128.refs_1_.refs_2_, f32[4,136,1152]{2,1,0:T(8,128)S(1)} %get-tuple-element.127.refs_2_.refs_7_.refs_3_, ...), custom_call_target="tpu_custom_call" | custom-call | flops 6266880 | tf_op jit(solution)/shard_map/pallas_call | solution.py:69
Async XLA Ops:
  4.8 6.7 %collective-permute-start = (f32[80,128]{1,0:T(8,128)S(1)}, f32[80,128]{1,0:T(8,128)S(1)}, u32[]{:S(2)}, u32[]{:S(2)}) collective-permute-start(f32[80,128]{1,0:T(8,128)S(1)} %get-tuple-element.79), channel_id=1, source_target_pairs={{0,1},{1,2},{2,3},{3,0},{4,5},{5,6},{6,7},{7,4},{8,9},{9,10},{10,1... | collective-permute-start | bytes 122888 | tf_op jit(solution)/shard_map/ppermute | solution.py:516
  7.0 4.5 %collective-permute-start.1 = (f32[80,128]{1,0:T(8,128)S(1)}, f32[80,128]{1,0:T(8,128)S(1)}, u32[]{:S(2)}, u32[]{:S(2)}) collective-permute-start(f32[80,128]{1,0:T(8,128)S(1)} %get-tuple-element.80), channel_id=1, source_target_pairs={{0,3},{1,0},{2,1},{3,2},{4,7},{5,4},{6,5},{7,6},{8,11},{9,8},{10,9... | collective-permute-start | bytes 122888 | tf_op jit(solution)/shard_map/ppermute | solution.py:516
  13.1 8.6 %collective-permute-start.6 = (f32[2,64,1152]{2,1,0:T(8,128)S(1)}, f32[2,64,1152]{2,1,0:T(8,128)S(1)}, u32[]{:S(2)}, u32[]{:S(2)}) collective-permute-start(f32[2,64,1152]{2,1,0:T(8,128)S(1)} %get-tuple-element.114.refs_7_), channel_id=1, source_target_pairs={{0,64},{64,0},{1,65},{65,1},{2,66},{66,2},{3,67},{67,3},{4,68},{68... | collective-permute-start | bytes 1769480 | tf_op jit(solution)/shard_map/ppermute | solution.py:516
  15.4 7.4 %collective-permute-start.5 = (f32[2,56,1152]{2,1,0:T(8,128)S(1)}, f32[2,56,1152]{2,1,0:T(8,128)S(1)}, u32[]{:S(2)}, u32[]{:S(2)}) collective-permute-start(f32[2,56,1152]{2,1,0:T(8,128)S(1)} %get-tuple-element.113.refs_7_), channel_id=1, source_target_pairs={{0,64},{64,0},{1,65},{65,1},{2,66},{66,2},{3,67},{67,3},{4,68},{68... | collective-permute-start | bytes 1548296 | tf_op jit(solution)/shard_map/ppermute | solution.py:516
  15.5 10.7 %collective-permute-start.2 = (f32[40,1152]{1,0:T(8,128)S(1)}, f32[40,1152]{1,0:T(8,128)S(1)}, u32[]{:S(2)}, u32[]{:S(2)}) collective-permute-start(f32[40,1152]{1,0:T(8,128)S(1)} %get-tuple-element.103), channel_id=1, source_target_pairs={{0,4},{4,8},{8,12},{12,16},{16,20},{20,24},{24,28},{28,32},{32,36}... | collective-permute-start | bytes 552968 | tf_op jit(solution)/shard_map/ppermute | solution.py:516
  17.3 8.9 %collective-permute-start.3 = (f32[40,1152]{1,0:T(8,128)S(1)}, f32[40,1152]{1,0:T(8,128)S(1)}, u32[]{:S(2)}, u32[]{:S(2)}) collective-permute-start(f32[40,1152]{1,0:T(8,128)S(1)} %get-tuple-element.104), channel_id=1, source_target_pairs={{0,60},{4,0},{8,4},{12,8},{16,12},{20,16},{24,20},{28,24},{32,28},... | collective-permute-start | bytes 552968 | tf_op jit(solution)/shard_map/ppermute | solution.py:516
  24.1 5.9 %collective-permute-start.8 = (f32[104,1152]{1,0:T(8,128)S(1)}, f32[104,1152]{1,0:T(8,128)S(1)}, u32[]{:S(2)}, u32[]{:S(2)}) collective-permute-start(f32[104,1152]{1,0:T(8,128)S(1)} %get-tuple-element.129.refs_4_), channel_id=1, source_target_pairs={{0,64},{64,0},{1,65},{65,1},{2,66},{66,2},{3,67},{67,3},{4,68},{68... | collective-permute-start | bytes 1437704 | tf_op jit(solution)/shard_map/ppermute | solution.py:516
  26.5 2.1 %collective-permute-start.4 = (f32[2,16,1152]{2,1,0:T(8,128)S(1)}, f32[2,16,1152]{2,1,0:T(8,128)S(1)}, u32[]{:S(2)}, u32[]{:S(2)}) collective-permute-start(f32[2,16,1152]{2,1,0:T(8,128)S(1)} %get-tuple-element.112.refs_7_), channel_id=1, source_target_pairs={{0,64},{64,0},{1,65},{65,1},{2,66},{66,2},{3,67},{67,3},{4,68},{68... | collective-permute-start | bytes 442376 | tf_op jit(solution)/shard_map/ppermute | solution.py:516
  29.2 2.5 %collective-permute-start.7 = (f32[32,1152]{1,0:T(8,128)S(1)}, f32[32,1152]{1,0:T(8,128)S(1)}, u32[]{:S(2)}, u32[]{:S(2)}) collective-permute-start(f32[32,1152]{1,0:T(8,128)S(1)} %get-tuple-element.125.refs_4_), channel_id=1, source_target_pairs={{0,64},{64,0},{1,65},{65,1},{2,66},{66,2},{3,67},{67,3},{4,68},{68... | collective-permute-start | bytes 442376 | tf_op jit(solution)/shard_map/ppermute | solution.py:516

commit v5 on v4

--- a/solution.py
+++ b/solution.py
@@ -13,7 +13,7 @@
 FIELDS = 5
 EARLY = (RIGHT, ROW)
 SUB, LANE = 8, 128
-INNER, IMAGE, DOTS, FINAL = 3, 3, 3, 2
+INNER, IMAGE, DOTS, FINAL = 4, 3, 4, 2
 PX = ("px_0", "px_1")
 ALL = ("layer", "px_0", "px_1", "py")
 
@@ -119,8 +119,8 @@
     msg_right, msg_left, masks, pack, sem = refs[11:]
     core, _, _ = position()
     last = cols - LANE
+    begin = functools.partial(start_copies, core, depth, rows, sources, e, masks, sem)
     every = range(FIELDS + 1)
-    begin = functools.partial(start_copies, core, depth, rows, sources, e, masks, sem)
     edges = begin(0, 0, LANE, 0, every) + begin(1, last, cols, LANE, every)
     others = begin(2, LANE, last, 0, EARLY)
     for copy in edges:
@@ -132,14 +132,13 @@
         return carry
 
     sweep(0, rows // SUB, 4, each(mask))
-    several = 2 * SUB
+    several = 8 * SUB
     lane = lanes((several, LANE))
     pair = lane // 2
 
     def place(i, _):
         at = pl.ds(pl.multiple_of(i * several, several), several)
-        to_right = jnp.zeros((several, LANE), jnp.float32)
-        to_left = jnp.zeros((several, LANE), jnp.float32)
+        to_right = to_left = jnp.zeros((several, LANE), jnp.float32)
         for f in range(FIELDS):
             for k in range(depth):
                 q = f * depth + k
@@ -148,9 +147,10 @@
                 if f == GROUND:
                     across = pltpu.roll(e[COL][k, at, last:cols], 1, 1)
                     tail = tail + jnp.where(lane == LANE - 2, across, 0.0)
-                shift = 4 * q + 2
-                to_right = jnp.where(pair == 2 * q, pltpu.roll(tail, shift, 1), to_right)
-                to_left = jnp.where(pair == 2 * q + 1, pltpu.roll(head, shift, 1), to_left)
+                if q:
+                    head = pltpu.roll(head, 2 * q, 1)
+                to_right = jnp.where(pair == q, pltpu.roll(tail, 2 * q + 2, 1), to_right)
+                to_left = jnp.where(pair == q, head, to_left)
         pack[0, at, :] = to_right
         pack[1, at, :] = to_left
         return 0
@@ -202,9 +202,19 @@
     from_left, from_right = refs[5:7]
     e = refs[7:12]
     msg_down, msg_up, both = refs[12:15]
-    used = from_left.shape[0]
     both[...] = jnp.zeros_like(both)
-    both[0:used] = from_left[...] + from_right[...]
+    part = sublanes((SUB, LANE)) // 2
+    for m in range(from_left.shape[0] // SUB):
+        left = from_left[m * SUB : (m + 1) * SUB, :]
+        right = from_right[m * SUB : (m + 1) * SUB, :]
+        turn = lambda x, by: pltpu.roll(x, by % SUB, 0) if by % SUB else x
+        for half in range(2):
+            back_by = -4 * half
+            value = jnp.where(part == 0, turn(left, back_by), turn(right, 2 + back_by))
+            value = jnp.where(part == 2, turn(left, 2 + back_by), value)
+            value = jnp.where(part == 3, turn(right, 4 + back_by), value)
+            at = (2 * m + half) * SUB
+            both[at : at + SUB, :] = value
     both[...] = both[...].T
     keep = kept_columns(places)
     unpack_columns(depth, cols, keep, 0, both, e)
@@ -392,7 +402,7 @@
 
 def outer_image_kernel(depth, rows, cols, *refs):
     (right, row, col, via, fwd, gain, inv, mine, theirs) = refs[0:9]
-    z, inv4, w, fwd2, out = refs[13:18]
+    early, (z, inv4, w, fwd2, out, acc) = refs[9], refs[14:20]
     count = rows // SUB + 1
     sub = sublanes((SUB, cols + LANE))
     join(depth, 0, 0, fwd, gain, mine, theirs, inv4, z)
@@ -400,6 +410,10 @@
     image_of(
         depth, count - 2, 4, count, sub, 0, (right, row, col, via, gain, inv, z, w, fwd2, out)
     )
+    carry = (early[0], early[1])
+    for t in (count - 2, 0, 1):
+        carry = first_dots(depth, cols, t, (right, z, w), carry)
+    acc[0], acc[1] = carry
 
 
 def gathered(sums, parts):
@@ -411,19 +425,21 @@
     return result
 
 
+def first_dots(depth, cols, t, refs, carry):
+    right, z, w = refs
+    rho, c = carry
+    for k in range(depth):
+        zz = z[k, tile(t), 0:cols]
+        rho = rho + right[k, tile(t), 0:cols] * zz
+        c = c + zz * w[k, tile(t), 0:cols]
+    return (rho, c)
+
+
 def early_kernel(depth, rows, cols, *refs):
-    (right, z, w, acc) = refs
-
-    def body(t, carry):
-        rho, c = carry
-        for k in range(depth):
-            zz = z[k, tile(t), 0:cols]
-            rho = rho + right[k, tile(t), 0:cols] * zz
-            c = c + zz * w[k, tile(t), 0:cols]
-        return (rho, c)
-
+    *refs, acc = refs
     zero = jnp.zeros((SUB, cols), jnp.float32)
-    acc[0], acc[1] = sweep(0, rows // SUB, 2, each(body), (zero, zero))
+    body = lambda t, carry: first_dots(depth, cols, t, refs, carry)
+    acc[0], acc[1] = sweep(2, rows // SUB - 1, 2, each(body), (zero, zero))
 
 
 def second_image_of(depth, cols, t, n, count, sub, refs, carry):
@@ -527,7 +543,7 @@
     part = functools.partial
 
     inputs = [right_side, row_conduct, column_conduct, via_conduct, ground_conduct, via_mask]
-    strips = (FIELDS * depth * 4, LANE)
+    strips = (FIELDS * depth * 2, LANE)
     *e, msg_right, msg_left = call(
         part(load_kernel, depth, rows, cols),
         inputs,
@@ -616,15 +632,6 @@
     right, row, col, via, _ = e
     theirs_outer = shift(mine_outer, "layer", 1)
     theirs2 = shift(mine2, "layer", 1)
-    z, inv4, w, fwd2, mine2_outer = call(
-        part(outer_image_kernel, depth, rows, cols),
-        [right, row, col, via, fwd, gain, inv, mine_outer, theirs_outer, z, inv4, w, fwd2],
-        [vmem] * 13,
-        [ext, (tall, wide), ext, ext, (4 * SUB, wide)],
-        alias={9: 0, 10: 1, 11: 2, 12: 3},
-        flops=8 * size,
-    )
-    theirs2_outer = shift(mine2_outer, "layer", 1)
     (early,) = call(
         part(early_kernel, depth, rows, cols),
         [right, z, w],
@@ -632,6 +639,15 @@
         [(2, SUB, cols)],
         flops=4 * size,
     )
+    z, inv4, w, fwd2, mine2_outer, early = call(
+        part(outer_image_kernel, depth, rows, cols),
+        [right, row, col, via, fwd, gain, inv, mine_outer, theirs_outer, early, z, inv4, w, fwd2],
+        [vmem] * 14,
+        [ext, (tall, wide), ext, ext, (4 * SUB, wide), (2, SUB, cols)],
+        alias={10: 0, 11: 1, 12: 2, 13: 3},
+        flops=8 * size,
+    )
+    theirs2_outer = shift(mine2_outer, "layer", 1)
     block = (depth, rows, cols)
     y, v, acc = call(
         part(inner_dots_kernel, depth, rows, cols),

time: 52.1 us -> 54.3 us (1.042)
  waiting for transfers between devices: 2.46 us -> 4.38 us
  Pallas kernels: 18.4 us -> 17.8 us
    ppermute x9, waiting for transfers between devices: 2.46 us -> 4.38 us  [shift(): lax.ppermute(value, axis, [(i, (i + by) % count) for i in range(count)])]
  transfers between devices with their start and end apart: 9 -> 9, of which waited for: 2 -> 3; matrix products, arithmetic and copies ran while one was open for 0% -> 0% of each run, Pallas kernels for 18% -> 17%
where the time goes in v5:
time: 54.3 us; the launch traced here: 54.2 us
  Pallas kernels  17.8 us (33%)
  blocking collectives  17.6 us (32%)
  starting transfers between devices  13.7 us (25%)
  waiting for transfers between devices  4.38 us (8%)
  between operations  0.74 us (1%)
    pallas_call x13, Pallas kernels, call(): pl.pallas_call(body, out_shape=shapes, in_specs=[spec_of(k) for k in kind...  17.8 us
    all_to_all x1, blocking collectives, shards(): lax.all_to_all(sums.reshape(devices, 1, LANE), ALL, 0, 0)  17.6 us
    ppermute x9, starting transfers between devices, shift(): lax.ppermute(value, axis, [(i, (i + by) % count) for i in range(count)])  13.7 us
    ppermute x9, waiting for transfers between devices, shift(): lax.ppermute(value, axis, [(i, (i + by) % count) for i in range(count)])  4.38 us
  transfers between devices with their start and end apart: 9, of which 3 were waited for; matrix products, arithmetic and copies ran while one was open for 0% of the time, Pallas kernels for 17%

profile of v5, /device:TPU:1, one launch (start us, length us, event | category | flops | bytes accessed | tf_op | source)
XLA Modules:
  0.0 54.2 jit_solution(3993647982485325428)
XLA Ops:
  0.6 3.8 %shard_map.77 = (f32[4,136,1152]{2,1,0:T(8,128)S(1)}, f32[4,136,1152]{2,1,0:T(8,128)S(1)}, f32[4,136,1152]{2,1,0:T(8,128)S(1)}, f32[4,136,1152]{2,1,0:T(8,128)S(...) custom-call(f32[4,128,1024]{2,1,0:T(8,128)} %refs_0_.3, f32[4,128,1024]{2,1,0:T(8,128)} %refs_1_.3, ...), custom_call_target="tpu_custom_call" | custom-call | flops 626688 | bytes 3760128 | tf_op jit(solution)/shard_map/pallas_call | solution.py:69
  4.4 2.2 %collective-permute-start = (f32[40,128]{1,0:T(8,128)S(1)}, f32[40,128]{1,0:T(8,128)S(1)}, u32[]{:S(2)}, u32[]{:S(2)}) collective-permute-start(f32[40,128]{1,0:T(8,128)S(1)} %get-tuple-element.80), channel_id=1, source_target_pairs={{0,1},{1,2},{2,3},{3,0},{4,5},{5,6},{6,7},{7,4},{8,9},{9,10},{10,1... | collective-permute-start | bytes 61448 | tf_op jit(solution)/shard_map/ppermute | solution.py:532
  6.6 1.5 %collective-permute-start.1 = (f32[40,128]{1,0:T(8,128)S(1)}, f32[40,128]{1,0:T(8,128)S(1)}, u32[]{:S(2)}, u32[]{:S(2)}) collective-permute-start(f32[40,128]{1,0:T(8,128)S(1)} %get-tuple-element.81), channel_id=1, source_target_pairs={{0,3},{1,0},{2,1},{3,2},{4,7},{5,4},{6,5},{7,6},{8,11},{9,8},{10,9... | collective-permute-start | bytes 61448 | tf_op jit(solution)/shard_map/ppermute | solution.py:532
  8.1 3.0 %shard_map.78 = (f32[4,136,1152]{2,1,0:T(8,128)S(1)}, f32[4,136,1152]{2,1,0:T(8,128)S(1)}, f32[4,136,1152]{2,1,0:T(8,128)S(1)}, f32[4,136,1152]{2,1,0:T(8,128)S(1)}, f32[4,136,1152]{2,1,0:T(8,128)S(1)}) custom-call(f32[4,128,1024]{2,1,0:T(8,128)} %refs_0_.3, ...), custom_call_target="tpu_custom_call", output_to_operand_aliasing={{0}: (6, {}), {1}: (7, {}), {2}: (8, {}), {3}: (9, {}), {4}... | custom-call | flops 6266880 | bytes 11280384 | tf_op jit(solution)/shard_map/pallas_call | solution.py:69
  11.1 0.0 collective-permute-done.refs_5_
  11.1 0.0 collective-permute-done.1.refs_6_
  11.1 0.3 shard_map.79
  11.4 1.4 %shard_map.80 = (f32[4,136,1152]{2,1,0:T(8,128)S(1)}, f32[4,136,1152]{2,1,0:T(8,128)S(1)}, f32[4,136,1152]{2,1,0:T(8,128)S(1)}, f32[4,136,1152]{2,1,0:T(8,128)S(...) custom-call(f32[4,136,1152]{2,1,0:T(8,128)S(1)} %get-tuple-element.8, ...), custom_call_target="tpu_custom_call", output_to_operand_aliasing={{0}: (0, {}), {1}: (1, {}), {2}: (2, {}), {3}: (3, {}), {4}... | custom-call | flops 9400320 | tf_op jit(solution)/shard_map/pallas_call | solution.py:69
  12.8 1.1 %collective-permute-start.6 = (f32[2,64,1152]{2,1,0:T(8,128)S(1)}, f32[2,64,1152]{2,1,0:T(8,128)S(1)}, u32[]{:S(2)}, u32[]{:S(2)}) collective-permute-start(f32[2,64,1152]{2,1,0:T(8,128)S(1)} %get-tuple-element.115.refs_7_), channel_id=1, source_target_pairs={{0,64},{64,0},{1,65},{65,1},{2,66},{66,2},{3,67},{67,3},{4,68},{68... | collective-permute-start | bytes 1769480 | tf_op jit(solution)/shard_map/ppermute | solution.py:532
  13.9 1.0 %shard_map.81 = (f32[4,136,1152]{2,1,0:T(8,128)S(1)}, f32[4,136,1152]{2,1,0:T(8,128)S(1)}, f32[4,136,1152]{2,1,0:T(8,128)S(1)}, f32[4,136,1152]{2,1,0:T(8,128)S(...) custom-call(f32[4,136,1152]{2,1,0:T(8,128)S(1)} %get-tuple-element.8, ...), custom_call_target="tpu_custom_call", output_to_operand_aliasing={{0}: (0, {}), {1}: (1, {}), {2}: (2, {}), {3}: (3, {}), {4}... | custom-call | flops 9400320 | tf_op jit(solution)/shard_map/pallas_call | solution.py:69
  14.9 0.1 collective-permute-start.5
  15.0 1.8 %collective-permute-start.2 = (f32[40,1152]{1,0:T(8,128)S(1)}, f32[40,1152]{1,0:T(8,128)S(1)}, u32[]{:S(2)}, u32[]{:S(2)}) collective-permute-start(f32[40,1152]{1,0:T(8,128)S(1)} %get-tuple-element.104), channel_id=1, source_target_pairs={{0,4},{4,8},{8,12},{12,16},{16,20},{20,24},{24,28},{28,32},{32,36}... | collective-permute-start | bytes 552968 | tf_op jit(solution)/shard_map/ppermute | solution.py:532
  16.8 0.0 collective-permute-done.6.refs_8_
  16.8 1.1 %shard_map.83 = (f32[4,136,1152]{2,1,0:T(8,128)S(1)}, f32[136,1152]{1,0:T(8,128)S(1)}, f32[4,136,1152]{2,1,0:T(8,128)S(1)}, f32[4,136,1152]{2,1,0:T(8,128)S(1)}, f32[104,1152]{1,0:T(8,128)S(1)}) custom-call(f32[4,136,1152]{2,1,0:T(8,128)S(1)} %get-tuple-element.96.refs_0_, f32[4,136,1152]{2,1,0:T(8,128)S(1)} %get-tuple-element.97.refs_1_, ...), custom_call_target="tpu_custom_call" | custom-call | flops 9400320 | tf_op jit(solution)/shard_map/pallas_call | solution.py:69
  17.9 0.0 collective-permute-done.5.refs_8_
  17.9 1.2 %shard_map.84 = (f32[4,136,1152]{2,1,0:T(8,128)S(1)}, f32[136,1152]{1,0:T(8,128)S(1)}, f32[4,136,1152]{2,1,0:T(8,128)S(1)}, f32[4,136,1152]{2,1,0:T(8,128)S(1)}, f32[104,1152]{1,0:T(8,128)S(1)}) custom-call(f32[4,136,1152]{2,1,0:T(8,128)S(1)} %get-tuple-element.96.refs_0_, ...), custom_call_target="tpu_custom_call", output_to_operand_aliasing={{0}: (9, {}), {1}: (10, {}), {2}: (11, {}), {3}: (12, {}), ... | custom-call | flops 9400320 | tf_op jit(solution)/shard_map/pallas_call | solution.py:69
  19.1 0.8 %collective-permute-start.8 = (f32[104,1152]{1,0:T(8,128)S(1)}, f32[104,1152]{1,0:T(8,128)S(1)}, u32[]{:S(2)}, u32[]{:S(2)}) collective-permute-start(f32[104,1152]{1,0:T(8,128)S(1)} %get-tuple-element.130.refs_4_), channel_id=1, source_target_pairs={{0,64},{64,0},{1,65},{65,1},{2,66},{66,2},{3,67},{67,3},{4,68},{68... | collective-permute-start | bytes 1437704 | tf_op jit(solution)/shard_map/ppermute | solution.py:532
  19.9 4.5 %collective-permute-start.3 = (f32[40,1152]{1,0:T(8,128)S(1)}, f32[40,1152]{1,0:T(8,128)S(1)}, u32[]{:S(2)}, u32[]{:S(2)}) collective-permute-start(f32[40,1152]{1,0:T(8,128)S(1)} %get-tuple-element.105), channel_id=1, source_target_pairs={{0,60},{4,0},{8,4},{12,8},{16,12},{20,16},{24,20},{28,24},{32,28},... | collective-permute-start | bytes 552968 | tf_op jit(solution)/shard_map/ppermute | solution.py:532
  24.4 1.3 %collective-permute-done.2.refs_8_ = f32[40,1152]{1,0:T(8,128)S(1)} collective-permute-done((f32[40,1152]{1,0:T(8,128)S(1)}, f32[40,1152]{1,0:T(8,128)S(1)}, u32[]{:S(2)}, u32[]{:S(2)}) %collective-permute-start.2) | collective-permute-done | bytes 184352 | tf_op jit(solution)/shard_map/ppermute | solution.py:532
  25.7 2.3 %collective-permute-done.3.refs_9_ = f32[40,1152]{1,0:T(8,128)S(1)} collective-permute-done((f32[40,1152]{1,0:T(8,128)S(1)}, f32[40,1152]{1,0:T(8,128)S(1)}, u32[]{:S(2)}, u32[]{:S(2)}) %collective-permute-start.3) | collective-permute-done | bytes 184352 | tf_op jit(solution)/shard_map/ppermute | solution.py:532
  28.0 0.3 shard_map.82
  28.3 1.3 %collective-permute-start.4 = (f32[2,16,1152]{2,1,0:T(8,128)S(1)}, f32[2,16,1152]{2,1,0:T(8,128)S(1)}, u32[]{:S(2)}, u32[]{:S(2)}) collective-permute-start(f32[2,16,1152]{2,1,0:T(8,128)S(1)} %get-tuple-element.113.refs_7_), channel_id=1, source_target_pairs={{0,64},{64,0},{1,65},{65,1},{2,66},{66,2},{3,67},{67,3},{4,68},{68... | collective-permute-start | bytes 442376 | tf_op jit(solution)/shard_map/ppermute | solution.py:532
  29.6 0.3 shard_map.85.refs_9_
  29.9 0.7 %collective-permute-done.4.refs_8_ = f32[2,16,1152]{2,1,0:T(8,128)S(1)} collective-permute-done((f32[2,16,1152]{2,1,0:T(8,128)S(1)}, f32[2,16,1152]{2,1,0:T(8,128)S(1)}, u32[]{:S(2)}, u32[]{:S(2)}) %collective-permute-start.4) | collective-permute-done | bytes 147488 | tf_op jit(solution)/shard_map/ppermute | solution.py:532
  30.6 0.7 %shard_map.86 = (f32[4,136,1152]{2,1,0:T(8,128)S(1)}, f32[136,1152]{1,0:T(8,128)S(1)}, f32[4,136,1152]{2,1,0:T(8,128)S(1)}, f32[4,136,1152]{2,1,0:T(8,128)S(1)},...) custom-call(f32[4,136,1152]{2,1,0:T(8,128)S(1)} %get-tuple-element.1, ...), custom_call_target="tpu_custom_call", output_to_operand_aliasing={{0}: (10, {}), {1}: (11, {}), {2}: (12, {}), {3}: (13, {})} | custom-call | flops 5013504 | tf_op jit(solution)/shard_map/pallas_call | solution.py:69
  31.3 0.4 collective-permute-start.7
  31.7 0.0 collective-permute-done.8.refs_5_
  31.7 1.7 %shard_map.87 = (f32[4,136,1152]{2,1,0:T(8,128)S(1)}, f32[4,128,1024]{2,1,0:T(8,128)S(1)}, f32[2,8,1024]{2,1,0:T(8,128)S(1)}) custom-call(f32[4,136,1152]{2,1,0:T(8,128)S(1)} %get-tuple-element.106.refs_1_.refs_0_, f32[4,136,1152]{2,1,0:T(8,128)S(1)} %get-tuple-element.107.refs_2_.refs_1_, f32[4,136,1152]{2,1,0:T(8,128)S(1)} %get-tuple-element.125.refs_2_, ...), custom_call_target="tpu_custom_call" | custom-call | flops 12533760 | tf_op jit(solution)/shard_map/pallas_call | solution.py:69
  33.4 0.0 collective-permute-done.7.refs_5_
  33.4 0.8 %shard_map.88 = (f32[4,136,1152]{2,1,0:T(8,128)S(1)}, f32[4,128,1024]{2,1,0:T(8,128)S(1)}, f32[128,128]{1,0:T(8,128)S(1)}) custom-call(f32[4,136,1152]{2,1,0:T(8,128)S(1)} %get-tuple-element.106.refs_1_.refs_0_, f32[4,136,1152]{2,1,0:T(8,128)S(1)} %get-tuple-element.107.refs_2_.refs_1_, ...), custom_call_target="tpu_custom_call", output_to_operand_aliasing={{0}: (10, {}), {1}: (11, {})} | custom-call | flops 5013504 | tf_op jit(solution)/shard_map/pallas_call | solution.py:69
  34.2 17.6 %all_to_all.5 = f32[128,1,128]{2,1,0:T(1,128)S(1)} all-to-all(f32[128,1,128]{2,1,0:T(1,128)S(1)} %bitcast.5), channel_id=1, replica_groups=mesh['layer'=2,'px_0'=4,'px_1'=4,'py'=4] {'layer','px_0','px_1','py'}, dimensions={0} | all-to-all | bytes 131072 | tf_op jit(solution)/shard_map/all_to_all | solution.py:667
  51.8 2.4 %shard_map.89 = (f32[4,128,1024]{2,1,0:T(8,128)}, f32[4,128,1024]{2,1,0:T(8,128)}) custom-call(f32[128,128]{1,0:T(8,128)S(1)} %bitcast.4, f32[4,136,1152]{2,1,0:T(8,128)S(1)} %get-tuple-element.108.refs_0_.refs_1_, f32[4,136,1152]{2,1,0:T(8,128)S(1)} %get-tuple-element.135.refs_2_, f32[4,136,1152]{2,1,0:T(8,128)S(1)} %get-tuple-element.128.refs_7_.refs_3_, ...), custom_call_target="tpu_custom_call" | custom-call | flops 6266880 | tf_op jit(solution)/shard_map/pallas_call | solution.py:69
Async XLA Ops:
  4.4 6.7 %collective-permute-start = (f32[40,128]{1,0:T(8,128)S(1)}, f32[40,128]{1,0:T(8,128)S(1)}, u32[]{:S(2)}, u32[]{:S(2)}) collective-permute-start(f32[40,128]{1,0:T(8,128)S(1)} %get-tuple-element.80), channel_id=1, source_target_pairs={{0,1},{1,2},{2,3},{3,0},{4,5},{5,6},{6,7},{7,4},{8,9},{9,10},{10,1... | collective-permute-start | bytes 61448 | tf_op jit(solution)/shard_map/ppermute | solution.py:532
  6.6 4.5 %collective-permute-start.1 = (f32[40,128]{1,0:T(8,128)S(1)}, f32[40,128]{1,0:T(8,128)S(1)}, u32[]{:S(2)}, u32[]{:S(2)}) collective-permute-start(f32[40,128]{1,0:T(8,128)S(1)} %get-tuple-element.81), channel_id=1, source_target_pairs={{0,3},{1,0},{2,1},{3,2},{4,7},{5,4},{6,5},{7,6},{8,11},{9,8},{10,9... | collective-permute-start | bytes 61448 | tf_op jit(solution)/shard_map/ppermute | solution.py:532
  12.8 4.0 %collective-permute-start.6 = (f32[2,64,1152]{2,1,0:T(8,128)S(1)}, f32[2,64,1152]{2,1,0:T(8,128)S(1)}, u32[]{:S(2)}, u32[]{:S(2)}) collective-permute-start(f32[2,64,1152]{2,1,0:T(8,128)S(1)} %get-tuple-element.115.refs_7_), channel_id=1, source_target_pairs={{0,64},{64,0},{1,65},{65,1},{2,66},{66,2},{3,67},{67,3},{4,68},{68... | collective-permute-start | bytes 1769480 | tf_op jit(solution)/shard_map/ppermute | solution.py:532
  14.9 3.0 %collective-permute-start.5 = (f32[2,56,1152]{2,1,0:T(8,128)S(1)}, f32[2,56,1152]{2,1,0:T(8,128)S(1)}, u32[]{:S(2)}, u32[]{:S(2)}) collective-permute-start(f32[2,56,1152]{2,1,0:T(8,128)S(1)} %get-tuple-element.114.refs_7_), channel_id=1, source_target_pairs={{0,64},{64,0},{1,65},{65,1},{2,66},{66,2},{3,67},{67,3},{4,68},{68... | collective-permute-start | bytes 1548296 | tf_op jit(solution)/shard_map/ppermute | solution.py:532
  15.0 10.7 %collective-permute-start.2 = (f32[40,1152]{1,0:T(8,128)S(1)}, f32[40,1152]{1,0:T(8,128)S(1)}, u32[]{:S(2)}, u32[]{:S(2)}) collective-permute-start(f32[40,1152]{1,0:T(8,128)S(1)} %get-tuple-element.104), channel_id=1, source_target_pairs={{0,4},{4,8},{8,12},{12,16},{16,20},{20,24},{24,28},{28,32},{32,36}... | collective-permute-start | bytes 552968 | tf_op jit(solution)/shard_map/ppermute | solution.py:532
  19.1 12.6 %collective-permute-start.8 = (f32[104,1152]{1,0:T(8,128)S(1)}, f32[104,1152]{1,0:T(8,128)S(1)}, u32[]{:S(2)}, u32[]{:S(2)}) collective-permute-start(f32[104,1152]{1,0:T(8,128)S(1)} %get-tuple-element.130.refs_4_), channel_id=1, source_target_pairs={{0,64},{64,0},{1,65},{65,1},{2,66},{66,2},{3,67},{67,3},{4,68},{68... | collective-permute-start | bytes 1437704 | tf_op jit(solution)/shard_map/ppermute | solution.py:532
  19.9 8.1 %collective-permute-start.3 = (f32[40,1152]{1,0:T(8,128)S(1)}, f32[40,1152]{1,0:T(8,128)S(1)}, u32[]{:S(2)}, u32[]{:S(2)}) collective-permute-start(f32[40,1152]{1,0:T(8,128)S(1)} %get-tuple-element.105), channel_id=1, source_target_pairs={{0,60},{4,0},{8,4},{12,8},{16,12},{20,16},{24,20},{28,24},{32,28},... | collective-permute-start | bytes 552968 | tf_op jit(solution)/shard_map/ppermute | solution.py:532
  28.3 2.3 %collective-permute-start.4 = (f32[2,16,1152]{2,1,0:T(8,128)S(1)}, f32[2,16,1152]{2,1,0:T(8,128)S(1)}, u32[]{:S(2)}, u32[]{:S(2)}) collective-permute-start(f32[2,16,1152]{2,1,0:T(8,128)S(1)} %get-tuple-element.113.refs_7_), channel_id=1, source_target_pairs={{0,64},{64,0},{1,65},{65,1},{2,66},{66,2},{3,67},{67,3},{4,68},{68... | collective-permute-start | bytes 442376 | tf_op jit(solution)/shard_map/ppermute | solution.py:532
  31.3 2.1 %collective-permute-start.7 = (f32[32,1152]{1,0:T(8,128)S(1)}, f32[32,1152]{1,0:T(8,128)S(1)}, u32[]{:S(2)}, u32[]{:S(2)}) collective-permute-start(f32[32,1152]{1,0:T(8,128)S(1)} %get-tuple-element.126.refs_4_), channel_id=1, source_target_pairs={{0,64},{64,0},{1,65},{65,1},{2,66},{66,2},{3,67},{67,3},{4,68},{68... | collective-permute-start | bytes 442376 | tf_op jit(solution)/shard_map/ppermute | solution.py:532

commit v6 on v5

--- a/solution.py
+++ b/solution.py
@@ -14,6 +14,7 @@
 EARLY = (RIGHT, ROW)
 SUB, LANE = 8, 128
 INNER, IMAGE, DOTS, FINAL = 4, 3, 4, 2
+TAIL = 3
 PX = ("px_0", "px_1")
 ALL = ("layer", "px_0", "px_1", "py")
 
@@ -376,7 +377,7 @@
                 out[tile(slots + i), :] = gain[k, at, :] * value
 
 
-def inner_image_kernel(depth, rows, cols, low, high, first, *refs):
+def inner_image_kernel(depth, rows, cols, low, high, begin, end, *refs):
     right, row, col, via, fwd, gain, inv, mine, theirs = refs[0:9]
     z, inv4, w, fwd2, out = refs[-5:]
     count = rows // SUB + 1
@@ -385,7 +386,6 @@
     def solve(t):
         join(depth, t, t - low, fwd, gain, mine, theirs, inv4, z)
 
-    begin = low + 1 if first else low - 1
     for t in range(low, begin + 1):
         solve(t)
 
@@ -397,12 +397,14 @@
         )
         return carry
 
-    sweep(begin, high - 1, IMAGE, body)
+    sweep(begin, end, IMAGE, body)
+    for t in range(end + 1, high):
+        solve(t)
 
 
 def outer_image_kernel(depth, rows, cols, *refs):
     (right, row, col, via, fwd, gain, inv, mine, theirs) = refs[0:9]
-    early, (z, inv4, w, fwd2, out, acc) = refs[9], refs[14:20]
+    early, (z, inv4, w, fwd2, out, acc) = refs[9], refs[15:21]
     count = rows // SUB + 1
     sub = sublanes((SUB, cols + LANE))
     join(depth, 0, 0, fwd, gain, mine, theirs, inv4, z)
@@ -435,10 +437,22 @@
     return (rho, c)
 
 
-def early_kernel(depth, rows, cols, *refs):
-    *refs, acc = refs
+def tail_kernel(depth, rows, cols, begin, *refs):
+    right, row, col, via, gain, inv, z = refs[0:7]
+    w, fwd2, out, acc = refs[9:13]
+    count = rows // SUB + 1
+    sub = sublanes((SUB, cols + LANE))
+    image_of(
+        depth,
+        begin,
+        count - 2 - begin,
+        count,
+        sub,
+        4,
+        (right, row, col, via, gain, inv, z, w, fwd2, out),
+    )
     zero = jnp.zeros((SUB, cols), jnp.float32)
-    body = lambda t, carry: first_dots(depth, cols, t, refs, carry)
+    body = lambda t, carry: first_dots(depth, cols, t, (right, z, w), carry)
     acc[0], acc[1] = sweep(2, rows // SUB - 1, 2, each(body), (zero, zero))
 
 
@@ -457,7 +471,7 @@
     return e, g
 
 
-def inner_dots_kernel(depth, rows, cols, *refs):
+def inner_dots_kernel(depth, rows, cols, end, *refs):
     (row, col, fwd2, gain, mine, theirs, inv4, w, y, v, acc) = refs
     count = rows // SUB + 1
     sub = sublanes((SUB, cols + LANE))
@@ -475,19 +489,19 @@
         return second_image_of(depth, cols, t, n, count, sub, (row, col, w, y, v), carry)
 
     zero = jnp.zeros((SUB, cols), jnp.float32)
-    acc[0], acc[1] = sweep(3, count - 3, DOTS, body, (zero, zero))
-
-
-def outer_dots_kernel(depth, rows, cols, *refs):
+    acc[0], acc[1] = sweep(3, end - 1, DOTS, body, (zero, zero))
+
+
+def outer_dots_kernel(depth, rows, cols, begin, *refs):
     (row, col, fwd2, gain, mine, theirs, inv4, w, early, acc) = refs[0:10]
     y, v, sums = refs[12:15]
     count = rows // SUB + 1
     sub = sublanes((SUB, cols + LANE))
-    for slot, t in enumerate((count - 2, count - 1, 0, 1)):
+    for slot, t in enumerate((count - 2, count - 1, 0, 1, *range(begin, count - 2))):
         middle = (mine[tile(slot), :] + theirs[tile(slot), :]) * inv4[tile(t), :]
         back(depth, t, fwd2, gain, middle, y)
     carry = (acc[0], acc[1])
-    for t, n in ((count - 3, 2), (0, 3)):
+    for t, n in ((begin - 1, count - begin), (0, 3)):
         carry = second_image_of(depth, cols, t, n, count, sub, (row, col, w, y, v), carry)
     sums[...] = gathered(sums, (early[0], early[1], *carry))
 
@@ -605,19 +619,20 @@
     )
     theirs_rest = shift(mine_rest, "layer", 1)
     right, row, col, via, _, fwd, gain, inv = state
-    images = [ext, (tall, wide), ext, ext, (tall - 4 * SUB, wide)]
-    images = call(
-        part(inner_image_kernel, depth, rows, cols, 1, split, True),
+    late = end - 1 - TAIL
+    images = [ext, (tall, wide), ext, ext, ((late - 2) * SUB, wide)]
+    first = call(
+        part(inner_image_kernel, depth, rows, cols, 1, split, 2, split - 1),
         [right, row, col, via, fwd, gain, inv, mine, theirs],
         [vmem] * 9,
         images,
         flops=flops,
     )
     z, inv4, w, fwd2, mine2 = call(
-        part(inner_image_kernel, depth, rows, cols, split, end, False),
-        [right, row, col, via, fwd, gain, inv, mine_rest, theirs_rest, *images],
+        part(inner_image_kernel, depth, rows, cols, split, end, split - 1, late),
+        [right, row, col, via, fwd, gain, inv, mine_rest, theirs_rest, *first],
         [vmem] * 14,
-        [ext, (tall, wide), ext, ext, (tall - 4 * SUB, wide)],
+        images,
         alias={9 + i: i for i in range(5)},
         flops=flops,
     )
@@ -632,32 +647,34 @@
     right, row, col, via, _ = e
     theirs_outer = shift(mine_outer, "layer", 1)
     theirs2 = shift(mine2, "layer", 1)
-    (early,) = call(
-        part(early_kernel, depth, rows, cols),
-        [right, z, w],
-        [vmem] * 3,
-        [(2, SUB, cols)],
-        flops=4 * size,
+    w, fwd2, mine2_outer, early = call(
+        part(tail_kernel, depth, rows, cols, late),
+        [right, row, col, via, gain, inv, z, w, fwd2],
+        [vmem] * 9,
+        [ext, ext, ((4 + TAIL) * SUB, wide), (2, SUB, cols)],
+        alias={7: 0, 8: 1},
+        flops=8 * size,
     )
     z, inv4, w, fwd2, mine2_outer, early = call(
         part(outer_image_kernel, depth, rows, cols),
-        [right, row, col, via, fwd, gain, inv, mine_outer, theirs_outer, early, z, inv4, w, fwd2],
-        [vmem] * 14,
-        [ext, (tall, wide), ext, ext, (4 * SUB, wide), (2, SUB, cols)],
-        alias={10: 0, 11: 1, 12: 2, 13: 3},
+        [right, row, col, via, fwd, gain, inv, mine_outer, theirs_outer, early]
+        + [z, inv4, w, fwd2, mine2_outer],
+        [vmem] * 15,
+        [ext, (tall, wide), ext, ext, ((4 + TAIL) * SUB, wide), (2, SUB, cols)],
+        alias={10: 0, 11: 1, 12: 2, 13: 3, 14: 4},
         flops=8 * size,
     )
     theirs2_outer = shift(mine2_outer, "layer", 1)
     block = (depth, rows, cols)
     y, v, acc = call(
-        part(inner_dots_kernel, depth, rows, cols),
+        part(inner_dots_kernel, depth, rows, cols, late),
         [row, col, fwd2, gain, mine2, theirs2, inv4, w],
         [vmem] * 8,
         [ext, block, (2, SUB, cols)],
         flops=20 * size,
     )
     y, v, sums = call(
-        part(outer_dots_kernel, depth, rows, cols),
+        part(outer_dots_kernel, depth, rows, cols, late),
         [row, col, fwd2, gain, mine2_outer, theirs2_outer, inv4, w, early, acc, y, v],
         [vmem] * 12,
         [ext, block, (devices, LANE)],

time: 54.3 us -> 51 us (0.939)
  waiting for transfers between devices: 4.38 us -> 3.03 us
  starting transfers between devices: 13.7 us -> 12.7 us
  blocking collectives: 17.6 us -> 17 us
    ppermute x9, waiting for transfers between devices: 4.38 us -> 3.03 us  [shift(): lax.ppermute(value, axis, [(i, (i + by) % count) for i in range(count)])]
    ppermute x9, starting transfers between devices: 13.7 us -> 12.7 us  [shift(): lax.ppermute(value, axis, [(i, (i + by) % count) for i in range(count)])]
    all_to_all x1, blocking collectives: 17.6 us -> 17 us  [shards(): lax.all_to_all(sums.reshape(devices, 1, LANE), ALL, 0, 0)]
  transfers between devices with their start and end apart: 9 -> 9, of which waited for: 3 -> 2; matrix products, arithmetic and copies ran while one was open for 0% -> 0% of each run, Pallas kernels for 17% -> 16%
where the time goes in v6:
time: 51 us; the launch traced here: 50.9 us
  Pallas kernels  17.5 us (34%)
  blocking collectives  17 us (33%)
  starting transfers between devices  12.7 us (25%)
  waiting for transfers between devices  3.03 us (6%)
  between operations  0.74 us (1%)
    pallas_call x13, Pallas kernels, call(): pl.pallas_call(body, out_shape=shapes, in_specs=[spec_of(k) for k in kind...  17.5 us
    all_to_all x1, blocking collectives, shards(): lax.all_to_all(sums.reshape(devices, 1, LANE), ALL, 0, 0)  17 us
    ppermute x9, starting transfers between devices, shift(): lax.ppermute(value, axis, [(i, (i + by) % count) for i in range(count)])  12.7 us
    ppermute x9, waiting for transfers between devices, shift(): lax.ppermute(value, axis, [(i, (i + by) % count) for i in range(count)])  3.03 us
  transfers between devices with their start and end apart: 9, of which 2 were waited for; matrix products, arithmetic and copies ran while one was open for 0% of the time, Pallas kernels for 16%

profile of v6, /device:TPU:1, one launch (start us, length us, event | category | flops | bytes accessed | tf_op | source)
XLA Modules:
  0.0 50.9 jit_solution(18074402151446939762)
XLA Ops:
  0.6 3.8 %shard_map.77 = (f32[4,136,1152]{2,1,0:T(8,128)S(1)}, f32[4,136,1152]{2,1,0:T(8,128)S(1)}, f32[4,136,1152]{2,1,0:T(8,128)S(1)}, f32[4,136,1152]{2,1,0:T(8,128)S(...) custom-call(f32[4,128,1024]{2,1,0:T(8,128)} %refs_0_.3, f32[4,128,1024]{2,1,0:T(8,128)} %refs_1_.3, ...), custom_call_target="tpu_custom_call" | custom-call | flops 626688 | bytes 3760128 | tf_op jit(solution)/shard_map/pallas_call | solution.py:70
  4.4 2.2 %collective-permute-start = (f32[40,128]{1,0:T(8,128)S(1)}, f32[40,128]{1,0:T(8,128)S(1)}, u32[]{:S(2)}, u32[]{:S(2)}) collective-permute-start(f32[40,128]{1,0:T(8,128)S(1)} %get-tuple-element.84), channel_id=1, source_target_pairs={{0,1},{1,2},{2,3},{3,0},{4,5},{5,6},{6,7},{7,4},{8,9},{9,10},{10,1... | collective-permute-start | bytes 61448 | tf_op jit(solution)/shard_map/ppermute | solution.py:546
  6.6 1.5 %collective-permute-start.1 = (f32[40,128]{1,0:T(8,128)S(1)}, f32[40,128]{1,0:T(8,128)S(1)}, u32[]{:S(2)}, u32[]{:S(2)}) collective-permute-start(f32[40,128]{1,0:T(8,128)S(1)} %get-tuple-element.85), channel_id=1, source_target_pairs={{0,3},{1,0},{2,1},{3,2},{4,7},{5,4},{6,5},{7,6},{8,11},{9,8},{10,9... | collective-permute-start | bytes 61448 | tf_op jit(solution)/shard_map/ppermute | solution.py:546
  8.1 3.0 %shard_map.78 = (f32[4,136,1152]{2,1,0:T(8,128)S(1)}, f32[4,136,1152]{2,1,0:T(8,128)S(1)}, f32[4,136,1152]{2,1,0:T(8,128)S(1)}, f32[4,136,1152]{2,1,0:T(8,128)S(1)}, f32[4,136,1152]{2,1,0:T(8,128)S(1)}) custom-call(f32[4,128,1024]{2,1,0:T(8,128)} %refs_0_.3, ...), custom_call_target="tpu_custom_call", output_to_operand_aliasing={{0}: (6, {}), {1}: (7, {}), {2}: (8, {}), {3}: (9, {}), {4}... | custom-call | flops 6266880 | bytes 11280384 | tf_op jit(solution)/shard_map/pallas_call | solution.py:70
  11.1 0.0 collective-permute-done.refs_5_
  11.1 0.0 collective-permute-done.1.refs_6_
  11.2 0.3 shard_map.79
  11.4 1.4 %shard_map.80 = (f32[4,136,1152]{2,1,0:T(8,128)S(1)}, f32[4,136,1152]{2,1,0:T(8,128)S(1)}, f32[4,136,1152]{2,1,0:T(8,128)S(1)}, f32[4,136,1152]{2,1,0:T(8,128)S(...) custom-call(f32[4,136,1152]{2,1,0:T(8,128)S(1)} %get-tuple-element.8, ...), custom_call_target="tpu_custom_call", output_to_operand_aliasing={{0}: (0, {}), {1}: (1, {}), {2}: (2, {}), {3}: (3, {}), {4}... | custom-call | flops 9400320 | tf_op jit(solution)/shard_map/pallas_call | solution.py:70
  12.8 1.1 %collective-permute-start.6 = (f32[2,64,1152]{2,1,0:T(8,128)S(1)}, f32[2,64,1152]{2,1,0:T(8,128)S(1)}, u32[]{:S(2)}, u32[]{:S(2)}) collective-permute-start(f32[2,64,1152]{2,1,0:T(8,128)S(1)} %get-tuple-element.119.refs_7_), channel_id=1, source_target_pairs={{0,64},{64,0},{1,65},{65,1},{2,66},{66,2},{3,67},{67,3},{4,68},{68... | collective-permute-start | bytes 1769480 | tf_op jit(solution)/shard_map/ppermute | solution.py:546
  13.9 1.0 %shard_map.81 = (f32[4,136,1152]{2,1,0:T(8,128)S(1)}, f32[4,136,1152]{2,1,0:T(8,128)S(1)}, f32[4,136,1152]{2,1,0:T(8,128)S(1)}, f32[4,136,1152]{2,1,0:T(8,128)S(...) custom-call(f32[4,136,1152]{2,1,0:T(8,128)S(1)} %get-tuple-element.9, ...), custom_call_target="tpu_custom_call", output_to_operand_aliasing={{0}: (0, {}), {1}: (1, {}), {2}: (2, {}), {3}: (3, {}), {4}... | custom-call | flops 9400320 | tf_op jit(solution)/shard_map/pallas_call | solution.py:70
  14.9 0.1 collective-permute-start.5
  15.0 1.8 %collective-permute-start.2 = (f32[40,1152]{1,0:T(8,128)S(1)}, f32[40,1152]{1,0:T(8,128)S(1)}, u32[]{:S(2)}, u32[]{:S(2)}) collective-permute-start(f32[40,1152]{1,0:T(8,128)S(1)} %get-tuple-element.108), channel_id=1, source_target_pairs={{0,4},{4,8},{8,12},{12,16},{16,20},{20,24},{24,28},{28,32},{32,36}... | collective-permute-start | bytes 552968 | tf_op jit(solution)/shard_map/ppermute | solution.py:546
  16.8 4.4 %collective-permute-start.3 = (f32[40,1152]{1,0:T(8,128)S(1)}, f32[40,1152]{1,0:T(8,128)S(1)}, u32[]{:S(2)}, u32[]{:S(2)}) collective-permute-start(f32[40,1152]{1,0:T(8,128)S(1)} %get-tuple-element.109), channel_id=1, source_target_pairs={{0,60},{4,0},{8,4},{12,8},{16,12},{20,16},{24,20},{28,24},{32,28},... | collective-permute-start | bytes 552968 | tf_op jit(solution)/shard_map/ppermute | solution.py:546
  21.2 0.0 collective-permute-done.6.refs_8_
  21.2 1.0 %shard_map.83 = (f32[4,136,1152]{2,1,0:T(8,128)S(1)}, f32[136,1152]{1,0:T(8,128)S(1)}, f32[4,136,1152]{2,1,0:T(8,128)S(1)}, f32[4,136,1152]{2,1,0:T(8,128)S(1)}, f32[80,1152]{1,0:T(8,128)S(1)}) custom-call(f32[4,136,1152]{2,1,0:T(8,128)S(1)} %get-tuple-element.100.refs_0_, f32[4,136,1152]{2,1,0:T(8,128)S(1)} %get-tuple-element.101.refs_1_, ...), custom_call_target="tpu_custom_call" | custom-call | flops 9400320 | tf_op jit(solution)/shard_map/pallas_call | solution.py:70
  22.2 0.0 collective-permute-done.5.refs_8_
  22.2 0.7 %shard_map.84 = (f32[4,136,1152]{2,1,0:T(8,128)S(1)}, f32[136,1152]{1,0:T(8,128)S(1)}, f32[4,136,1152]{2,1,0:T(8,128)S(1)}, f32[4,136,1152]{2,1,0:T(8,128)S(1)}, f32[80,1152]{1,0:T(8,128)S(1)}) custom-call(f32[4,136,1152]{2,1,0:T(8,128)S(1)} %get-tuple-element.100.refs_0_, ...), custom_call_target="tpu_custom_call", output_to_operand_aliasing={{0}: (9, {}), {1}: (10, {}), {2}: (11, {}), {3}: (12, {}), ... | custom-call | flops 9400320 | tf_op jit(solution)/shard_map/pallas_call | solution.py:70
  22.9 2.8 %collective-permute-done.2.refs_8_ = f32[40,1152]{1,0:T(8,128)S(1)} collective-permute-done((f32[40,1152]{1,0:T(8,128)S(1)}, f32[40,1152]{1,0:T(8,128)S(1)}, u32[]{:S(2)}, u32[]{:S(2)}) %collective-permute-start.2) | collective-permute-done | bytes 184352 | tf_op jit(solution)/shard_map/ppermute | solution.py:546
  25.7 0.0 collective-permute-done.3.refs_9_
  25.7 0.3 shard_map.82
  26.0 1.1 %collective-permute-start.4 = (f32[2,16,1152]{2,1,0:T(8,128)S(1)}, f32[2,16,1152]{2,1,0:T(8,128)S(1)}, u32[]{:S(2)}, u32[]{:S(2)}) collective-permute-start(f32[2,16,1152]{2,1,0:T(8,128)S(1)} %get-tuple-element.117.refs_7_), channel_id=1, source_target_pairs={{0,64},{64,0},{1,65},{65,1},{2,66},{66,2},{3,67},{67,3},{4,68},{68... | collective-permute-start | bytes 442376 | tf_op jit(solution)/shard_map/ppermute | solution.py:546
  27.1 0.1 collective-permute-start.8
  27.2 0.7 %shard_map.85 = (f32[4,136,1152]{2,1,0:T(8,128)S(1)}, f32[4,136,1152]{2,1,0:T(8,128)S(1)}, f32[56,1152]{1,0:T(8,128)S(1)}, f32[2,8,1024]{2,1,0:T(8,128)S(1)}) custom-call(f32[4,136,1152]{2,1,0:T(8,128)S(1)} %get-tuple-element.112.refs_0_.refs_1_, ...), custom_call_target="tpu_custom_call", output_to_operand_aliasing={{0}: (7, {}), {1}: (8, {})} | custom-call | flops 5013504 | tf_op jit(solution)/shard_map/pallas_call | solution.py:70
  27.8 0.2 collective-permute-done.4.refs_8_
  28.1 0.7 %shard_map.86 = (f32[4,136,1152]{2,1,0:T(8,128)S(1)}, f32[136,1152]{1,0:T(8,128)S(1)}, f32[4,136,1152]{2,1,0:T(8,128)S(1)}, f32[4,136,1152]{2,1,0:T(8,128)S(1)},...) custom-call(f32[4,136,1152]{2,1,0:T(8,128)S(1)} %get-tuple-element.1, ...), custom_call_target="tpu_custom_call", output_to_operand_aliasing={{0}: (10, {}), {1}: (11, {}), {2}: (12, {}), {3}: (13, {}),... | custom-call | flops 5013504 | tf_op jit(solution)/shard_map/pallas_call | solution.py:70
  28.7 0.4 collective-permute-start.7
  29.2 0.0 collective-permute-done.8.refs_5_
  29.2 1.3 %shard_map.87 = (f32[4,136,1152]{2,1,0:T(8,128)S(1)}, f32[4,128,1024]{2,1,0:T(8,128)S(1)}, f32[2,8,1024]{2,1,0:T(8,128)S(1)}) custom-call(f32[4,136,1152]{2,1,0:T(8,128)S(1)} %get-tuple-element.110.refs_1_.refs_0_, f32[4,136,1152]{2,1,0:T(8,128)S(1)} %get-tuple-element.111.refs_2_.refs_1_, f32[4,136,1152]{2,1,0:T(8,128)S(1)} %get-tuple-element.133.refs_2_, ...), custom_call_target="tpu_custom_call" | custom-call | flops 12533760 | tf_op jit(solution)/shard_map/pallas_call | solution.py:70
  30.5 0.0 collective-permute-done.7.refs_5_
  30.5 1.1 %shard_map.88 = (f32[4,136,1152]{2,1,0:T(8,128)S(1)}, f32[4,128,1024]{2,1,0:T(8,128)S(1)}, f32[128,128]{1,0:T(8,128)S(1)}) custom-call(f32[4,136,1152]{2,1,0:T(8,128)S(1)} %get-tuple-element.110.refs_1_.refs_0_, f32[4,136,1152]{2,1,0:T(8,128)S(1)} %get-tuple-element.111.refs_2_.refs_1_, ...), custom_call_target="tpu_custom_call", output_to_operand_aliasing={{0}: (10, {}), {1}: (11, {})} | custom-call | flops 5013504 | tf_op jit(solution)/shard_map/pallas_call | solution.py:70
  31.6 17.0 %all_to_all.5 = f32[128,1,128]{2,1,0:T(1,128)S(1)} all-to-all(f32[128,1,128]{2,1,0:T(1,128)S(1)} %bitcast.5), channel_id=1, replica_groups=mesh['layer'=2,'px_0'=4,'px_1'=4,'py'=4] {'layer','px_0','px_1','py'}, dimensions={0} | all-to-all | bytes 131072 | tf_op jit(solution)/shard_map/all_to_all | solution.py:684
  48.5 2.4 %shard_map.89 = (f32[4,128,1024]{2,1,0:T(8,128)}, f32[4,128,1024]{2,1,0:T(8,128)}) custom-call(f32[128,128]{1,0:T(8,128)S(1)} %bitcast.4, f32[4,136,1152]{2,1,0:T(8,128)S(1)} %get-tuple-element.112.refs_0_.refs_1_, f32[4,136,1152]{2,1,0:T(8,128)S(1)} %get-tuple-element.143.refs_2_, f32[4,136,1152]{2,1,0:T(8,128)S(1)} %get-tuple-element.136.refs_7_.refs_3_, ...), custom_call_target="tpu_custom_call" | custom-call | flops 6266880 | tf_op jit(solution)/shard_map/pallas_call | solution.py:70
Async XLA Ops:
  4.4 6.7 %collective-permute-start = (f32[40,128]{1,0:T(8,128)S(1)}, f32[40,128]{1,0:T(8,128)S(1)}, u32[]{:S(2)}, u32[]{:S(2)}) collective-permute-start(f32[40,128]{1,0:T(8,128)S(1)} %get-tuple-element.84), channel_id=1, source_target_pairs={{0,1},{1,2},{2,3},{3,0},{4,5},{5,6},{6,7},{7,4},{8,9},{9,10},{10,1... | collective-permute-start | bytes 61448 | tf_op jit(solution)/shard_map/ppermute | solution.py:546
  6.6 4.5 %collective-permute-start.1 = (f32[40,128]{1,0:T(8,128)S(1)}, f32[40,128]{1,0:T(8,128)S(1)}, u32[]{:S(2)}, u32[]{:S(2)}) collective-permute-start(f32[40,128]{1,0:T(8,128)S(1)} %get-tuple-element.85), channel_id=1, source_target_pairs={{0,3},{1,0},{2,1},{3,2},{4,7},{5,4},{6,5},{7,6},{8,11},{9,8},{10,9... | collective-permute-start | bytes 61448 | tf_op jit(solution)/shard_map/ppermute | solution.py:546
  12.8 8.4 %collective-permute-start.6 = (f32[2,64,1152]{2,1,0:T(8,128)S(1)}, f32[2,64,1152]{2,1,0:T(8,128)S(1)}, u32[]{:S(2)}, u32[]{:S(2)}) collective-permute-start(f32[2,64,1152]{2,1,0:T(8,128)S(1)} %get-tuple-element.119.refs_7_), channel_id=1, source_target_pairs={{0,64},{64,0},{1,65},{65,1},{2,66},{66,2},{3,67},{67,3},{4,68},{68... | collective-permute-start | bytes 1769480 | tf_op jit(solution)/shard_map/ppermute | solution.py:546
  14.9 7.4 %collective-permute-start.5 = (f32[2,56,1152]{2,1,0:T(8,128)S(1)}, f32[2,56,1152]{2,1,0:T(8,128)S(1)}, u32[]{:S(2)}, u32[]{:S(2)}) collective-permute-start(f32[2,56,1152]{2,1,0:T(8,128)S(1)} %get-tuple-element.118.refs_7_), channel_id=1, source_target_pairs={{0,64},{64,0},{1,65},{65,1},{2,66},{66,2},{3,67},{67,3},{4,68},{68... | collective-permute-start | bytes 1548296 | tf_op jit(solution)/shard_map/ppermute | solution.py:546
  15.0 10.7 %collective-permute-start.2 = (f32[40,1152]{1,0:T(8,128)S(1)}, f32[40,1152]{1,0:T(8,128)S(1)}, u32[]{:S(2)}, u32[]{:S(2)}) collective-permute-start(f32[40,1152]{1,0:T(8,128)S(1)} %get-tuple-element.108), channel_id=1, source_target_pairs={{0,4},{4,8},{8,12},{12,16},{16,20},{20,24},{24,28},{28,32},{32,36}... | collective-permute-start | bytes 552968 | tf_op jit(solution)/shard_map/ppermute | solution.py:546
  16.8 8.9 %collective-permute-start.3 = (f32[40,1152]{1,0:T(8,128)S(1)}, f32[40,1152]{1,0:T(8,128)S(1)}, u32[]{:S(2)}, u32[]{:S(2)}) collective-permute-start(f32[40,1152]{1,0:T(8,128)S(1)} %get-tuple-element.109), channel_id=1, source_target_pairs={{0,60},{4,0},{8,4},{12,8},{16,12},{20,16},{24,20},{28,24},{32,28},... | collective-permute-start | bytes 552968 | tf_op jit(solution)/shard_map/ppermute | solution.py:546
  26.0 2.1 %collective-permute-start.4 = (f32[2,16,1152]{2,1,0:T(8,128)S(1)}, f32[2,16,1152]{2,1,0:T(8,128)S(1)}, u32[]{:S(2)}, u32[]{:S(2)}) collective-permute-start(f32[2,16,1152]{2,1,0:T(8,128)S(1)} %get-tuple-element.117.refs_7_), channel_id=1, source_target_pairs={{0,64},{64,0},{1,65},{65,1},{2,66},{66,2},{3,67},{67,3},{4,68},{68... | collective-permute-start | bytes 442376 | tf_op jit(solution)/shard_map/ppermute | solution.py:546
  27.1 2.1 %collective-permute-start.8 = (f32[80,1152]{1,0:T(8,128)S(1)}, f32[80,1152]{1,0:T(8,128)S(1)}, u32[]{:S(2)}, u32[]{:S(2)}) collective-permute-start(f32[80,1152]{1,0:T(8,128)S(1)} %get-tuple-element.138.refs_4_), channel_id=1, source_target_pairs={{0,64},{64,0},{1,65},{65,1},{2,66},{66,2},{3,67},{67,3},{4,68},{68... | collective-permute-start | bytes 1105928 | tf_op jit(solution)/shard_map/ppermute | solution.py:546
  28.7 1.7 %collective-permute-start.7 = (f32[56,1152]{1,0:T(8,128)S(1)}, f32[56,1152]{1,0:T(8,128)S(1)}, u32[]{:S(2)}, u32[]{:S(2)}) collective-permute-start(f32[56,1152]{1,0:T(8,128)S(1)} %get-tuple-element.134.refs_4_), channel_id=1, source_target_pairs={{0,64},{64,0},{1,65},{65,1},{2,66},{66,2},{3,67},{67,3},{4,68},{68... | collective-permute-start | bytes 774152 | tf_op jit(solution)/shard_map/ppermute | solution.py:546

commit v7 on v6

--- a/solution.py
+++ b/solution.py
@@ -13,8 +13,8 @@
 FIELDS = 5
 EARLY = (RIGHT, ROW)
 SUB, LANE = 8, 128
-INNER, IMAGE, DOTS, FINAL = 4, 3, 4, 2
-TAIL = 3
+INNER, IMAGE, DOTS, FINAL = 4, 3, 3, 2
+TAIL = 2
 PX = ("px_0", "px_1")
 ALL = ("layer", "px_0", "px_1", "py")
 
@@ -518,7 +518,7 @@
     rho1 = alpha * (alpha * e - c)
     beta = rho1 / rho
     curvature = c - 2.0 * alpha * e + alpha * alpha * g
-    alpha1 = rho1 / (curvature - beta * rho1 / alpha)
+    alpha1 = rho1 / (curvature - beta * beta * c)
     near = jnp.broadcast_to(alpha + alpha1 * (1.0 + beta), (SUB, cols))
     far = jnp.broadcast_to(alpha1 * alpha, (SUB, cols))
     copies = []

time: 51 us -> 50.7 us (level)
  starting transfers between devices: 12.7 us -> 13.3 us
    ppermute x9, starting transfers between devices: 12.7 us -> 13.3 us  [shift(): lax.ppermute(value, axis, [(i, (i + by) % count) for i in range(count)])]
  transfers between devices with their start and end apart: 9 -> 9, of which waited for: 2 -> 2; matrix products, arithmetic and copies ran while one was open for 0% -> 0% of each run, Pallas kernels for 16% -> 17%
where the time goes in v7:
time: 50.7 us; the launch traced here: 50.6 us
  Pallas kernels  17 us (34%)
  blocking collectives  16.9 us (33%)
  starting transfers between devices  13.3 us (26%)
  waiting for transfers between devices  2.6 us (5%)
  between operations  0.74 us (1%)
    pallas_call x13, Pallas kernels, call(): pl.pallas_call(body, out_shape=shapes, in_specs=[spec_of(k) for k in kind...  17 us
    all_to_all x1, blocking collectives, shards(): lax.all_to_all(sums.reshape(devices, 1, LANE), ALL, 0, 0)  16.9 us
    ppermute x9, starting transfers between devices, shift(): lax.ppermute(value, axis, [(i, (i + by) % count) for i in range(count)])  13.3 us
    ppermute x9, waiting for transfers between devices, shift(): lax.ppermute(value, axis, [(i, (i + by) % count) for i in range(count)])  2.6 us
  transfers between devices with their start and end apart: 9, of which 2 were waited for; matrix products, arithmetic and copies ran while one was open for 0% of the time, Pallas kernels for 17%

profile of v7, /device:TPU:1, one launch (start us, length us, event | category | flops | bytes accessed | tf_op | source)
XLA Modules:
  0.0 50.6 jit_solution(6412676279129302176)
XLA Ops:
  0.6 3.8 %shard_map.77 = (f32[4,136,1152]{2,1,0:T(8,128)S(1)}, f32[4,136,1152]{2,1,0:T(8,128)S(1)}, f32[4,136,1152]{2,1,0:T(8,128)S(1)}, f32[4,136,1152]{2,1,0:T(8,128)S(...) custom-call(f32[4,128,1024]{2,1,0:T(8,128)} %refs_0_.3, f32[4,128,1024]{2,1,0:T(8,128)} %refs_1_.3, ...), custom_call_target="tpu_custom_call" | custom-call | flops 626688 | bytes 3760128 | tf_op jit(solution)/shard_map/pallas_call | solution.py:70
  4.4 2.2 %collective-permute-start = (f32[40,128]{1,0:T(8,128)S(1)}, f32[40,128]{1,0:T(8,128)S(1)}, u32[]{:S(2)}, u32[]{:S(2)}) collective-permute-start(f32[40,128]{1,0:T(8,128)S(1)} %get-tuple-element.84), channel_id=1, source_target_pairs={{0,1},{1,2},{2,3},{3,0},{4,5},{5,6},{6,7},{7,4},{8,9},{9,10},{10,1... | collective-permute-start | bytes 61448 | tf_op jit(solution)/shard_map/ppermute | solution.py:546
  6.6 1.5 %collective-permute-start.1 = (f32[40,128]{1,0:T(8,128)S(1)}, f32[40,128]{1,0:T(8,128)S(1)}, u32[]{:S(2)}, u32[]{:S(2)}) collective-permute-start(f32[40,128]{1,0:T(8,128)S(1)} %get-tuple-element.85), channel_id=1, source_target_pairs={{0,3},{1,0},{2,1},{3,2},{4,7},{5,4},{6,5},{7,6},{8,11},{9,8},{10,9... | collective-permute-start | bytes 61448 | tf_op jit(solution)/shard_map/ppermute | solution.py:546
  8.1 3.0 %shard_map.78 = (f32[4,136,1152]{2,1,0:T(8,128)S(1)}, f32[4,136,1152]{2,1,0:T(8,128)S(1)}, f32[4,136,1152]{2,1,0:T(8,128)S(1)}, f32[4,136,1152]{2,1,0:T(8,128)S(1)}, f32[4,136,1152]{2,1,0:T(8,128)S(1)}) custom-call(f32[4,128,1024]{2,1,0:T(8,128)} %refs_0_.3, ...), custom_call_target="tpu_custom_call", output_to_operand_aliasing={{0}: (6, {}), {1}: (7, {}), {2}: (8, {}), {3}: (9, {}), {4}... | custom-call | flops 6266880 | bytes 11280384 | tf_op jit(solution)/shard_map/pallas_call | solution.py:70
  11.1 0.0 collective-permute-done.refs_5_
  11.1 0.0 collective-permute-done.1.refs_6_
  11.1 0.3 shard_map.79
  11.4 1.4 %shard_map.80 = (f32[4,136,1152]{2,1,0:T(8,128)S(1)}, f32[4,136,1152]{2,1,0:T(8,128)S(1)}, f32[4,136,1152]{2,1,0:T(8,128)S(1)}, f32[4,136,1152]{2,1,0:T(8,128)S(...) custom-call(f32[4,136,1152]{2,1,0:T(8,128)S(1)} %get-tuple-element.8, ...), custom_call_target="tpu_custom_call", output_to_operand_aliasing={{0}: (0, {}), {1}: (1, {}), {2}: (2, {}), {3}: (3, {}), {4}... | custom-call | flops 9400320 | tf_op jit(solution)/shard_map/pallas_call | solution.py:70
  12.8 1.1 %collective-permute-start.6 = (f32[2,64,1152]{2,1,0:T(8,128)S(1)}, f32[2,64,1152]{2,1,0:T(8,128)S(1)}, u32[]{:S(2)}, u32[]{:S(2)}) collective-permute-start(f32[2,64,1152]{2,1,0:T(8,128)S(1)} %get-tuple-element.119.refs_7_), channel_id=1, source_target_pairs={{0,64},{64,0},{1,65},{65,1},{2,66},{66,2},{3,67},{67,3},{4,68},{68... | collective-permute-start | bytes 1769480 | tf_op jit(solution)/shard_map/ppermute | solution.py:546
  13.9 0.9 %shard_map.81 = (f32[4,136,1152]{2,1,0:T(8,128)S(1)}, f32[4,136,1152]{2,1,0:T(8,128)S(1)}, f32[4,136,1152]{2,1,0:T(8,128)S(1)}, f32[4,136,1152]{2,1,0:T(8,128)S(...) custom-call(f32[4,136,1152]{2,1,0:T(8,128)S(1)} %get-tuple-element.9, ...), custom_call_target="tpu_custom_call", output_to_operand_aliasing={{0}: (0, {}), {1}: (1, {}), {2}: (2, {}), {3}: (3, {}), {4}... | custom-call | flops 9400320 | tf_op jit(solution)/shard_map/pallas_call | solution.py:70
  14.8 0.1 collective-permute-start.5
  14.9 1.8 %collective-permute-start.2 = (f32[40,1152]{1,0:T(8,128)S(1)}, f32[40,1152]{1,0:T(8,128)S(1)}, u32[]{:S(2)}, u32[]{:S(2)}) collective-permute-start(f32[40,1152]{1,0:T(8,128)S(1)} %get-tuple-element.108), channel_id=1, source_target_pairs={{0,4},{4,8},{8,12},{12,16},{16,20},{20,24},{24,28},{28,32},{32,36}... | collective-permute-start | bytes 552968 | tf_op jit(solution)/shard_map/ppermute | solution.py:546
  16.7 4.4 %collective-permute-start.3 = (f32[40,1152]{1,0:T(8,128)S(1)}, f32[40,1152]{1,0:T(8,128)S(1)}, u32[]{:S(2)}, u32[]{:S(2)}) collective-permute-start(f32[40,1152]{1,0:T(8,128)S(1)} %get-tuple-element.109), channel_id=1, source_target_pairs={{0,60},{4,0},{8,4},{12,8},{16,12},{20,16},{24,20},{28,24},{32,28},... | collective-permute-start | bytes 552968 | tf_op jit(solution)/shard_map/ppermute | solution.py:546
  21.1 0.0 collective-permute-done.6.refs_8_
  21.1 1.0 %shard_map.83 = (f32[4,136,1152]{2,1,0:T(8,128)S(1)}, f32[136,1152]{1,0:T(8,128)S(1)}, f32[4,136,1152]{2,1,0:T(8,128)S(1)}, f32[4,136,1152]{2,1,0:T(8,128)S(1)}, f32[88,1152]{1,0:T(8,128)S(1)}) custom-call(f32[4,136,1152]{2,1,0:T(8,128)S(1)} %get-tuple-element.100.refs_0_, f32[4,136,1152]{2,1,0:T(8,128)S(1)} %get-tuple-element.101.refs_1_, ...), custom_call_target="tpu_custom_call" | custom-call | flops 9400320 | tf_op jit(solution)/shard_map/pallas_call | solution.py:70
  22.1 0.0 collective-permute-done.5.refs_8_
  22.1 0.7 %shard_map.84 = (f32[4,136,1152]{2,1,0:T(8,128)S(1)}, f32[136,1152]{1,0:T(8,128)S(1)}, f32[4,136,1152]{2,1,0:T(8,128)S(1)}, f32[4,136,1152]{2,1,0:T(8,128)S(1)}, f32[88,1152]{1,0:T(8,128)S(1)}) custom-call(f32[4,136,1152]{2,1,0:T(8,128)S(1)} %get-tuple-element.100.refs_0_, ...), custom_call_target="tpu_custom_call", output_to_operand_aliasing={{0}: (9, {}), {1}: (10, {}), {2}: (11, {}), {3}: (12, {}), ... | custom-call | flops 9400320 | tf_op jit(solution)/shard_map/pallas_call | solution.py:70
  22.8 0.7 %collective-permute-start.8 = (f32[88,1152]{1,0:T(8,128)S(1)}, f32[88,1152]{1,0:T(8,128)S(1)}, u32[]{:S(2)}, u32[]{:S(2)}) collective-permute-start(f32[88,1152]{1,0:T(8,128)S(1)} %get-tuple-element.138.refs_4_), channel_id=1, source_target_pairs={{0,64},{64,0},{1,65},{65,1},{2,66},{66,2},{3,67},{67,3},{4,68},{68... | collective-permute-start | bytes 1216520 | tf_op jit(solution)/shard_map/ppermute | solution.py:546
  23.5 2.1 %collective-permute-done.2.refs_8_ = f32[40,1152]{1,0:T(8,128)S(1)} collective-permute-done((f32[40,1152]{1,0:T(8,128)S(1)}, f32[40,1152]{1,0:T(8,128)S(1)}, u32[]{:S(2)}, u32[]{:S(2)}) %collective-permute-start.2) | collective-permute-done | bytes 184352 | tf_op jit(solution)/shard_map/ppermute | solution.py:546
  25.6 0.0 collective-permute-done.3.refs_9_
  25.6 0.3 shard_map.82
  25.9 1.1 %collective-permute-start.4 = (f32[2,16,1152]{2,1,0:T(8,128)S(1)}, f32[2,16,1152]{2,1,0:T(8,128)S(1)}, u32[]{:S(2)}, u32[]{:S(2)}) collective-permute-start(f32[2,16,1152]{2,1,0:T(8,128)S(1)} %get-tuple-element.117.refs_7_), channel_id=1, source_target_pairs={{0,64},{64,0},{1,65},{65,1},{2,66},{66,2},{3,67},{67,3},{4,68},{68... | collective-permute-start | bytes 442376 | tf_op jit(solution)/shard_map/ppermute | solution.py:546
  27.0 0.5 %shard_map.85 = (f32[4,136,1152]{2,1,0:T(8,128)S(1)}, f32[4,136,1152]{2,1,0:T(8,128)S(1)}, f32[48,1152]{1,0:T(8,128)S(1)}, f32[2,8,1024]{2,1,0:T(8,128)S(1)}) custom-call(f32[4,136,1152]{2,1,0:T(8,128)S(1)} %get-tuple-element.112.refs_0_.refs_1_, ...), custom_call_target="tpu_custom_call", output_to_operand_aliasing={{0}: (7, {}), {1}: (8, {})} | custom-call | flops 5013504 | tf_op jit(solution)/shard_map/pallas_call | solution.py:70
  27.5 0.5 collective-permute-done.4.refs_8_
  28.0 0.5 %shard_map.86 = (f32[4,136,1152]{2,1,0:T(8,128)S(1)}, f32[136,1152]{1,0:T(8,128)S(1)}, f32[4,136,1152]{2,1,0:T(8,128)S(1)}, f32[4,136,1152]{2,1,0:T(8,128)S(1)},...) custom-call(f32[4,136,1152]{2,1,0:T(8,128)S(1)} %get-tuple-element.1, ...), custom_call_target="tpu_custom_call", output_to_operand_aliasing={{0}: (10, {}), {1}: (11, {}), {2}: (12, {}), {3}: (13, {}),... | custom-call | flops 5013504 | tf_op jit(solution)/shard_map/pallas_call | solution.py:70
  28.5 0.4 collective-permute-start.7
  29.0 0.0 collective-permute-done.8.refs_5_
  29.0 1.4 %shard_map.87 = (f32[4,136,1152]{2,1,0:T(8,128)S(1)}, f32[4,128,1024]{2,1,0:T(8,128)S(1)}, f32[2,8,1024]{2,1,0:T(8,128)S(1)}) custom-call(f32[4,136,1152]{2,1,0:T(8,128)S(1)} %get-tuple-element.110.refs_1_.refs_0_, f32[4,136,1152]{2,1,0:T(8,128)S(1)} %get-tuple-element.111.refs_2_.refs_1_, f32[4,136,1152]{2,1,0:T(8,128)S(1)} %get-tuple-element.133.refs_2_, ...), custom_call_target="tpu_custom_call" | custom-call | flops 12533760 | tf_op jit(solution)/shard_map/pallas_call | solution.py:70
  30.4 0.0 collective-permute-done.7.refs_5_
  30.4 0.8 %shard_map.88 = (f32[4,136,1152]{2,1,0:T(8,128)S(1)}, f32[4,128,1024]{2,1,0:T(8,128)S(1)}, f32[128,128]{1,0:T(8,128)S(1)}) custom-call(f32[4,136,1152]{2,1,0:T(8,128)S(1)} %get-tuple-element.110.refs_1_.refs_0_, f32[4,136,1152]{2,1,0:T(8,128)S(1)} %get-tuple-element.111.refs_2_.refs_1_, ...), custom_call_target="tpu_custom_call", output_to_operand_aliasing={{0}: (10, {}), {1}: (11, {})} | custom-call | flops 5013504 | tf_op jit(solution)/shard_map/pallas_call | solution.py:70
  31.3 16.9 %all_to_all.5 = f32[128,1,128]{2,1,0:T(1,128)S(1)} all-to-all(f32[128,1,128]{2,1,0:T(1,128)S(1)} %bitcast.5), channel_id=1, replica_groups=mesh['layer'=2,'px_0'=4,'px_1'=4,'py'=4] {'layer','px_0','px_1','py'}, dimensions={0} | all-to-all | bytes 131072 | tf_op jit(solution)/shard_map/all_to_all | solution.py:684
  48.2 2.4 %shard_map.89 = (f32[4,128,1024]{2,1,0:T(8,128)}, f32[4,128,1024]{2,1,0:T(8,128)}) custom-call(f32[128,128]{1,0:T(8,128)S(1)} %bitcast.4, f32[4,136,1152]{2,1,0:T(8,128)S(1)} %get-tuple-element.112.refs_0_.refs_1_, f32[4,136,1152]{2,1,0:T(8,128)S(1)} %get-tuple-element.143.refs_2_, f32[4,136,1152]{2,1,0:T(8,128)S(1)} %get-tuple-element.136.refs_7_.refs_3_, ...), custom_call_target="tpu_custom_call" | custom-call | flops 6266880 | tf_op jit(solution)/shard_map/pallas_call | solution.py:70
Async XLA Ops:
  4.4 6.7 %collective-permute-start = (f32[40,128]{1,0:T(8,128)S(1)}, f32[40,128]{1,0:T(8,128)S(1)}, u32[]{:S(2)}, u32[]{:S(2)}) collective-permute-start(f32[40,128]{1,0:T(8,128)S(1)} %get-tuple-element.84), channel_id=1, source_target_pairs={{0,1},{1,2},{2,3},{3,0},{4,5},{5,6},{6,7},{7,4},{8,9},{9,10},{10,1... | collective-permute-start | bytes 61448 | tf_op jit(solution)/shard_map/ppermute | solution.py:546
  6.6 4.5 %collective-permute-start.1 = (f32[40,128]{1,0:T(8,128)S(1)}, f32[40,128]{1,0:T(8,128)S(1)}, u32[]{:S(2)}, u32[]{:S(2)}) collective-permute-start(f32[40,128]{1,0:T(8,128)S(1)} %get-tuple-element.85), channel_id=1, source_target_pairs={{0,3},{1,0},{2,1},{3,2},{4,7},{5,4},{6,5},{7,6},{8,11},{9,8},{10,9... | collective-permute-start | bytes 61448 | tf_op jit(solution)/shard_map/ppermute | solution.py:546
  12.8 8.3 %collective-permute-start.6 = (f32[2,64,1152]{2,1,0:T(8,128)S(1)}, f32[2,64,1152]{2,1,0:T(8,128)S(1)}, u32[]{:S(2)}, u32[]{:S(2)}) collective-permute-start(f32[2,64,1152]{2,1,0:T(8,128)S(1)} %get-tuple-element.119.refs_7_), channel_id=1, source_target_pairs={{0,64},{64,0},{1,65},{65,1},{2,66},{66,2},{3,67},{67,3},{4,68},{68... | collective-permute-start | bytes 1769480 | tf_op jit(solution)/shard_map/ppermute | solution.py:546
  14.8 7.3 %collective-permute-start.5 = (f32[2,56,1152]{2,1,0:T(8,128)S(1)}, f32[2,56,1152]{2,1,0:T(8,128)S(1)}, u32[]{:S(2)}, u32[]{:S(2)}) collective-permute-start(f32[2,56,1152]{2,1,0:T(8,128)S(1)} %get-tuple-element.118.refs_7_), channel_id=1, source_target_pairs={{0,64},{64,0},{1,65},{65,1},{2,66},{66,2},{3,67},{67,3},{4,68},{68... | collective-permute-start | bytes 1548296 | tf_op jit(solution)/shard_map/ppermute | solution.py:546
  14.9 10.7 %collective-permute-start.2 = (f32[40,1152]{1,0:T(8,128)S(1)}, f32[40,1152]{1,0:T(8,128)S(1)}, u32[]{:S(2)}, u32[]{:S(2)}) collective-permute-start(f32[40,1152]{1,0:T(8,128)S(1)} %get-tuple-element.108), channel_id=1, source_target_pairs={{0,4},{4,8},{8,12},{12,16},{16,20},{20,24},{24,28},{28,32},{32,36}... | collective-permute-start | bytes 552968 | tf_op jit(solution)/shard_map/ppermute | solution.py:546
  16.7 8.9 %collective-permute-start.3 = (f32[40,1152]{1,0:T(8,128)S(1)}, f32[40,1152]{1,0:T(8,128)S(1)}, u32[]{:S(2)}, u32[]{:S(2)}) collective-permute-start(f32[40,1152]{1,0:T(8,128)S(1)} %get-tuple-element.109), channel_id=1, source_target_pairs={{0,60},{4,0},{8,4},{12,8},{16,12},{20,16},{24,20},{28,24},{32,28},... | collective-permute-start | bytes 552968 | tf_op jit(solution)/shard_map/ppermute | solution.py:546
  22.8 6.2 %collective-permute-start.8 = (f32[88,1152]{1,0:T(8,128)S(1)}, f32[88,1152]{1,0:T(8,128)S(1)}, u32[]{:S(2)}, u32[]{:S(2)}) collective-permute-start(f32[88,1152]{1,0:T(8,128)S(1)} %get-tuple-element.138.refs_4_), channel_id=1, source_target_pairs={{0,64},{64,0},{1,65},{65,1},{2,66},{66,2},{3,67},{67,3},{4,68},{68... | collective-permute-start | bytes 1216520 | tf_op jit(solution)/shard_map/ppermute | solution.py:546
  25.9 2.1 %collective-permute-start.4 = (f32[2,16,1152]{2,1,0:T(8,128)S(1)}, f32[2,16,1152]{2,1,0:T(8,128)S(1)}, u32[]{:S(2)}, u32[]{:S(2)}) collective-permute-start(f32[2,16,1152]{2,1,0:T(8,128)S(1)} %get-tuple-element.117.refs_7_), channel_id=1, source_target_pairs={{0,64},{64,0},{1,65},{65,1},{2,66},{66,2},{3,67},{67,3},{4,68},{68... | collective-permute-start | bytes 442376 | tf_op jit(solution)/shard_map/ppermute | solution.py:546
  28.5 1.9 %collective-permute-start.7 = (f32[48,1152]{1,0:T(8,128)S(1)}, f32[48,1152]{1,0:T(8,128)S(1)}, u32[]{:S(2)}, u32[]{:S(2)}) collective-permute-start(f32[48,1152]{1,0:T(8,128)S(1)} %get-tuple-element.134.refs_4_), channel_id=1, source_target_pairs={{0,64},{64,0},{1,65},{65,1},{2,66},{66,2},{3,67},{67,3},{4,68},{68... | collective-permute-start | bytes 663560 | tf_op jit(solution)/shard_map/ppermute | solution.py:546
